TPU v7x, 32 devices: a whole 2x2x4 slice. The times are simulated.
32 devices in a mesh: fsdp: 8 (over z, y), model: 4 (over x, core).
Axes of the slice: x: 2, y: 2, z: 4, core: 2. Of those that a mesh axis runs over, the one named last changes fastest.
Arguments:
- x_in: bfloat16 [16, 128, 2048], P('fsdp', 'model')
- grad_out: bfloat16 [16, 128, 2048], P('fsdp', 'model')
- gain_attn: float32 [2048], replicated
- gain_mlp: float32 [2048], replicated
- w_qkv: bfloat16 [2048, 6144], P('fsdp', 'model')
- w_out: bfloat16 [2048, 2048], P('model', 'fsdp')
- w_gate: bfloat16 [2048, 8192], P('fsdp', 'model')
- w_up: bfloat16 [2048, 8192], P('fsdp', 'model')
- w_down: bfloat16 [8192, 2048], P('model', 'fsdp')
- rope_cos: float32 [128, 64], replicated
- rope_sin: float32 [128, 64], replicated
Outputs:
- output 1: bfloat16 [16, 128, 2048], P('fsdp', 'model')
- output 2: bfloat16 [16, 128, 2048], P('fsdp', 'model')
- output 3: float32 [2048], replicated
- output 4: float32 [2048], replicated
- output 5: float32 [2048, 6144], P('fsdp', 'model')
- output 6: float32 [2048, 2048], P('model', 'fsdp')
- output 7: float32 [2048, 8192], P('fsdp', 'model')
- output 8: float32 [2048, 8192], P('fsdp', 'model')
- output 9: float32 [8192, 2048], P('model', 'fsdp')
All inputs are finite; a program needn't handle non-finite values.
Results may differ from a plain program's by a relative error of at most 0.0159797.
Values are sent between devices in bfloat16 or wider.
A program may use at most 1 GiB of HBM per device.

v0:
```python
import jax
import jax.numpy as jnp
from jax import lax
from jax.sharding import PartitionSpec as P

NORM_EPS = 1e-5


def rms_scale(x_f32, gain):
    inv_rms = lax.rsqrt(jnp.mean(x_f32 * x_f32, axis=-1, keepdims=True) + NORM_EPS)
    return x_f32 * inv_rms * gain


def rotate(tensor, cos_t, sin_t):
    half = tensor.shape[-1] // 2
    first = tensor[..., :half]
    second = tensor[..., half:]
    return jnp.concatenate([first * cos_t - second * sin_t, second * cos_t + first * sin_t], axis=-1)


def rotate_back(cotangent, cos_t, sin_t):
    half = cotangent.shape[-1] // 2
    first = cotangent[..., :half]
    second = cotangent[..., half:]
    return jnp.concatenate([first * cos_t + second * sin_t, second * cos_t - first * sin_t], axis=-1)


def solution(mesh):
    fsdp_size = mesh.shape['fsdp']
    act_spec = P('fsdp', 'model', None)
    rows_spec = P('fsdp', 'model')
    cols_spec = P('model', 'fsdp')

    def gather_rows(w_shard):
        return lax.all_gather(w_shard, 'fsdp', axis=0, tiled=True)

    def gather_cols(w_shard):
        return lax.all_gather(w_shard, 'fsdp', axis=1, tiled=True)

    def gather_seq(tensor):
        return lax.all_gather(tensor, 'model', axis=1, tiled=True)

    def scatter_seq(tensor):
        return lax.psum_scatter(tensor, 'model', scatter_dimension=1, tiled=True)

    def device_fn(x_loc, dy_loc, gain_attn, gain_mlp, wqkv_sh, wout_sh, wgate_sh, wup_sh, wdown_sh, rope_cos, rope_sin):
        head_dim = 2 * rope_cos.shape[1]
        seq_full = rope_cos.shape[0]
        local_heads = wout_sh.shape[0] // head_dim
        local_kv = (wqkv_sh.shape[1] // head_dim - local_heads) // 2
        group_size = local_heads // local_kv
        micro_rows = x_loc.shape[0] // 2
        scale = head_dim ** -0.5
        pos_ids = jnp.arange(seq_full)
        causal = pos_ids[:, None] >= pos_ids[None, :]
        cos_q = rope_cos[:, None, None, :]
        sin_q = rope_sin[:, None, None, :]
        cos_k = rope_cos[:, None, :]
        sin_k = rope_sin[:, None, :]

        def micro_step(x_mb, dy_mb, accum):
            acc_gattn, acc_gmlp, acc_qkv, acc_out, acc_gate, acc_up, acc_down = accum
            x_f32 = x_mb.astype(jnp.float32)
            h_attn_f, norm_back_attn = jax.vjp(rms_scale, x_f32, gain_attn)
            h_attn = gather_seq(h_attn_f.astype(jnp.bfloat16))
            w_qkv = gather_rows(wqkv_sh)
            qkv = jnp.einsum('bsd,dc->bsc', h_attn, w_qkv, preferred_element_type=jnp.float32)
            qkv = qkv.reshape(micro_rows, seq_full, local_kv, group_size + 2, head_dim)
            query = rotate(qkv[:, :, :, :group_size], cos_q, sin_q).astype(jnp.bfloat16)
            key_rot = rotate(qkv[:, :, :, group_size], cos_k, sin_k).astype(jnp.bfloat16)
            value = qkv[:, :, :, group_size + 1].astype(jnp.bfloat16)
            scores = jnp.einsum('bqkgd,btkd->bkgqt', query, key_rot, preferred_element_type=jnp.float32) * scale
            attn_prob = jax.nn.softmax(jnp.where(causal, scores, -1e30), axis=-1)
            prob_bf = attn_prob.astype(jnp.bfloat16)
            attn = jnp.einsum('bkgqt,btkd->bqkgd', prob_bf, value, preferred_element_type=jnp.float32)
            attn_flat = attn.astype(jnp.bfloat16).reshape(micro_rows, seq_full, local_heads * head_dim)
            w_out = gather_cols(wout_sh)
            attn_red = scatter_seq(jnp.einsum('bsh,hd->bsd', attn_flat, w_out, preferred_element_type=jnp.float32))
            mid_f32 = (x_f32 + attn_red.astype(jnp.bfloat16).astype(jnp.float32)).astype(jnp.bfloat16).astype(jnp.float32)
            h_mlp_f, norm_back_mlp = jax.vjp(rms_scale, mid_f32, gain_mlp)
            h_mlp = gather_seq(h_mlp_f.astype(jnp.bfloat16))
            w_gate = gather_rows(wgate_sh)
            w_up = gather_rows(wup_sh)
            gate = jnp.einsum('bsd,df->bsf', h_mlp, w_gate, preferred_element_type=jnp.float32)
            up_proj = jnp.einsum('bsd,df->bsf', h_mlp, w_up, preferred_element_type=jnp.float32)
            sig_gate = jax.nn.sigmoid(gate)
            silu_gate = gate * sig_gate
            gated_act = (silu_gate * up_proj).astype(jnp.bfloat16)
            w_down = gather_cols(wdown_sh)
            mlp_red = scatter_seq(jnp.einsum('bsf,fd->bsd', gated_act, w_down, preferred_element_type=jnp.float32))
            y_mb = (mid_f32 + mlp_red.astype(jnp.bfloat16).astype(jnp.float32)).astype(jnp.bfloat16)

            dy_full = gather_seq(dy_mb)
            w_down_b = gather_cols(wdown_sh)
            d_act = jnp.einsum('bsd,fd->bsf', dy_full, w_down_b, preferred_element_type=jnp.float32).astype(jnp.bfloat16).astype(jnp.float32)
            acc_down = acc_down + jnp.einsum('bsf,bsd->fd', gated_act, dy_full, preferred_element_type=jnp.float32)
            d_gate = (d_act * up_proj * sig_gate * (1.0 + gate * (1.0 - sig_gate))).astype(jnp.bfloat16)
            d_up = (d_act * silu_gate).astype(jnp.bfloat16)
            w_gate_b = gather_rows(wgate_sh)
            w_up_b = gather_rows(wup_sh)
            dh_mlp = scatter_seq(jnp.einsum('bsf,df->bsd', d_gate, w_gate_b, preferred_element_type=jnp.float32)
                                 + jnp.einsum('bsf,df->bsd', d_up, w_up_b, preferred_element_type=jnp.float32))
            acc_gate = acc_gate + jnp.einsum('bsd,bsf->df', h_mlp, d_gate, preferred_element_type=jnp.float32)
            acc_up = acc_up + jnp.einsum('bsd,bsf->df', h_mlp, d_up, preferred_element_type=jnp.float32)
            d_mid_norm, d_gain_mlp = norm_back_mlp(dh_mlp.astype(jnp.bfloat16).astype(jnp.float32))
            d_mid = (dy_mb.astype(jnp.float32) + d_mid_norm).astype(jnp.bfloat16)

            d_mid_full = gather_seq(d_mid)
            w_out_b = gather_cols(wout_sh)
            d_attn = jnp.einsum('bsd,hd->bsh', d_mid_full, w_out_b, preferred_element_type=jnp.float32).astype(jnp.bfloat16)
            acc_out = acc_out + jnp.einsum('bsh,bsd->hd', attn_flat, d_mid_full, preferred_element_type=jnp.float32)
            d_attn = d_attn.reshape(micro_rows, seq_full, local_kv, group_size, head_dim)
            d_prob = jnp.einsum('bqkgd,btkd->bkgqt', d_attn, value, preferred_element_type=jnp.float32)
            d_value = jnp.einsum('bkgqt,bqkgd->btkd', prob_bf, d_attn, preferred_element_type=jnp.float32)
            row_dot = jnp.sum(d_prob * attn_prob, axis=-1, keepdims=True)
            d_scores = (attn_prob * (d_prob - row_dot) * scale).astype(jnp.bfloat16)
            d_query = jnp.einsum('bkgqt,btkd->bqkgd', d_scores, key_rot, preferred_element_type=jnp.float32)
            d_key = jnp.einsum('bkgqt,bqkgd->btkd', d_scores, query, preferred_element_type=jnp.float32)
            d_qkv = jnp.concatenate([rotate_back(d_query, cos_q, sin_q),
                                     rotate_back(d_key, cos_k, sin_k)[:, :, :, None],
                                     d_value[:, :, :, None]], axis=3)
            d_qkv = d_qkv.astype(jnp.bfloat16).reshape(micro_rows, seq_full, -1)
            w_qkv_b = gather_rows(wqkv_sh)
            dh_attn = scatter_seq(jnp.einsum('bsc,dc->bsd', d_qkv, w_qkv_b, preferred_element_type=jnp.float32))
            acc_qkv = acc_qkv + jnp.einsum('bsd,bsc->dc', h_attn, d_qkv, preferred_element_type=jnp.float32)
            d_x_norm, d_gain_attn = norm_back_attn(dh_attn.astype(jnp.bfloat16).astype(jnp.float32))
            dx_mb = (d_mid.astype(jnp.float32) + d_x_norm).astype(jnp.bfloat16)
            new_accum = (acc_gattn + d_gain_attn, acc_gmlp + d_gain_mlp, acc_qkv, acc_out, acc_gate, acc_up, acc_down)
            return y_mb, dx_mb, new_accum

        accum = (jnp.zeros_like(gain_attn), jnp.zeros_like(gain_mlp),
                 jnp.zeros((wqkv_sh.shape[0] * fsdp_size, wqkv_sh.shape[1]), jnp.float32),
                 jnp.zeros((wout_sh.shape[0], wout_sh.shape[1] * fsdp_size), jnp.float32),
                 jnp.zeros((wgate_sh.shape[0] * fsdp_size, wgate_sh.shape[1]), jnp.float32),
                 jnp.zeros((wup_sh.shape[0] * fsdp_size, wup_sh.shape[1]), jnp.float32),
                 jnp.zeros((wdown_sh.shape[0], wdown_sh.shape[1] * fsdp_size), jnp.float32))
        y_parts = []
        dx_parts = []
        for micro_idx in range(2):
            lo_row = micro_idx * micro_rows
            y_mb, dx_mb, accum = micro_step(x_loc[lo_row:lo_row + micro_rows], dy_loc[lo_row:lo_row + micro_rows], accum)
            y_parts.append(y_mb)
            dx_parts.append(dx_mb)
        gain_grads = lax.psum((accum[0], accum[1]), ('fsdp', 'model'))
        return (jnp.concatenate(y_parts, axis=0), jnp.concatenate(dx_parts, axis=0), gain_grads[0], gain_grads[1],
                lax.psum_scatter(accum[2], 'fsdp', scatter_dimension=0, tiled=True),
                lax.psum_scatter(accum[3], 'fsdp', scatter_dimension=1, tiled=True),
                lax.psum_scatter(accum[4], 'fsdp', scatter_dimension=0, tiled=True),
                lax.psum_scatter(accum[5], 'fsdp', scatter_dimension=0, tiled=True),
                lax.psum_scatter(accum[6], 'fsdp', scatter_dimension=1, tiled=True))

    in_specs = (act_spec, act_spec, P(), P(), rows_spec, cols_spec, rows_spec, rows_spec, cols_spec, P(), P())
    out_specs = (act_spec, act_spec, P(), P(), rows_spec, cols_spec, rows_spec, rows_spec, cols_spec)
    return jax.shard_map(device_fn, mesh=mesh, in_specs=in_specs, out_specs=out_specs, check_vma=False)
```

profile of v0, /device:TPU:0, one launch (start us, length us, event | category | flops | bytes accessed | tf_op | source)
XLA Modules:
  0.0 1993.9 jit_solution(16706514760803160463)
XLA Ops:
  11.0 8.7 all_gather.26
  19.7 7.3 all_gather.61
  27.0 84.3 %all-gather.6.cloned.1.call-done = bf16[2048,1536]{1,0:T(8,128)(2,1)} async-done(((bf16[256,1536]{1,0:T(8,128)(2,1)}), bf16[2048,1536]{1,0:T(8,128)(2,1)}) %all-gather.6.cloned.1.call-update) | async-done | bytes 6291472 | tf_op jit(solution)/shard_map/all_gather | solution.py:35
  111.3 8.7 copy.45
  128.2 33.6 %all-gather.8.cloned.1.call-done = bf16[512,2048]{1,0:T(8,128)(2,1)} async-done(((bf16[512,256]{1,0:T(8,128)(2,1)}), bf16[512,2048]{1,0:T(8,128)(2,1)}) %all-gather.8.cloned.1.call-update) | async-done | bytes 2097168 | tf_op jit(solution)/shard_map/all_gather | solution.py:38
  171.9 6.9 all_gather.63
  178.9 9.1 reduce-scatter.18.cloned.1.call-done
  188.0 27.7 %reduce-scatter.14.cloned.1.call-done = f32[1,32,2048]{2,1,0:T(8,128)} async-done(((f32[1,128,2048]{2,1,0:T(8,128)}), f32[1,32,2048]{2,1,0:T(8,128)}) %reduce-scatter.14.cloned.1.call-update) | async-done | bytes 262160 | tf_op jit(solution)/shard_map/reduce_scatter | solution.py:44
  217.1 7.0 all_gather.57
  224.1 117.3 %all-gather.12.cloned.1.call-done = bf16[2048,2048]{1,0:T(8,128)(2,1)} async-done(((bf16[256,2048]{1,0:T(8,128)(2,1)}), bf16[2048,2048]{1,0:T(8,128)(2,1)}) %all-gather.12.cloned.1.call-update) | async-done | bytes 8388624 | tf_op jit(solution)/shard_map/all_gather | solution.py:35
  346.1 119.7 %all-gather.10.cloned.1.call-done = bf16[2048,2048]{1,0:T(8,128)(2,1)} async-done(((bf16[256,2048]{1,0:T(8,128)(2,1)}), bf16[2048,2048]{1,0:T(8,128)(2,1)}) %all-gather.10.cloned.1.call-update) | async-done | bytes 8388624 | tf_op jit(solution)/shard_map/all_gather | solution.py:35
  470.4 120.3 %all-gather.14.cloned.1.call-done = bf16[2048,2048]{1,0:T(8,128)(2,1)} async-done(((bf16[2048,256]{1,0:T(8,128)(2,1)}), bf16[2048,2048]{1,0:T(8,128)(2,1)}) %all-gather.14.cloned.1.call-update) | async-done | bytes 8388624 | tf_op jit(solution)/shard_map/all_gather | solution.py:38
  590.7 7.4 multiply_convert_fusion.2
  601.0 7.3 fusion.3
  608.4 7.1 all_gather.65
  615.6 16.0 reduce-scatter.22.cloned.1.call-done
  633.5 6.7 all_gather.62
  648.2 6.4 multiply_convert_fusion
  675.7 12.4 reduce-scatter.26.cloned.1.call-done
  690.9 24.8 %reduce-scatter.16.cloned.1.call-done = f32[1,32,2048]{2,1,0:T(8,128)} async-done(((f32[1,128,2048]{2,1,0:T(8,128)}), f32[1,32,2048]{2,1,0:T(8,128)}) %reduce-scatter.16.cloned.1.call-update) | async-done | bytes 262160 | tf_op jit(solution)/shard_map/reduce_scatter | solution.py:44
  715.7 27.8 %reduce-scatter.20.cloned.1.call-done = f32[1,32,2048]{2,1,0:T(8,128)} async-done(((f32[1,128,2048]{2,1,0:T(8,128)}), f32[1,32,2048]{2,1,0:T(8,128)}) %reduce-scatter.20.cloned.1.call-update) | async-done | bytes 262160 | tf_op jit(solution)/shard_map/reduce_scatter | solution.py:44
  746.4 6.5 all_gather.64
  761.2 7.3 all_gather.66
  808.8 8.2 convolution_add_fusion.1
  820.6 8.2 convolution_add_fusion.2
  832.2 8.2 convolution_add_fusion.3
  843.5 41.8 %all-reduce = (f32[2048]{0:T(1024)}, f32[2048]{0:T(1024)}) all-reduce(f32[2048]{0:T(1024)S(1)} %add.199, f32[2048]{0:T(1024)S(1)} %add.200), channel_id=1, replica_groups=mesh['fsdp'=8,'model'=4] {'fsdp','model'}, use_global_device_ids=true, to_apply=%region_24.25 | all-reduce | flops 4096 | bytes 32768 | tf_op jit(solution)/shard_map/psum | solution.py:144
  887.3 44.1 %reduce-scatter.32.cloned.1.call-done = f32[512,256]{1,0:T(8,128)} async-done(((f32[512,2048]{1,0:T(8,128)}), f32[512,256]{1,0:T(8,128)}) %reduce-scatter.32.cloned.1.call-update) | async-done | bytes 524304 | tf_op jit(solution)/shard_map/reduce_scatter | solution.py:147
  931.4 208.6 %reduce-scatter.30.cloned.1.call-done = f32[256,1536]{1,0:T(8,128)} async-done(((f32[2048,1536]{1,0:T(8,128)}), f32[256,1536]{1,0:T(8,128)}) %reduce-scatter.30.cloned.1.call-update) | async-done | bytes 1572880 | tf_op jit(solution)/shard_map/reduce_scatter | solution.py:146
  1140.0 282.1 %reduce-scatter.38.cloned.1.call-done = f32[2048,256]{1,0:T(8,128)} async-done(((f32[2048,2048]{1,0:T(8,128)}), f32[2048,256]{1,0:T(8,128)}) %reduce-scatter.38.cloned.1.call-update) | async-done | bytes 2097168 | tf_op jit(solution)/shard_map/reduce_scatter | solution.py:150
  1422.0 282.4 %reduce-scatter.36.cloned.1.call-done = f32[256,2048]{1,0:T(8,128)} async-done(((f32[2048,2048]{1,0:T(8,128)}), f32[256,2048]{1,0:T(8,128)}) %reduce-scatter.36.cloned.1.call-update) | async-done | bytes 2097168 | tf_op jit(solution)/shard_map/reduce_scatter | solution.py:149
  1704.4 282.4 %reduce-scatter.34.cloned.1.call-done = f32[256,2048]{1,0:T(8,128)} async-done(((f32[2048,2048]{1,0:T(8,128)}), f32[256,2048]{1,0:T(8,128)}) %reduce-scatter.34.cloned.1.call-update) | async-done | bytes 2097168 | tf_op jit(solution)/shard_map/reduce_scatter | solution.py:148
  (303 shorter events, 132.0 us)
Async XLA Ops:
  7.2 104.1 %all-gather.6.cloned.1.call-start = ((), (), s32[]{:S(2)}) async-start(), calls=%async_computation.13 | async-start | bytes 7077888 | tf_op jit(solution)/shard_map/all_gather | solution.py:35
  7.9 153.9 %all-gather.8.cloned.1.call-start = ((), (), s32[]{:S(2)}) async-start(), calls=%async_computation.14 | async-start | bytes 2359296 | tf_op jit(solution)/shard_map/all_gather | solution.py:38
  8.7 179.3 %reduce-scatter.18.cloned.1.call-start = ((), (), s32[]{:S(2)}) async-start(), calls=%async_computation.20 | async-start | bytes 1310720 | tf_op jit(solution)/shard_map/reduce_scatter | solution.py:44
  19.7 105.1 %copy-start.8 = (bf16[1,128,2048]{2,1,0:T(8,128)(2,1)}, bf16[1,128,2048]{2,1,0:T(8,128)(2,1)S(1)}, u32[]{:S(2)}) copy-start(bf16[1,128,2048]{2,1,0:T(8,128)(2,1)S(1)} %all_gather.26) | copy-start | bytes 1572868
  27.0 97.7 %copy-start.23 = (bf16[1,128,2048]{2,1,0:T(8,128)(2,1)}, bf16[1,128,2048]{2,1,0:T(8,128)(2,1)S(1)}, u32[]{:S(2)}) copy-start(bf16[1,128,2048]{2,1,0:T(8,128)(2,1)S(1)} %all_gather.61) | copy-start | bytes 1572868
  127.9 88.9 %copy-start.71 = (f32[4,128]{1,0:T(4,128)}, f32[4,128]{1,0:T(4,128)S(1)}, u32[]{:S(2)}) copy-start(f32[4,128]{1,0:T(4,128)S(1)} %fusion.83) | copy-start | bytes 6148
  127.9 87.7 %copy-start.5 = (bf16[2,32,2048]{2,1,0:T(8,128)(2,1)S(1)}, bf16[2,32,2048]{2,1,0:T(8,128)(2,1)}, u32[]{:S(2)}) copy-start(bf16[2,32,2048]{2,1,0:T(8,128)(2,1)} %param.11) | copy-start | bytes 786436
  128.1 88.9 %copy-start.43 = (bf16[4,128,128]{2,1,0:T(8,128)(2,1)}, bf16[4,128,128]{2,1,0:T(8,128)(2,1)S(1)}, u32[]{:S(2)}) copy-start(bf16[4,128,128]{2,1,0:T(8,128)(2,1)S(1)} %convolution_convert_fusion.4) | copy-start | bytes 393220
  128.1 88.8 %copy-start.63 = (f32[2048]{0:T(1024)S(1)}, f32[2048]{0:T(1024)}, u32[]{:S(2)}) copy-start(f32[2048]{0:T(1024)} %param.14) | copy-start | bytes 24580
  164.9 50.8 %reduce-scatter.14.cloned.1.call-start = ((), (), s32[]{:S(2)}) async-start(), calls=%async_computation.15 | async-start | bytes 1310720 | tf_op jit(solution)/shard_map/reduce_scatter | solution.py:44
  169.3 172.2 %all-gather.12.cloned.1.call-start = ((), (), s32[]{:S(2)}) async-start(), calls=%async_computation.17 | async-start | bytes 9437184 | tf_op jit(solution)/shard_map/all_gather | solution.py:35
  169.8 295.9 %all-gather.10.cloned.1.call-start = ((), (), s32[]{:S(2)}) async-start(), calls=%async_computation.16 | async-start | bytes 9437184 | tf_op jit(solution)/shard_map/all_gather | solution.py:35
  170.4 420.3 %all-gather.14.cloned.1.call-start = ((), (), s32[]{:S(2)}) async-start(), calls=%async_computation.18 | async-start | bytes 9437184 | tf_op jit(solution)/shard_map/all_gather | solution.py:38
  171.2 460.4 %reduce-scatter.22.cloned.1.call-start = ((), (), s32[]{:S(2)}) async-start(), calls=%async_computation.22 | async-start | bytes 1310720 | tf_op jit(solution)/shard_map/reduce_scatter | solution.py:44
  178.9 411.9 %copy-start.25 = (bf16[1,128,2048]{2,1,0:T(8,128)(2,1)}, bf16[1,128,2048]{2,1,0:T(8,128)(2,1)S(1)}, u32[]{:S(2)}) copy-start(bf16[1,128,2048]{2,1,0:T(8,128)(2,1)S(1)} %all_gather.63) | copy-start | bytes 1572868
  216.9 253.5 %copy-start.83 = (f32[32]{0:T(128)}, f32[32]{0:T(128)S(1)}, u32[]{:S(2)}) copy-start(f32[32]{0:T(128)S(1)} %get-tuple-element.23) | copy-start | bytes 388
  216.9 398.7 %copy-start.82 = (f32[32]{0:T(128)}, f32[32]{0:T(128)S(1)}, u32[]{:S(2)}) copy-start(f32[32]{0:T(128)S(1)} %get-tuple-element.55) | copy-start | bytes 388
  216.9 414.7 %copy-start.29 = (bf16[1,32,2048]{2,1,0:T(8,128)(2,1)}, bf16[1,32,2048]{2,1,0:T(8,128)(2,1)S(1)}, u32[]{:S(2)}) copy-start(bf16[1,32,2048]{2,1,0:T(8,128)(2,1)S(1)} %get-tuple-element.56) | copy-start | bytes 393220
  216.9 414.7 %copy-start.31 = (bf16[1,32,2048]{2,1,0:T(8,128)(2,1)}, bf16[1,32,2048]{2,1,0:T(8,128)(2,1)S(1)}, u32[]{:S(2)}) copy-start(bf16[1,32,2048]{2,1,0:T(8,128)(2,1)S(1)} %get-tuple-element.24) | copy-start | bytes 393220
  216.9 414.7 %copy-start.76 = (f32[32]{0:T(128)}, f32[32]{0:T(128)S(1)}, u32[]{:S(2)}) copy-start(f32[32]{0:T(128)S(1)} %fusion.112) | copy-start | bytes 388
  224.1 246.3 %copy-start.3 = (bf16[1,128,2048]{2,1,0:T(8,128)(2,1)}, bf16[1,128,2048]{2,1,0:T(8,128)(2,1)S(1)}, u32[]{:S(2)}) copy-start(bf16[1,128,2048]{2,1,0:T(8,128)(2,1)S(1)} %all_gather.57) | copy-start | bytes 1572868
  608.4 79.7 %reduce-scatter.26.cloned.1.call-start = ((), (), s32[]{:S(2)}) async-start(), calls=%async_computation.24 | async-start | bytes 1310720 | tf_op jit(solution)/shard_map/reduce_scatter | solution.py:44
  662.6 53.1 %reduce-scatter.16.cloned.1.call-start = ((), (), s32[]{:S(2)}) async-start(), calls=%async_computation.19 | async-start | bytes 1310720 | tf_op jit(solution)/shard_map/reduce_scatter | solution.py:44
  668.4 75.2 %reduce-scatter.20.cloned.1.call-start = ((), (), s32[]{:S(2)}) async-start(), calls=%async_computation.21 | async-start | bytes 1310720 | tf_op jit(solution)/shard_map/reduce_scatter | solution.py:44
  674.2 102.1 %copy-start.52 = (bf16[128,4,64]{0,2,1:T(8,128)(2,1)S(1)}, bf16[128,4,64]{0,2,1:T(8,128)(2,1)}, u32[]{:S(2)}) copy-start(bf16[128,4,64]{0,2,1:T(8,128)(2,1)} %copy-done.51) | copy-start | bytes 196612
  674.2 167.9 %reduce-scatter.28.cloned.1.call-start = ((), (), s32[]{:S(2)}) async-start(), calls=%async_computation.25 | async-start | bytes 1310720 | tf_op jit(solution)/shard_map/reduce_scatter | solution.py:44
  785.0 57.1 %reduce-scatter.24.cloned.1.call-start = ((), (), s32[]{:S(2)}) async-start(), calls=%async_computation.23 | async-start | bytes 1310720 | tf_op jit(solution)/shard_map/reduce_scatter | solution.py:44
  793.4 138.0 %reduce-scatter.32.cloned.1.call-start = ((), (), s32[]{:S(2)}) async-start(), calls=%async_computation.27 | async-start | bytes 4718592 | tf_op jit(solution)/shard_map/reduce_scatter | solution.py:147
  796.9 343.0 %reduce-scatter.30.cloned.1.call-start = ((), (), s32[]{:S(2)}) async-start(), calls=%async_computation.26 | async-start | bytes 14155776 | tf_op jit(solution)/shard_map/reduce_scatter | solution.py:146
  805.3 616.7 %reduce-scatter.38.cloned.1.call-start = ((), (), s32[]{:S(2)}) async-start(), calls=%async_computation.30 | async-start | bytes 18874368 | tf_op jit(solution)/shard_map/reduce_scatter | solution.py:150
  817.1 887.4 %reduce-scatter.36.cloned.1.call-start = ((), (), s32[]{:S(2)}) async-start(), calls=%async_computation.29 | async-start | bytes 18874368 | tf_op jit(solution)/shard_map/reduce_scatter | solution.py:149
  828.8 1158.0 %reduce-scatter.34.cloned.1.call-start = ((), (), s32[]{:S(2)}) async-start(), calls=%async_computation.28 | async-start | bytes 18874368 | tf_op jit(solution)/shard_map/reduce_scatter | solution.py:148
  (78 other events, 1348.6 us)
Sparse Core Ops, SparseCore 0:
  10.2 101.0 all-gather.5
  113.3 48.4 all-gather.7
  165.0 22.9 reduce-scatter.17
  190.9 24.6 reduce-scatter.13
  217.6 123.7 all-gather.11
  343.4 122.2 all-gather.9
  467.8 122.9 all-gather.13
  608.5 23.0 reduce-scatter.21
  662.7 25.2 reduce-scatter.25
  691.0 24.6 reduce-scatter.15
  718.8 24.6 reduce-scatter.19
  785.1 25.3 reduce-scatter.27
  813.0 24.6 reduce-scatter.23
  841.8 89.5 reduce-scatter.31
  935.4 204.5 reduce-scatter.29
  1144.2 277.8 reduce-scatter.37
  1426.3 278.1 reduce-scatter.35
  1708.7 278.1 reduce-scatter.33
where the time goes:
time: 2000 us; the launch traced here: 1990 us
  waiting for transfers between devices  1700 us (85%)
  matrix products  140 us (7%)
  blocking collectives  99.4 us (5%)
  other arithmetic  22.5 us (1%)
    all_gather x3, waiting for transfers between devices, gather_rows(): return lax.all_gather(w_shard, 'fsdp', axis=0, tiled=True)  321 us
    reduce_scatter x1, waiting for transfers between devices, device_fn(): lax.psum_scatter(accum[4], 'fsdp', scatter_dimension=0, tiled=True)  282 us
    reduce_scatter x1, waiting for transfers between devices, device_fn(): lax.psum_scatter(accum[5], 'fsdp', scatter_dimension=0, tiled=True)  282 us
    reduce_scatter x1, waiting for transfers between devices, device_fn(): lax.psum_scatter(accum[6], 'fsdp', scatter_dimension=1, tiled=True)  282 us
    reduce_scatter x1, waiting for transfers between devices, device_fn(): lax.psum_scatter(accum[2], 'fsdp', scatter_dimension=0, tiled=True)  209 us
    all_gather x2, waiting for transfers between devices, gather_cols(): return lax.all_gather(w_shard, 'fsdp', axis=1, tiled=True)  154 us
    reduce_scatter x8, waiting for transfers between devices, scatter_seq(): return lax.psum_scatter(tensor, 'model', scatter_dimension=1, tiled=True)  118 us
    all_gather x8, blocking collectives, gather_seq(): return lax.all_gather(tensor, 'model', axis=1, tiled=True)  57.6 us
  transfers between devices with their start and end apart: 18, of which 16 were waited for; matrix products, arithmetic and copies ran while one was open for 5% of the time, Pallas kernels for 0%

commit v1 on v0

v1 whole, which is shorter than its diff:
```python
import functools

import jax
import jax.numpy as jnp
from jax import lax
from jax.experimental import pallas as pl
from jax.experimental.pallas import tpu as pltpu
from jax.sharding import PartitionSpec as P

NORM_EPS = 1e-5
MESH = pl.DeviceIdType.MESH


def rms_scale(x_f32, gain):
    inv_rms = lax.rsqrt(jnp.mean(x_f32 * x_f32, axis=-1, keepdims=True) + NORM_EPS)
    return x_f32 * inv_rms * gain


def rotate(tensor, cos_t, sin_t):
    half = tensor.shape[-1] // 2
    first = tensor[..., :half]
    second = tensor[..., half:]
    return jnp.concatenate([first * cos_t - second * sin_t, second * cos_t + first * sin_t], axis=-1)


def rotate_back(cotangent, cos_t, sin_t):
    half = cotangent.shape[-1] // 2
    first = cotangent[..., :half]
    second = cotangent[..., half:]
    return jnp.concatenate([first * cos_t + second * sin_t, second * cos_t - first * sin_t], axis=-1)


def ring_place(index):
    z, y = index // 2, index % 2
    return z + y * (7 - 2 * z)


def ring_device(place):
    y = place // 4
    return 2 * (place + y * (7 - 2 * place)) + y


def ring_kernel(dims, *refs):
    count = len(dims)
    ins, outs = refs[:count], refs[count:2 * count]
    send_sem, recv_sem, local_sem = refs[2 * count:]
    me = lax.axis_index('fsdp')
    place = ring_place(me)
    targets = (ring_device((place + 1) % 8), ring_device((place + 7) % 8))

    barrier = pltpu.get_barrier_semaphore()
    for target in targets:
        pl.semaphore_signal(barrier, inc=1, device_id={'fsdp': target}, device_id_type=MESH)
    pl.semaphore_wait(barrier, 2)

    def piece(idx, owner, way):
        rows, cols = ins[idx].shape
        half = rows // 2
        if dims[idx] == 0:
            start = pl.multiple_of(owner * rows + way * half, half)
            return outs[idx].at[pl.ds(start, half), :]
        return outs[idx].at[pl.ds(way * half, half), pl.ds(pl.multiple_of(owner * cols, cols), cols)]

    def send(idx, way, step):
        owner = ring_device((place + (8 - step if way == 0 else step)) % 8)
        dst = piece(idx, owner, way)
        half = ins[idx].shape[0] // 2
        src = ins[idx].at[pl.ds(way * half, half), :] if step == 0 else dst
        return pltpu.make_async_remote_copy(
            src_ref=src, dst_ref=dst, send_sem=send_sem.at[idx, way, step], recv_sem=recv_sem.at[idx, way, step],
            device_id={'fsdp': targets[way]}, device_id_type=MESH)

    def landed(idx, way, step):
        owner = ring_device((place + (7 - step if way == 0 else step + 1)) % 8)
        dst = piece(idx, owner, way)
        return pltpu.make_async_remote_copy(
            src_ref=dst, dst_ref=dst, send_sem=send_sem.at[idx, way, step], recv_sem=recv_sem.at[idx, way, step],
            device_id={'fsdp': targets[way]}, device_id_type=MESH)

    def own(idx, way):
        half = ins[idx].shape[0] // 2
        return pltpu.make_async_copy(ins[idx].at[pl.ds(way * half, half), :], piece(idx, me, way), local_sem.at[idx, way])

    for step in range(7):
        for idx in range(count):
            for way in range(2):
                if step > 0:
                    landed(idx, way, step - 1).wait_recv()
                send(idx, way, step).start()
                if step == 0:
                    own(idx, way).start()
    for idx in range(count):
        for way in range(2):
            landed(idx, way, 6).wait_recv()
            own(idx, way).wait()
            for step in range(7):
                send(idx, way, step).wait_send()


def ring_gather(arrays, dims, collective_id):
    shapes = []
    for array, dim in zip(arrays, dims):
        shape = list(array.shape)
        shape[dim] *= 8
        shapes.append(jax.ShapeDtypeStruct(tuple(shape), array.dtype))
    count = len(arrays)
    return pl.pallas_call(
        functools.partial(ring_kernel, tuple(dims)),
        out_shape=shapes,
        in_specs=[pl.BlockSpec(memory_space=pl.ANY)] * count,
        out_specs=[pl.BlockSpec(memory_space=pl.ANY)] * count,
        scratch_shapes=[pltpu.SemaphoreType.DMA((count, 2, 7)), pltpu.SemaphoreType.DMA((count, 2, 7)),
                        pltpu.SemaphoreType.DMA((count, 2))],
        compiler_params=pltpu.CompilerParams(collective_id=collective_id, has_side_effects=True),
        name=f'ring_gather_{collective_id}',
    )(*arrays)


def solution(mesh):
    act_spec = P('fsdp', 'model', None)
    rows_spec = P('fsdp', 'model')
    cols_spec = P('model', 'fsdp')
    f32 = jnp.float32
    bf16 = jnp.bfloat16

    def gather_seq(tensor):
        return lax.all_gather(tensor, 'model', axis=1, tiled=True)

    def scatter_seq(tensor):
        return lax.psum_scatter(tensor, 'model', scatter_dimension=1, tiled=True)

    def device_fn(x_loc, dy_loc, gain_attn, gain_mlp, wqkv_sh, wout_sh, wgate_sh, wup_sh, wdown_sh, rope_cos, rope_sin):
        head_dim = 2 * rope_cos.shape[1]
        seq_full = rope_cos.shape[0]
        local_heads = wout_sh.shape[0] // head_dim
        local_kv = (wqkv_sh.shape[1] // head_dim - local_heads) // 2
        group_size = local_heads // local_kv
        rows = x_loc.shape[0]
        tokens = rows * seq_full
        scale = head_dim ** -0.5
        pos_ids = jnp.arange(seq_full)
        causal = pos_ids[:, None] >= pos_ids[None, :]
        cos_q = rope_cos[:, None, None, :]
        sin_q = rope_sin[:, None, None, :]
        cos_k = rope_cos[:, None, :]
        sin_k = rope_sin[:, None, :]

        w_qkv, w_out, w_gate, w_up, w_down = ring_gather(
            [wqkv_sh, wout_sh, wgate_sh, wup_sh, wdown_sh], [0, 1, 0, 0, 1], 0)

        x_f32 = x_loc.astype(f32)
        h_attn_f, norm_back_attn = jax.vjp(rms_scale, x_f32, gain_attn)
        h_attn_loc = h_attn_f.astype(bf16)
        h_attn = gather_seq(h_attn_loc)
        dy_full = gather_seq(dy_loc)
        qkv = jnp.einsum('bsd,dc->bsc', h_attn, w_qkv, preferred_element_type=f32)
        qkv = qkv.reshape(rows, seq_full, local_kv, group_size + 2, head_dim)
        query = rotate(qkv[:, :, :, :group_size], cos_q, sin_q).astype(bf16)
        key_rot = rotate(qkv[:, :, :, group_size], cos_k, sin_k).astype(bf16)
        value = qkv[:, :, :, group_size + 1].astype(bf16)
        scores = jnp.einsum('bqkgd,btkd->bkgqt', query, key_rot, preferred_element_type=f32) * scale
        attn_prob = jax.nn.softmax(jnp.where(causal, scores, -1e30), axis=-1)
        prob_bf = attn_prob.astype(bf16)
        attn = jnp.einsum('bkgqt,btkd->bqkgd', prob_bf, value, preferred_element_type=f32)
        attn_flat = attn.astype(bf16).reshape(rows, seq_full, local_heads * head_dim)
        attn_red = scatter_seq(jnp.einsum('bsh,hd->bsd', attn_flat, w_out, preferred_element_type=f32))
        mid_f32 = (x_f32 + attn_red.astype(bf16).astype(f32)).astype(bf16).astype(f32)
        h_mlp_f, norm_back_mlp = jax.vjp(rms_scale, mid_f32, gain_mlp)
        h_mlp_loc = h_mlp_f.astype(bf16)
        h_mlp = gather_seq(h_mlp_loc)
        gate = jnp.einsum('bsd,df->bsf', h_mlp, w_gate, preferred_element_type=f32)
        up_proj = jnp.einsum('bsd,df->bsf', h_mlp, w_up, preferred_element_type=f32)
        sig_gate = jax.nn.sigmoid(gate)
        silu_gate = gate * sig_gate
        gated_act = (silu_gate * up_proj).astype(bf16)
        mlp_red = scatter_seq(jnp.einsum('bsf,fd->bsd', gated_act, w_down, preferred_element_type=f32))
        y_loc = (mid_f32 + mlp_red.astype(bf16).astype(f32)).astype(bf16)

        d_act = jnp.einsum('bsd,fd->bsf', dy_full, w_down, preferred_element_type=f32).astype(bf16).astype(f32)
        d_gate = (d_act * up_proj * sig_gate * (1.0 + gate * (1.0 - sig_gate))).astype(bf16)
        d_up = (d_act * silu_gate).astype(bf16)
        dh_mlp = scatter_seq(jnp.einsum('bsf,df->bsd', d_gate, w_gate, preferred_element_type=f32)
                             + jnp.einsum('bsf,df->bsd', d_up, w_up, preferred_element_type=f32))
        d_mid_norm, d_gain_mlp = norm_back_mlp(dh_mlp.astype(bf16).astype(f32))
        d_mid = (dy_loc.astype(f32) + d_mid_norm).astype(bf16)

        d_mid_full = gather_seq(d_mid)
        d_attn = jnp.einsum('bsd,hd->bsh', d_mid_full, w_out, preferred_element_type=f32).astype(bf16)
        d_attn = d_attn.reshape(rows, seq_full, local_kv, group_size, head_dim)
        d_prob = jnp.einsum('bqkgd,btkd->bkgqt', d_attn, value, preferred_element_type=f32)
        d_value = jnp.einsum('bkgqt,bqkgd->btkd', prob_bf, d_attn, preferred_element_type=f32)
        row_dot = jnp.sum(d_prob * attn_prob, axis=-1, keepdims=True)
        d_scores = (attn_prob * (d_prob - row_dot) * scale).astype(bf16)
        d_query = jnp.einsum('bkgqt,btkd->bqkgd', d_scores, key_rot, preferred_element_type=f32)
        d_key = jnp.einsum('bkgqt,bqkgd->btkd', d_scores, query, preferred_element_type=f32)
        d_qkv = jnp.concatenate([rotate_back(d_query, cos_q, sin_q),
                                 rotate_back(d_key, cos_k, sin_k)[:, :, :, None],
                                 d_value[:, :, :, None]], axis=3)
        d_qkv = d_qkv.astype(bf16).reshape(rows, seq_full, -1)
        dh_attn = scatter_seq(jnp.einsum('bsc,dc->bsd', d_qkv, w_qkv, preferred_element_type=f32))
        d_x_norm, d_gain_attn = norm_back_attn(dh_attn.astype(bf16).astype(f32))
        dx_loc = (d_mid.astype(f32) + d_x_norm).astype(bf16)
        gain_grads = lax.psum((d_gain_attn, d_gain_mlp), ('fsdp', 'model'))

        fsdp_size = 8
        width = x_loc.shape[2] // fsdp_size
        pos_loc = x_loc.shape[1]
        packed = jnp.stack([h_attn_loc, h_mlp_loc, dy_loc, d_mid], axis=0)
        packed = packed.reshape(4, rows, pos_loc, fsdp_size, width).transpose(3, 0, 1, 2, 4)
        packed = lax.all_to_all(packed, 'fsdp', 0, 0, tiled=True)
        packed = lax.all_gather(packed, 'model', axis=0)
        packed = packed.transpose(2, 1, 3, 0, 4, 5).reshape(4, fsdp_size * tokens, width)

        d_qkv_all, attn_all, d_gate_all, d_up_all, act_all = ring_gather(
            [d_qkv.reshape(tokens, -1), attn_flat.reshape(tokens, -1), d_gate.reshape(tokens, -1),
             d_up.reshape(tokens, -1), gated_act.reshape(tokens, -1)], [0, 0, 0, 0, 0], 1)

        def pair(left, right):
            return lax.dot_general(left, right, (((0,), (0,)), ((), ())), preferred_element_type=f32)

        return (y_loc, dx_loc, gain_grads[0], gain_grads[1],
                pair(packed[0], d_qkv_all), pair(attn_all, packed[3]),
                pair(packed[1], d_gate_all), pair(packed[1], d_up_all), pair(act_all, packed[2]))

    in_specs = (act_spec, act_spec, P(), P(), rows_spec, cols_spec, rows_spec, rows_spec, cols_spec, P(), P())
    out_specs = (act_spec, act_spec, P(), P(), rows_spec, cols_spec, rows_spec, rows_spec, cols_spec)
    return jax.shard_map(device_fn, mesh=mesh, in_specs=in_specs, out_specs=out_specs, check_vma=False)
```

time: 2000 us -> 961 us (0.48)
  waiting for transfers between devices: 1700 us -> 132 us
  Pallas kernels: 0 us -> 639 us
  matrix products: 140 us -> 73.5 us
  blocking collectives: 99.4 us -> 71 us
    reduce_scatter x5 -> x0, waiting for transfers between devices: 1100 us -> none  [the longest x1 282 us: device_fn(): lax.psum_scatter(accum[4], 'fsdp', scatter_dimension=0, tiled=True)]
    pallas_call x0 -> x2, Pallas kernels: none -> 639 us  [ring_gather(): pl.pallas_call(functools.partial(ring_kernel, tuple(dims)), out_shape=sha...]
    all_gather x5, waiting for transfers between devices: 475 us -> 44 us  [the longest x4 44 us: gather_seq(): return lax.all_gather(tensor, 'model', axis=1, tiled=True)]
    dot_general x42 -> x21, matrix products: 140 us -> 73.5 us  [the longest x5 19.2 us: pair(): lax.dot_general(left, right, (((0,), (0,)), ((), ())), preferred_element_...]
    all_gather x8 -> x0, blocking collectives: 57.6 us -> none  [gather_seq(): return lax.all_gather(tensor, 'model', axis=1, tiled=True)]
    all_to_all x0 -> x1, blocking collectives: none -> 31.5 us  [device_fn(): packed = lax.all_to_all(packed, 'fsdp', 0, 0, tiled=True)]
    reduce_scatter x8 -> x4, waiting for transfers between devices: 118 us -> 87.3 us  [scatter_seq(): return lax.psum_scatter(tensor, 'model', scatter_dimension=1, tiled=True)]
  transfers between devices with their start and end apart: 18 -> 9, of which waited for: 16 -> 6; matrix products, arithmetic and copies ran while one was open for 5% -> 3% of each run, Pallas kernels for 0% -> 67%
where the time goes in v1:
time: 961 us; the launch traced here: 957 us
  Pallas kernels  639 us (66%)
  waiting for transfers between devices  132 us (14%)
  matrix products  73.5 us (8%)
  blocking collectives  71 us (7%)
  between operations  14.6 us (2%)
  other arithmetic  13.2 us (1%)
  local copies, waits for them, and re-layouts  11.9 us (1%)
    pallas_call x2, Pallas kernels, ring_gather(): pl.pallas_call(functools.partial(ring_kernel, tuple(dims)), out_shape=sha...  639 us
    reduce_scatter x4, waiting for transfers between devices, scatter_seq(): return lax.psum_scatter(tensor, 'model', scatter_dimension=1, tiled=True)  87.3 us
    all_gather x4, waiting for transfers between devices, gather_seq(): return lax.all_gather(tensor, 'model', axis=1, tiled=True)  44 us
    psum x1, blocking collectives, device_fn(): gain_grads = lax.psum((d_gain_attn, d_gain_mlp), ('fsdp', 'model'))  39.4 us
    all_to_all x1, blocking collectives, device_fn(): packed = lax.all_to_all(packed, 'fsdp', 0, 0, tiled=True)  31.5 us
  transfers between devices with their start and end apart: 9, of which 6 were waited for; matrix products, arithmetic and copies ran while one was open for 3% of the time, Pallas kernels for 67%

profile of v1, /device:TPU:0, one launch (start us, length us, event | category | flops | bytes accessed | tf_op | source)
XLA Modules:
  0.0 956.5 jit_solution(2792664229732085010)
XLA Ops:
  8.3 1.8 fusion.43
  11.9 321.3 %ring_gather_0.1 = (bf16[2048,1536]{1,0:T(8,128)(2,1)}, bf16[512,2048]{1,0:T(8,128)(2,1)}, bf16[2048,2048]{1,0:T(8,128)(2,1)}, bf16[2048,2048]{1,0:T(8,128)(2,1)}, bf16[2048,2048]{1,0:T(8,128)(2,1)}) custom-call(bf16[256,1536]{1,0:T(8,128)(2,1)} %refs_0_.1, bf16[512,256]{1,0:T(8,128)(2,1)} %refs_1_.1, bf16[256,2048]{1,0:T(8,128)(2,1)} %refs_2_.1, ...), custom_call_target="tpu_custom_call" | custom-call | tf_op jit(solution)/shard_map/ring_gather_0/pallas_call | solution.py:107
  333.3 4.9 fusion.14
  340.9 1.4 convolution_convert_fusion
  342.3 2.0 fusion.30
  345.2 30.7 %reduce-scatter.5.cloned.1.call-done = f32[2,32,2048]{2,1,0:T(8,128)} async-done(((f32[2,128,2048]{2,1,0:T(8,128)}), f32[2,32,2048]{2,1,0:T(8,128)}) %reduce-scatter.5.cloned.1.call-update) | async-done | bytes 524304 | tf_op jit(solution)/shard_map/reduce_scatter | solution.py:130
  378.4 15.7 %all-gather.11.cloned.1.call-done = bf16[2,128,2048]{2,1,0:T(8,128)(2,1)} async-done(((bf16[2,32,2048]{2,1,0:T(8,128)(2,1)}), bf16[2,128,2048]{2,1,0:T(8,128)(2,1)}) %all-gather.11.cloned.1.call-update) | async-done | bytes 1048592 | tf_op jit(solution)/shard_map/all_gather | solution.py:127
  394.1 7.3 fusion.25
  401.4 11.4 %all-gather.9.cloned.1.call-done = bf16[2,128,2048]{2,1,0:T(8,128)(2,1)} async-done(((bf16[2,32,2048]{2,1,0:T(8,128)(2,1)}), bf16[2,128,2048]{2,1,0:T(8,128)(2,1)}) %all-gather.9.cloned.1.call-update) | async-done | bytes 1048592 | tf_op jit(solution)/shard_map/all_gather | solution.py:127
  412.9 6.2 fusion.6
  419.1 7.7 multiply_convert_fusion.1
  426.9 2.4 fusion.4
  429.3 3.7 fusion.16
  433.2 7.4 fusion.2
  440.7 23.7 %reduce-scatter.9.cloned.1.call-done = f32[2,32,2048]{2,1,0:T(8,128)} async-done(((f32[2,128,2048]{2,1,0:T(8,128)}), f32[2,32,2048]{2,1,0:T(8,128)}) %reduce-scatter.9.cloned.1.call-update) | async-done | bytes 524304 | tf_op jit(solution)/shard_map/reduce_scatter | solution.py:130
  465.6 32.9 %reduce-scatter.7.cloned.1.call-done = f32[2,32,2048]{2,1,0:T(8,128)} async-done(((f32[2,128,2048]{2,1,0:T(8,128)}), f32[2,32,2048]{2,1,0:T(8,128)}) %reduce-scatter.7.cloned.1.call-update) | async-done | bytes 524304 | tf_op jit(solution)/shard_map/reduce_scatter | solution.py:130
  498.5 2.2 fusion.47
  500.8 16.8 %all-gather.13.cloned.1.call-done = bf16[2,128,2048]{2,1,0:T(8,128)(2,1)} async-done(((bf16[2,32,2048]{2,1,0:T(8,128)(2,1)}), bf16[2,128,2048]{2,1,0:T(8,128)(2,1)}) %all-gather.13.cloned.1.call-update) | async-done | bytes 1048592 | tf_op jit(solution)/shard_map/all_gather | solution.py:127
  517.6 2.7 fusion.34
  520.7 1.3 multiply_reduce_fusion
  524.2 6.0 fusion.12
  531.7 31.5 %all_to_all.5 = bf16[8,4,2,32,256]{4,3,2,1,0:T(8,128)(2,1)} all-to-all(bf16[8,4,2,32,256]{4,3,2,1,0:T(8,128)(2,1)S(1)} %copy.192), channel_id=1, replica_groups=mesh['fsdp'=8,'model'=4] {'fsdp'}, dimensions={0} | all-to-all | bytes 2097152 | tf_op jit(solution)/shard_map/all_to_all | solution.py:210
  564.9 1.4 reshape.173.refs_0_
  566.3 318.0 %ring_gather_1.1 = (bf16[2048,1536]{1,0:T(8,128)(2,1)}, bf16[2048,512]{1,0:T(8,128)(2,1)}, bf16[2048,2048]{1,0:T(8,128)(2,1)}, bf16[2048,2048]{1,0:T(8,128)(2,1)}, bf16[2048,2048]{1,0:T(8,128)(2,1)}) custom-call(bf16[256,1536]{1,0:T(8,128)(2,1)} %reshape.173.refs_0_, bf16[256,512]{1,0:T(8,128)(2,1)} %bitcast.161, bf16[256,2048]{1,0:T(8,128)(2,1)} %bitcast.164, ...), custom_call_target="tpu_custom_call" | custom-call | tf_op jit(solution)/shard_map/ring_gather_1/pallas_call | solution.py:107
  885.5 39.4 %all-reduce = (f32[2048]{0:T(1024)}, f32[2048]{0:T(1024)}) all-reduce(f32[2048]{0:T(1024)S(1)} %get-tuple-element.31, f32[2048]{0:T(1024)S(1)} %get-tuple-element.29), channel_id=1, replica_groups=mesh['fsdp'=8,'model'=4] {'fsdp','model'}, use_global_device_ids=true, to_apply=%region_12.13 | all-reduce | flops 4096 | bytes 32768 | tf_op jit(solution)/shard_map/psum | solution.py:203
  925.0 1.9 fusion.49
  926.9 3.0 fusion.76
  930.3 7.2 fusion.81
  937.5 3.7 fusion.82
  941.3 2.9 fusion.79
  944.3 1.5 fusion.80
  945.9 3.8 fusion.83
  (118 shorter events, 17.9 us)
Async XLA Ops:
  7.2 326.1 %all-gather.7.cloned.1.call-start = ((), (), s32[]{:S(2)}) async-start(), calls=%async_computation.5 | async-start | bytes 1310720 | tf_op jit(solution)/shard_map/all_gather | solution.py:127
  10.1 365.7 %reduce-scatter.5.cloned.1.call-start = ((), (), s32[]{:S(2)}) async-start(), calls=%async_computation.6 | async-start | bytes 2621440 | tf_op jit(solution)/shard_map/reduce_scatter | solution.py:130
  338.2 1.1 copy-start.9
  340.4 1.9 copy-start.6
  344.4 31.5 %copy-start = (bf16[2,32,2048]{2,1,0:T(8,128)(2,1)S(1)}, bf16[2,32,2048]{2,1,0:T(8,128)(2,1)}, u32[]{:S(2)}) copy-start(bf16[2,32,2048]{2,1,0:T(8,128)(2,1)} %param.11) | copy-start | bytes 786436
  344.4 32.7 %copy-start.10 = (f32[2048]{0:T(1024)S(1)}, f32[2048]{0:T(1024)}, u32[]{:S(2)}) copy-start(f32[2048]{0:T(1024)} %param.14) | copy-start | bytes 24580
  344.4 49.7 %all-gather.11.cloned.1.call-start = ((), (), s32[]{:S(2)}) async-start(), calls=%async_computation.9 | async-start | bytes 1310720 | tf_op jit(solution)/shard_map/all_gather | solution.py:127
  345.1 67.7 %all-gather.9.cloned.1.call-start = ((), (), s32[]{:S(2)}) async-start(), calls=%async_computation.7 | async-start | bytes 1310720 | tf_op jit(solution)/shard_map/all_gather | solution.py:127
  377.9 86.4 %reduce-scatter.9.cloned.1.call-start = ((), (), s32[]{:S(2)}) async-start(), calls=%async_computation.10 | async-start | bytes 2621440 | tf_op jit(solution)/shard_map/reduce_scatter | solution.py:130
  412.9 6.2 copy-start.12
  412.9 6.2 copy-start.13
  412.9 14.0 %slice-start.6 = ((s8[8388608]{0:T(1024)(128)(4,1)}), s8[4194304]{0:T(1024)(128)(4,1)S(1)}, s32[]{:S(2)}) async-start(s8[8388608]{0:T(1024)(128)(4,1)} %bitcast.180), calls=%async_computation.20 | async-start | bytes 8388608
  412.9 16.4 %slice-start.4 = ((s8[8388608]{0:T(1024)(128)(4,1)}), s8[4194304]{0:T(1024)(128)(4,1)S(1)}, s32[]{:S(2)}) async-start(s8[8388608]{0:T(1024)(128)(4,1)} %bitcast.178), calls=%async_computation.18 | async-start | bytes 8388608
  419.1 7.8 slice-start.7
  419.1 10.2 %slice-start.5 = ((s8[8388608]{0:T(1024)(128)(4,1)}), s8[4194304]{0:T(1024)(128)(4,1)S(1)}, s32[]{:S(2)}) async-start(s8[8388608]{0:T(1024)(128)(4,1)} %bitcast.178), calls=%async_computation.19 | async-start | bytes 8388608
  426.8 2.4 copy-start.8
  426.8 2.4 copy-start.7
  433.0 65.5 %reduce-scatter.7.cloned.1.call-start = ((), (), s32[]{:S(2)}) async-start(), calls=%async_computation.8 | async-start | bytes 2621440 | tf_op jit(solution)/shard_map/reduce_scatter | solution.py:130
  440.6 57.9 %copy-start.2 = (bf16[2,32,2048]{2,1,0:T(8,128)(2,1)S(1)}, bf16[2,32,2048]{2,1,0:T(8,128)(2,1)}, u32[]{:S(2)}) copy-start(bf16[2,32,2048]{2,1,0:T(8,128)(2,1)} %param.12) | copy-start | bytes 786436
  440.6 77.0 %all-gather.13.cloned.1.call-start = ((), (), s32[]{:S(2)}) async-start(), calls=%async_computation.11 | async-start | bytes 1310720 | tf_op jit(solution)/shard_map/all_gather | solution.py:127
  500.7 383.6 %reduce-scatter.11.cloned.1.call-start = ((), (), s32[]{:S(2)}) async-start(), calls=%async_computation.12 | async-start | bytes 2621440 | tf_op jit(solution)/shard_map/reduce_scatter | solution.py:130
  530.1 1.0 copy-start.4
  530.1 1.1 copy-start.1
  530.2 396.8 %all-gather.15.cloned.1.call-start = ((), (), s32[]{:S(2)}) async-start(), calls=%async_computation.13 | async-start | bytes 5242880 | tf_op jit(solution)/shard_map/all_gather | solution.py:211
  566.3 318.0 %copy-start.11 = (f32[2048]{0:T(1024)S(1)}, f32[2048]{0:T(1024)}, u32[]{:S(2)}) copy-start(f32[2048]{0:T(1024)} %param.13) | copy-start | bytes 24580
  930.1 7.3 slice-start.2
  930.3 7.2 slice-start.3
  937.5 3.8 slice-start
  937.5 3.8 slice-start.1
  941.3 4.6 slice-start.8
  941.3 3.0 copy-start.5
  941.3 4.6 slice-start.9
  (1 other events, 0.9 us)
Sparse Core Ops, SparseCore 0:
  10.3 19.4 all-gather.6
  344.5 31.2 reduce-scatter.4
  377.4 16.6 all-gather.10
  396.1 16.6 all-gather.8
  433.1 31.1 reduce-scatter.8
  467.3 31.1 reduce-scatter.6
  500.9 16.6 all-gather.12
  530.3 31.1 reduce-scatter.10
  563.4 34.1 all-gather.14

commit v2 on v1

--- a/solution.py
+++ b/solution.py
@@ -40,18 +40,31 @@
     return 2 * (place + y * (7 - 2 * place)) + y
 
 
-def ring_kernel(dims, *refs):
+def ring_kernel(dims, slices, sums, *refs):
     count = len(dims)
-    ins, outs = refs[:count], refs[count:2 * count]
-    send_sem, recv_sem, local_sem = refs[2 * count:]
+    total = count + slices + sums
+    ins, outs = refs[:total], refs[total:2 * total]
+    send_sem, recv_sem, local_sem, slice_send, slice_recv, slice_local, sum_send, sum_recv, sum_local = refs[2 * total:]
     me = lax.axis_index('fsdp')
+    me_model = lax.axis_index('model')
+    me_all = 4 * me + me_model
     place = ring_place(me)
     targets = (ring_device((place + 1) % 8), ring_device((place + 7) % 8))
 
     barrier = pltpu.get_barrier_semaphore()
-    for target in targets:
-        pl.semaphore_signal(barrier, inc=1, device_id={'fsdp': target}, device_id_type=MESH)
-    pl.semaphore_wait(barrier, 2)
+    if sums:
+        for hop in range(1, 32):
+            peer = (me_all + hop) % 32
+            pl.semaphore_signal(barrier, inc=1, device_id={'fsdp': peer // 4, 'model': peer % 4}, device_id_type=MESH)
+        pl.semaphore_wait(barrier, 31)
+    elif slices:
+        for hop in range(1, 8):
+            pl.semaphore_signal(barrier, inc=1, device_id={'fsdp': (me + hop) % 8}, device_id_type=MESH)
+        pl.semaphore_wait(barrier, 7)
+    else:
+        for target in targets:
+            pl.semaphore_signal(barrier, inc=1, device_id={'fsdp': target}, device_id_type=MESH)
+        pl.semaphore_wait(barrier, 2)
 
     def piece(idx, owner, way):
         rows, cols = ins[idx].shape
@@ -81,13 +94,53 @@
         half = ins[idx].shape[0] // 2
         return pltpu.make_async_copy(ins[idx].at[pl.ds(way * half, half), :], piece(idx, me, way), local_sem.at[idx, way])
 
+    def columns(idx, peer):
+        src = ins[count + idx]
+        width = src.shape[2] // 8
+        return src.at[:, :, pl.ds(pl.multiple_of(peer * width, width), width)]
+
+    def slice_out(idx, hop):
+        peer = (me + hop) % 8
+        return pltpu.make_async_remote_copy(
+            src_ref=columns(idx, peer), dst_ref=outs[count + idx].at[me], send_sem=slice_send.at[idx, hop],
+            recv_sem=slice_recv.at[idx, hop], device_id={'fsdp': peer}, device_id_type=MESH)
+
+    def slice_in(idx, hop):
+        slot = outs[count + idx].at[(me + 8 - hop) % 8]
+        return pltpu.make_async_remote_copy(
+            src_ref=slot, dst_ref=slot, send_sem=slice_send.at[idx, hop], recv_sem=slice_recv.at[idx, hop],
+            device_id={'fsdp': (me + hop) % 8}, device_id_type=MESH)
+
+    def slice_own(idx):
+        return pltpu.make_async_copy(columns(idx, me), outs[count + idx].at[me], slice_local.at[idx])
+
+    def sum_copy(idx, hop, incoming):
+        peer = (me_all + hop) % 32
+        slot = outs[count + slices + idx].at[(me_all + 32 - hop) % 32 if incoming else me_all]
+        return pltpu.make_async_remote_copy(
+            src_ref=slot if incoming else ins[count + slices + idx], dst_ref=slot, send_sem=sum_send.at[idx, hop],
+            recv_sem=sum_recv.at[idx, hop], device_id={'fsdp': peer // 4, 'model': peer % 4}, device_id_type=MESH)
+
+    def sum_own(idx):
+        return pltpu.make_async_copy(ins[count + slices + idx], outs[count + slices + idx].at[me_all], sum_local.at[idx])
+
     for step in range(7):
         for idx in range(count):
             for way in range(2):
                 if step > 0:
                     landed(idx, way, step - 1).wait_recv()
                 send(idx, way, step).start()
-                if step == 0:
+        if step == 0:
+            for idx in range(slices):
+                slice_own(idx).start()
+                for hop in range(1, 8):
+                    slice_out(idx, hop).start()
+            for idx in range(sums):
+                sum_own(idx).start()
+                for hop in range(1, 32):
+                    sum_copy(idx, hop, False).start()
+            for idx in range(count):
+                for way in range(2):
                     own(idx, way).start()
     for idx in range(count):
         for way in range(2):
@@ -95,25 +148,48 @@
             own(idx, way).wait()
             for step in range(7):
                 send(idx, way, step).wait_send()
-
-
-def ring_gather(arrays, dims, collective_id):
+    for idx in range(slices):
+        slice_own(idx).wait()
+        for hop in range(1, 8):
+            slice_in(idx, hop).wait_recv()
+            slice_out(idx, hop).wait_send()
+    for idx in range(sums):
+        sum_own(idx).wait()
+        for hop in range(1, 32):
+            sum_copy(idx, hop, True).wait_recv()
+            sum_copy(idx, hop, False).wait_send()
+
+
+def ring_gather(collective_id, arrays, dims, slices=(), sums=()):
     shapes = []
+    sent = 0
     for array, dim in zip(arrays, dims):
         shape = list(array.shape)
         shape[dim] *= 8
         shapes.append(jax.ShapeDtypeStruct(tuple(shape), array.dtype))
-    count = len(arrays)
+        sent += 7 * array.size * 2
+    for array in slices:
+        shapes.append(jax.ShapeDtypeStruct((8,) + array.shape[:2] + (array.shape[2] // 8,), array.dtype))
+    for array in sums:
+        shapes.append(jax.ShapeDtypeStruct((32,) + array.shape, array.dtype))
+    count, n_slices, n_sums = len(arrays), len(slices), len(sums)
+    dma = pltpu.SemaphoreType.DMA
     return pl.pallas_call(
-        functools.partial(ring_kernel, tuple(dims)),
+        functools.partial(ring_kernel, tuple(dims), n_slices, n_sums),
         out_shape=shapes,
-        in_specs=[pl.BlockSpec(memory_space=pl.ANY)] * count,
-        out_specs=[pl.BlockSpec(memory_space=pl.ANY)] * count,
-        scratch_shapes=[pltpu.SemaphoreType.DMA((count, 2, 7)), pltpu.SemaphoreType.DMA((count, 2, 7)),
-                        pltpu.SemaphoreType.DMA((count, 2))],
+        in_specs=[pl.BlockSpec(memory_space=pl.ANY)] * len(shapes),
+        out_specs=[pl.BlockSpec(memory_space=pl.ANY)] * len(shapes),
+        scratch_shapes=[dma((count, 2, 7)), dma((count, 2, 7)), dma((count, 2)),
+                        dma((max(n_slices, 1), 8)), dma((max(n_slices, 1), 8)), dma((max(n_slices, 1),)),
+                        dma((max(n_sums, 1), 32)), dma((max(n_sums, 1), 32)), dma((max(n_sums, 1),))],
         compiler_params=pltpu.CompilerParams(collective_id=collective_id, has_side_effects=True),
+        cost_estimate=pl.CostEstimate(flops=sent * 3000, bytes_accessed=2 * sent, transcendentals=0),
         name=f'ring_gather_{collective_id}',
-    )(*arrays)
+    )(*arrays, *slices, *sums)
+
+
+def after(values, *deps):
+    return lax.optimization_barrier((tuple(values), deps))[0]
 
 
 def solution(mesh):
@@ -145,14 +221,12 @@
         cos_k = rope_cos[:, None, :]
         sin_k = rope_sin[:, None, :]
 
-        w_qkv, w_out, w_gate, w_up, w_down = ring_gather(
-            [wqkv_sh, wout_sh, wgate_sh, wup_sh, wdown_sh], [0, 1, 0, 0, 1], 0)
-
         x_f32 = x_loc.astype(f32)
         h_attn_f, norm_back_attn = jax.vjp(rms_scale, x_f32, gain_attn)
         h_attn_loc = h_attn_f.astype(bf16)
         h_attn = gather_seq(h_attn_loc)
         dy_full = gather_seq(dy_loc)
+        w_qkv, w_out, h_attn_cols, dy_cols = ring_gather(0, [wqkv_sh, wout_sh], [0, 1], [h_attn_loc, dy_loc])
         qkv = jnp.einsum('bsd,dc->bsc', h_attn, w_qkv, preferred_element_type=f32)
         qkv = qkv.reshape(rows, seq_full, local_kv, group_size + 2, head_dim)
         query = rotate(qkv[:, :, :, :group_size], cos_q, sin_q).astype(bf16)
@@ -163,28 +237,41 @@
         prob_bf = attn_prob.astype(bf16)
         attn = jnp.einsum('bkgqt,btkd->bqkgd', prob_bf, value, preferred_element_type=f32)
         attn_flat = attn.astype(bf16).reshape(rows, seq_full, local_heads * head_dim)
-        attn_red = scatter_seq(jnp.einsum('bsh,hd->bsd', attn_flat, w_out, preferred_element_type=f32))
+        attn_part = jnp.einsum('bsh,hd->bsd', attn_flat, w_out, preferred_element_type=f32)
+        attn_red = scatter_seq(attn_part)
+        w_gate, w_up = ring_gather(1, after([wgate_sh, wup_sh], attn_part), [0, 0])
+        attn_red, = after([attn_red], w_gate)
         mid_f32 = (x_f32 + attn_red.astype(bf16).astype(f32)).astype(bf16).astype(f32)
         h_mlp_f, norm_back_mlp = jax.vjp(rms_scale, mid_f32, gain_mlp)
         h_mlp_loc = h_mlp_f.astype(bf16)
         h_mlp = gather_seq(h_mlp_loc)
+        wdown_sh, h_mlp_src = after([wdown_sh, h_mlp_loc])
+        w_down, h_mlp_cols = ring_gather(2, [wdown_sh], [1], [h_mlp_src])
+        h_mlp, = after([h_mlp], w_down)
         gate = jnp.einsum('bsd,df->bsf', h_mlp, w_gate, preferred_element_type=f32)
         up_proj = jnp.einsum('bsd,df->bsf', h_mlp, w_up, preferred_element_type=f32)
         sig_gate = jax.nn.sigmoid(gate)
         silu_gate = gate * sig_gate
         gated_act = (silu_gate * up_proj).astype(bf16)
-        mlp_red = scatter_seq(jnp.einsum('bsf,fd->bsd', gated_act, w_down, preferred_element_type=f32))
-        y_loc = (mid_f32 + mlp_red.astype(bf16).astype(f32)).astype(bf16)
+        mlp_part = jnp.einsum('bsf,fd->bsd', gated_act, w_down, preferred_element_type=f32)
 
         d_act = jnp.einsum('bsd,fd->bsf', dy_full, w_down, preferred_element_type=f32).astype(bf16).astype(f32)
         d_gate = (d_act * up_proj * sig_gate * (1.0 + gate * (1.0 - sig_gate))).astype(bf16)
         d_up = (d_act * silu_gate).astype(bf16)
-        dh_mlp = scatter_seq(jnp.einsum('bsf,df->bsd', d_gate, w_gate, preferred_element_type=f32)
-                             + jnp.einsum('bsf,df->bsd', d_up, w_up, preferred_element_type=f32))
+        dh_part = (jnp.einsum('bsf,df->bsd', d_gate, w_gate, preferred_element_type=f32)
+                   + jnp.einsum('bsf,df->bsd', d_up, w_up, preferred_element_type=f32))
+        dh_mlp = scatter_seq(dh_part)
+        mlp_red = scatter_seq(mlp_part)
+        act_all, = ring_gather(3, after([gated_act.reshape(tokens, -1)], dh_part, mlp_part), [0])
+        dh_mlp, mlp_red = after([dh_mlp, mlp_red], act_all)
+        y_loc = (mid_f32 + mlp_red.astype(bf16).astype(f32)).astype(bf16)
         d_mid_norm, d_gain_mlp = norm_back_mlp(dh_mlp.astype(bf16).astype(f32))
         d_mid = (dy_loc.astype(f32) + d_mid_norm).astype(bf16)
 
         d_mid_full = gather_seq(d_mid)
+        flat_gate, flat_attn, d_mid_src = after([d_gate.reshape(tokens, -1), attn_flat.reshape(tokens, -1), d_mid])
+        d_gate_all, attn_all, d_mid_cols = ring_gather(4, [flat_gate, flat_attn], [0, 0], [d_mid_src])
+        d_mid_full, = after([d_mid_full], d_gate_all)
         d_attn = jnp.einsum('bsd,hd->bsh', d_mid_full, w_out, preferred_element_type=f32).astype(bf16)
         d_attn = d_attn.reshape(rows, seq_full, local_kv, group_size, head_dim)
         d_prob = jnp.einsum('bqkgd,btkd->bkgqt', d_attn, value, preferred_element_type=f32)
@@ -197,30 +284,29 @@
                                  rotate_back(d_key, cos_k, sin_k)[:, :, :, None],
                                  d_value[:, :, :, None]], axis=3)
         d_qkv = d_qkv.astype(bf16).reshape(rows, seq_full, -1)
-        dh_attn = scatter_seq(jnp.einsum('bsc,dc->bsd', d_qkv, w_qkv, preferred_element_type=f32))
+        dh_attn_part = jnp.einsum('bsc,dc->bsd', d_qkv, w_qkv, preferred_element_type=f32)
+        dh_attn = scatter_seq(dh_attn_part)
+        d_up_all, = ring_gather(5, after([d_up.reshape(tokens, -1)], dh_attn_part), [0])
+        dh_attn, = after([dh_attn], d_up_all)
         d_x_norm, d_gain_attn = norm_back_attn(dh_attn.astype(bf16).astype(f32))
         dx_loc = (d_mid.astype(f32) + d_x_norm).astype(bf16)
-        gain_grads = lax.psum((d_gain_attn, d_gain_mlp), ('fsdp', 'model'))
-
-        fsdp_size = 8
-        width = x_loc.shape[2] // fsdp_size
-        pos_loc = x_loc.shape[1]
-        packed = jnp.stack([h_attn_loc, h_mlp_loc, dy_loc, d_mid], axis=0)
-        packed = packed.reshape(4, rows, pos_loc, fsdp_size, width).transpose(3, 0, 1, 2, 4)
-        packed = lax.all_to_all(packed, 'fsdp', 0, 0, tiled=True)
-        packed = lax.all_gather(packed, 'model', axis=0)
-        packed = packed.transpose(2, 1, 3, 0, 4, 5).reshape(4, fsdp_size * tokens, width)
-
-        d_qkv_all, attn_all, d_gate_all, d_up_all, act_all = ring_gather(
-            [d_qkv.reshape(tokens, -1), attn_flat.reshape(tokens, -1), d_gate.reshape(tokens, -1),
-             d_up.reshape(tokens, -1), gated_act.reshape(tokens, -1)], [0, 0, 0, 0, 0], 1)
+        gains = jnp.stack([d_gain_attn, d_gain_mlp]).reshape(16, -1)
+        flat_qkv, gains = after([d_qkv.reshape(tokens, -1), gains])
+        d_qkv_all, gains_all = ring_gather(6, [flat_qkv], [0], (), [gains])
+        gain_grads = jnp.sum(gains_all, axis=0).reshape(2, -1)
+
+        def spread(pieces):
+            pieces = lax.all_gather(pieces, 'model', axis=0)
+            return pieces.transpose(1, 2, 0, 3, 4).reshape(8 * tokens, -1)
+
+        h_attn_cols, dy_cols, h_mlp_cols, d_mid_cols = map(spread, (h_attn_cols, dy_cols, h_mlp_cols, d_mid_cols))
 
         def pair(left, right):
             return lax.dot_general(left, right, (((0,), (0,)), ((), ())), preferred_element_type=f32)
 
         return (y_loc, dx_loc, gain_grads[0], gain_grads[1],
-                pair(packed[0], d_qkv_all), pair(attn_all, packed[3]),
-                pair(packed[1], d_gate_all), pair(packed[1], d_up_all), pair(act_all, packed[2]))
+                pair(h_attn_cols, d_qkv_all), pair(attn_all, d_mid_cols),
+                pair(h_mlp_cols, d_gate_all), pair(h_mlp_cols, d_up_all), pair(act_all, dy_cols))
 
     in_specs = (act_spec, act_spec, P(), P(), rows_spec, cols_spec, rows_spec, rows_spec, cols_spec, P(), P())
     out_specs = (act_spec, act_spec, P(), P(), rows_spec, cols_spec, rows_spec, rows_spec, cols_spec)

time: 961 us -> 849 us (0.88)
  waiting for transfers between devices: 132 us -> 2.37 us
  blocking collectives: 71 us -> 0 us
  Pallas kernels: 639 us -> 706 us
  matrix products: 73.5 us -> 84.5 us
    reduce_scatter x4, waiting for transfers between devices: 87.3 us -> 0.06 us  [scatter_seq(): return lax.psum_scatter(tensor, 'model', scatter_dimension=1, tiled=True)]
    pallas_call x2 -> x7, Pallas kernels: 639 us -> 706 us  [ring_gather(): pl.pallas_call(functools.partial(ring_kernel, tuple(dims), n_slices, n_su...]
    all_gather x4, waiting for transfers between devices: 44 us -> 0.06 us  [gather_seq(): return lax.all_gather(tensor, 'model', axis=1, tiled=True)]
    psum x1 -> x0, blocking collectives: 39.4 us -> none  [device_fn(): gain_grads = lax.psum((d_gain_attn, d_gain_mlp), ('fsdp', 'model'))]
    all_to_all x1 -> x0, blocking collectives: 31.5 us -> none  [device_fn(): packed = lax.all_to_all(packed, 'fsdp', 0, 0, tiled=True)]
    dot_general x5, matrix products: 19.2 us -> 29.2 us  [pair(): lax.dot_general(left, right, (((0,), (0,)), ((), ())), preferred_element_...]
  transfers between devices with their start and end apart: 9 -> 12, of which waited for: 6 -> 0; matrix products, arithmetic and copies ran while one was open for 3% -> 9% of each run, Pallas kernels for 67% -> 74%
where the time goes in v2:
time: 849 us; the launch traced here: 843 us
  Pallas kernels  706 us (83%)
  matrix products  84.5 us (10%)
  local copies, waits for them, and re-layouts  20.2 us (2%)
  between operations  15.2 us (2%)
  other arithmetic  13.1 us (2%)
    pallas_call x7, Pallas kernels, ring_gather(): pl.pallas_call(functools.partial(ring_kernel, tuple(dims), n_slices, n_su...  706 us
    dot_general x5, matrix products, pair(): lax.dot_general(left, right, (((0,), (0,)), ((), ())), preferred_element_...  29.2 us
  transfers between devices with their start and end apart: 12, of which 0 were waited for; matrix products, arithmetic and copies ran while one was open for 9% of the time, Pallas kernels for 74%

profile of v2, /device:TPU:0, one launch (start us, length us, event | category | flops | bytes accessed | tf_op | source)
XLA Modules:
  0.0 843.0 jit_solution(16882045697288759239)
XLA Ops:
  9.4 1.8 fusion.43.refs_2_
  13.0 96.7 %ring_gather_0.1 = (bf16[2048,1536]{1,0:T(8,128)(2,1)}, bf16[512,2048]{1,0:T(8,128)(2,1)}, bf16[8,2,32,256]{3,2,1,0:T(8,128)(2,1)}, bf16[8,2,32,256]{3,2,1,0:T(8,128)(2,1)}) custom-call(bf16[256,1536]{1,0:T(8,128)(2,1)} %refs_0_.1, bf16[512,256]{1,0:T(8,128)(2,1)} %refs_1_.1, bf16[2,32,2048]{2,1,0:T(8,128)(2,1)} %fusion.43.refs_2_, bf16[2,32,2048]{2,1,0:T(8,128)(2,1)} %refs_3_.1), custom_call_target="tpu_custom_call" | custom-call | flops 22020096000 | bytes 14680064 | tf_op jit(solution)/shard_map/ring_gather_0/pallas_call | solution.py:177
  109.7 4.9 fusion.14
  118.1 1.3 convolution_convert_fusion
  119.5 2.0 fusion.30
  122.4 162.6 %ring_gather_1.1 = (bf16[2048,2048]{1,0:T(8,128)(2,1)}, bf16[2048,2048]{1,0:T(8,128)(2,1)}) custom-call(bf16[256,2048]{1,0:T(8,128)(2,1)} %refs_0_.2, bf16[256,2048]{1,0:T(8,128)(2,1)} %refs_1_.2), custom_call_target="tpu_custom_call" | custom-call | flops 44040192000 | bytes 29360128 | tf_op jit(solution)/shard_map/ring_gather_1/pallas_call | solution.py:177
  287.5 88.3 %ring_gather_2.1 = (bf16[2048,2048]{1,0:T(8,128)(2,1)}, bf16[8,2,32,256]{3,2,1,0:T(8,128)(2,1)}) custom-call(bf16[2048,256]{1,0:T(8,128)(2,1)} %refs_0_.3, bf16[2,32,2048]{2,1,0:T(8,128)(2,1)} %fusion.42.refs_1_), custom_call_target="tpu_custom_call" | custom-call | flops 22020096000 | bytes 14680064 | tf_op jit(solution)/shard_map/ring_gather_2/pallas_call | solution.py:177
  375.8 7.3 fusion.25
  383.1 6.2 fusion.2
  389.5 4.9 multiply_convert_fusion
  395.4 3.7 fusion.8
  399.7 5.7 fusion
  405.5 7.4 fusion.16
  414.5 86.1 %ring_gather_3.1 = bf16[2048,2048]{1,0:T(8,128)(2,1)} custom-call(bf16[256,2048]{1,0:T(8,128)(2,1)} %bitcast.180), custom_call_target="tpu_custom_call" | custom-call | flops 22020096000 | bytes 14680064 | tf_op jit(solution)/shard_map/ring_gather_3/pallas_call | solution.py:177
  500.7 1.2 fusion.44
  501.9 2.2 fusion.47
  505.2 1.3 copy.128
  506.5 1.3 copy.131
  507.9 103.6 %ring_gather_4.1 = (bf16[2048,2048]{1,0:T(8,128)(2,1)}, bf16[2048,512]{1,0:T(8,128)(2,1)}, bf16[8,2,32,256]{3,2,1,0:T(8,128)(2,1)}) custom-call(bf16[256,2048]{1,0:T(8,128)(2,1)} %bitcast.179, bf16[256,512]{1,0:T(8,128)(2,1)} %bitcast.171, bf16[2,32,2048]{2,1,0:T(8,128)(2,1)} %get-tuple-element.55.refs_2_), custom_call_target="tpu_custom_call" | custom-call | flops 27525120000 | bytes 18350080 | tf_op jit(solution)/shard_map/ring_gather_4/pallas_call | solution.py:177
  611.8 2.7 fusion.34
  614.8 1.4 multiply_reduce_fusion
  619.7 6.3 fusion.12
  626.0 7.2 fusion.82
  633.2 1.3 copy.130
  634.5 7.7 fusion.80
  642.2 2.0 copy.126
  644.2 1.5 copy.129
  646.4 1.5 fusion.79
  647.9 90.0 %ring_gather_5.1 = bf16[2048,2048]{1,0:T(8,128)(2,1)} custom-call(bf16[256,2048]{1,0:T(8,128)(2,1)} %bitcast.178), custom_call_target="tpu_custom_call" | custom-call | flops 22020096000 | bytes 14680064 | tf_op jit(solution)/shard_map/ring_gather_5/pallas_call | solution.py:177
  737.9 7.1 fusion.81
  748.0 79.0 %ring_gather_6.1 = (bf16[2048,1536]{1,0:T(8,128)(2,1)}, f32[32,16,256]{2,1,0:T(8,128)}) custom-call(bf16[256,1536]{1,0:T(8,128)(2,1)} %copy.127.refs_0_, f32[16,256]{1,0:T(8,128)} %reshape.171.refs_1_), custom_call_target="tpu_custom_call" | custom-call | flops 16515072000 | bytes 11010048 | tf_op jit(solution)/shard_map/ring_gather_6/pallas_call | solution.py:177
  830.2 5.7 fusion.78
  (158 shorter events, 25.9 us)
Async XLA Ops:
  7.2 102.5 %all-gather.13.cloned.1.call-start = ((), (), s32[]{:S(2)}) async-start(), calls=%async_computation.4 | async-start | bytes 1310720 | tf_op jit(solution)/shard_map/all_gather | solution.py:203
  11.2 273.8 %reduce-scatter.5.cloned.1.call-start = ((), (), s32[]{:S(2)}) async-start(), calls=%async_computation.5 | async-start | bytes 2621440 | tf_op jit(solution)/shard_map/reduce_scatter | solution.py:206
  12.1 104.5 %copy-start.17 = (f32[128,64]{1,0:T(8,128)}, f32[128,64]{1,0:T(8,128)S(1)}, u32[]{:S(2)}) copy-start(f32[128,64]{1,0:T(8,128)S(1)} %copy.104) | copy-start | bytes 98308
  13.0 103.7 %copy-start.19 = (f32[128,64]{1,0:T(8,128)}, f32[128,64]{1,0:T(8,128)S(1)}, u32[]{:S(2)}) copy-start(f32[128,64]{1,0:T(8,128)S(1)} %copy.105) | copy-start | bytes 98308
  121.6 254.2 %all-gather.15.cloned.1.call-start = ((), (), s32[]{:S(2)}) async-start(), calls=%async_computation.6 | async-start | bytes 1310720 | tf_op jit(solution)/shard_map/all_gather | solution.py:203
  122.3 162.7 %copy-start = (bf16[2,32,2048]{2,1,0:T(8,128)(2,1)S(1)}, bf16[2,32,2048]{2,1,0:T(8,128)(2,1)}, u32[]{:S(2)}) copy-start(bf16[2,32,2048]{2,1,0:T(8,128)(2,1)} %param.11) | copy-start | bytes 786436
  122.3 163.9 %copy-start.23 = (f32[2048]{0:T(1024)S(1)}, f32[2048]{0:T(1024)}, u32[]{:S(2)}) copy-start(f32[2048]{0:T(1024)} %param.14) | copy-start | bytes 24580
  122.3 260.7 %all-gather.17.cloned.1.call-start = ((), (), s32[]{:S(2)}) async-start(), calls=%async_computation.7 | async-start | bytes 1310720 | tf_op jit(solution)/shard_map/all_gather | solution.py:203
  287.1 213.5 %reduce-scatter.9.cloned.1.call-start = ((), (), s32[]{:S(2)}) async-start(), calls=%async_computation.9 | async-start | bytes 2621440 | tf_op jit(solution)/shard_map/reduce_scatter | solution.py:206
  383.1 6.2 copy-start.33
  383.1 6.4 copy-start.37
  383.1 12.3 %slice-start = ((s8[8388608]{0:T(1024)(128)(4,1)}), s8[4194304]{0:T(1024)(128)(4,1)S(1)}, s32[]{:S(2)}) async-start(s8[8388608]{0:T(1024)(128)(4,1)} %bitcast.181), calls=%async_computation.16 | async-start | bytes 8388608
  389.5 5.9 slice-start.1
  394.4 5.3 copy-start.35
  394.5 11.0 %copy-start.34 = (bf16[2,128,2048]{2,1,0:T(8,128)(2,1)}, bf16[2,128,2048]{2,1,0:T(8,128)(2,1)S(1)}, u32[]{:S(2)}) copy-start(bf16[2,128,2048]{2,1,0:T(8,128)(2,1)S(1)} %get-tuple-element.77) | copy-start | bytes 3145732
  399.2 101.5 %reduce-scatter.7.cloned.1.call-start = ((), (), s32[]{:S(2)}) async-start(), calls=%async_computation.8 | async-start | bytes 2621440 | tf_op jit(solution)/shard_map/reduce_scatter | solution.py:206
  413.0 92.2 %all-gather.21.cloned.1.call-start = ((), (), s32[]{:S(2)}) async-start(), calls=%async_computation.12 | async-start | bytes 1310720 | tf_op jit(solution)/shard_map/all_gather | solution.py:299
  413.7 92.8 %all-gather.27.cloned.1.call-start = ((), (), s32[]{:S(2)}) async-start(), calls=%async_computation.15 | async-start | bytes 1310720 | tf_op jit(solution)/shard_map/all_gather | solution.py:299
  414.5 197.3 %all-gather.19.cloned.1.call-start = ((), (), s32[]{:S(2)}) async-start(), calls=%async_computation.10 | async-start | bytes 1310720 | tf_op jit(solution)/shard_map/all_gather | solution.py:203
  414.5 87.4 %copy-start.21 = (bf16[2,32,2048]{2,1,0:T(8,128)(2,1)S(1)}, bf16[2,32,2048]{2,1,0:T(8,128)(2,1)}, u32[]{:S(2)}) copy-start(bf16[2,32,2048]{2,1,0:T(8,128)(2,1)} %refs_3_.1) | copy-start | bytes 786436
  504.2 129.0 %all-gather.25.cloned.1.call-start = ((), (), s32[]{:S(2)}) async-start(), calls=%async_computation.14 | async-start | bytes 1310720 | tf_op jit(solution)/shard_map/all_gather | solution.py:299
  507.9 136.3 %all-gather.23.cloned.1.call-start = ((), (), s32[]{:S(2)}) async-start(), calls=%async_computation.13 | async-start | bytes 1310720 | tf_op jit(solution)/shard_map/all_gather | solution.py:299
  611.5 133.5 %reduce-scatter.11.cloned.1.call-start = ((), (), s32[]{:S(2)}) async-start(), calls=%async_computation.11 | async-start | bytes 2621440 | tf_op jit(solution)/shard_map/reduce_scatter | solution.py:206
  611.8 2.9 copy-start.3
  611.8 2.9 copy-start.26
  611.8 2.9 copy-start.28
  737.9 7.1 copy-start.1
  737.9 7.1 copy-start.24
  737.9 7.1 copy-start.30
  748.0 81.3 %copy-start.32 = (f32[2,32]{1,0:T(2,128)S(1)}, f32[2,32]{1,0:T(2,128)}, u32[]{:S(2)}) copy-start(f32[2,32]{1,0:T(2,128)} %copy-done.31) | copy-start | bytes 772
  748.0 81.3 %copy-start.5 = (bf16[2,32,2048]{2,1,0:T(8,128)(2,1)S(1)}, bf16[2,32,2048]{2,1,0:T(8,128)(2,1)}, u32[]{:S(2)}) copy-start(bf16[2,32,2048]{2,1,0:T(8,128)(2,1)} %get-tuple-element.55.refs_2_) | copy-start | bytes 786436
  748.0 81.3 %copy-start.15 = (f32[2,32,2048]{2,1,0:T(8,128)S(1)}, f32[2,32,2048]{2,1,0:T(8,128)}, u32[]{:S(2)}) copy-start(f32[2,32,2048]{2,1,0:T(8,128)} %reduce-scatter.11.cloned.1.call-done) | copy-start | bytes 1572868
  (20 other events, 33.7 us)
Sparse Core Ops, SparseCore 0:
  11.3 19.4 all-gather.12
  121.7 31.3 reduce-scatter.4
  154.7 16.6 all-gather.14
  287.2 15.7 all-gather.16
  399.3 30.2 reduce-scatter.8
  432.5 31.1 reduce-scatter.6
  465.3 16.6 all-gather.20
  483.6 16.6 all-gather.26
  504.3 15.1 all-gather.18
  520.9 16.6 all-gather.24
  611.7 15.3 all-gather.22
  629.4 31.1 reduce-scatter.10

commit v3 on v2

--- a/solution.py
+++ b/solution.py
@@ -40,48 +40,48 @@
     return 2 * (place + y * (7 - 2 * place)) + y
 
 
-def ring_kernel(dims, slices, sums, *refs):
+def ring_kernel(dims, spans, slices, sums, *refs):
     count = len(dims)
     total = count + slices + sums
     ins, outs = refs[:total], refs[total:2 * total]
-    send_sem, recv_sem, local_sem, slice_send, slice_recv, slice_local, sum_send, sum_recv, sum_local = refs[2 * total:]
+    mix = refs[2 * total] if sums else None
+    send_sem, recv_sem, local_sem, slice_send, slice_recv, slice_local, mix_send, mix_recv, mix_local = refs[-9:]
     me = lax.axis_index('fsdp')
     me_model = lax.axis_index('model')
-    me_all = 4 * me + me_model
     place = ring_place(me)
     targets = (ring_device((place + 1) % 8), ring_device((place + 7) % 8))
 
     barrier = pltpu.get_barrier_semaphore()
+    peers = [(me + hop) % 8 for hop in range(1, 8)] if slices else targets
+    for peer in peers:
+        pl.semaphore_signal(barrier, inc=1, device_id={'fsdp': peer}, device_id_type=MESH)
     if sums:
-        for hop in range(1, 32):
-            peer = (me_all + hop) % 32
-            pl.semaphore_signal(barrier, inc=1, device_id={'fsdp': peer // 4, 'model': peer % 4}, device_id_type=MESH)
-        pl.semaphore_wait(barrier, 31)
-    elif slices:
-        for hop in range(1, 8):
-            pl.semaphore_signal(barrier, inc=1, device_id={'fsdp': (me + hop) % 8}, device_id_type=MESH)
-        pl.semaphore_wait(barrier, 7)
-    else:
-        for target in targets:
-            pl.semaphore_signal(barrier, inc=1, device_id={'fsdp': target}, device_id_type=MESH)
-        pl.semaphore_wait(barrier, 2)
+        for hop in range(1, 4):
+            pl.semaphore_signal(barrier, inc=1, device_id={'model': (me_model + hop) % 4}, device_id_type=MESH)
+    pl.semaphore_wait(barrier, len(peers) + 3 * sums)
 
     def piece(idx, owner, way):
-        rows, cols = ins[idx].shape
-        half = rows // 2
+        if idx == count:
+            return outs[count + slices].at[owner, pl.ds(2 * way, 2)]
+        half = spans[idx][1] // 2
+        cols = ins[idx].shape[1]
         if dims[idx] == 0:
-            start = pl.multiple_of(owner * rows + way * half, half)
+            start = pl.multiple_of(owner * (2 * half) + way * half, half)
             return outs[idx].at[pl.ds(start, half), :]
         return outs[idx].at[pl.ds(way * half, half), pl.ds(pl.multiple_of(owner * cols, cols), cols)]
+
+    def source(idx, way):
+        if idx == count:
+            return mix.at[pl.ds(2 * way, 2)]
+        start, length = spans[idx]
+        return ins[idx].at[pl.ds(start + way * (length // 2), length // 2), :]
 
     def send(idx, way, step):
         owner = ring_device((place + (8 - step if way == 0 else step)) % 8)
         dst = piece(idx, owner, way)
-        half = ins[idx].shape[0] // 2
-        src = ins[idx].at[pl.ds(way * half, half), :] if step == 0 else dst
-        return pltpu.make_async_remote_copy(
-            src_ref=src, dst_ref=dst, send_sem=send_sem.at[idx, way, step], recv_sem=recv_sem.at[idx, way, step],
-            device_id={'fsdp': targets[way]}, device_id_type=MESH)
+        return pltpu.make_async_remote_copy(
+            src_ref=source(idx, way) if step == 0 else dst, dst_ref=dst, send_sem=send_sem.at[idx, way, step],
+            recv_sem=recv_sem.at[idx, way, step], device_id={'fsdp': targets[way]}, device_id_type=MESH)
 
     def landed(idx, way, step):
         owner = ring_device((place + (7 - step if way == 0 else step + 1)) % 8)
@@ -91,8 +91,7 @@
             device_id={'fsdp': targets[way]}, device_id_type=MESH)
 
     def own(idx, way):
-        half = ins[idx].shape[0] // 2
-        return pltpu.make_async_copy(ins[idx].at[pl.ds(way * half, half), :], piece(idx, me, way), local_sem.at[idx, way])
+        return pltpu.make_async_copy(source(idx, way), piece(idx, me, way), local_sem.at[idx, way])
 
     def columns(idx, peer):
         src = ins[count + idx]
@@ -114,35 +113,39 @@
     def slice_own(idx):
         return pltpu.make_async_copy(columns(idx, me), outs[count + idx].at[me], slice_local.at[idx])
 
-    def sum_copy(idx, hop, incoming):
-        peer = (me_all + hop) % 32
-        slot = outs[count + slices + idx].at[(me_all + 32 - hop) % 32 if incoming else me_all]
-        return pltpu.make_async_remote_copy(
-            src_ref=slot if incoming else ins[count + slices + idx], dst_ref=slot, send_sem=sum_send.at[idx, hop],
-            recv_sem=sum_recv.at[idx, hop], device_id={'fsdp': peer // 4, 'model': peer % 4}, device_id_type=MESH)
-
-    def sum_own(idx):
-        return pltpu.make_async_copy(ins[count + slices + idx], outs[count + slices + idx].at[me_all], sum_local.at[idx])
-
+    def mix_copy(hop, incoming):
+        slot = mix.at[(me_model + 4 - hop) % 4 if incoming else me_model]
+        return pltpu.make_async_remote_copy(
+            src_ref=slot if incoming else ins[count + slices], dst_ref=slot, send_sem=mix_send.at[hop],
+            recv_sem=mix_recv.at[hop], device_id={'model': (me_model + hop) % 4}, device_id_type=MESH)
+
+    def mix_own():
+        return pltpu.make_async_copy(ins[count + slices], mix.at[me_model], mix_local)
+
+    if sums:
+        mix_own().start()
+        for hop in range(1, 4):
+            mix_copy(hop, False).start()
     for step in range(7):
-        for idx in range(count):
+        for idx in range(count + sums):
             for way in range(2):
                 if step > 0:
                     landed(idx, way, step - 1).wait_recv()
+                elif idx == count and way == 0:
+                    mix_own().wait()
+                    for hop in range(1, 4):
+                        mix_copy(hop, True).wait_recv()
+                        mix_copy(hop, False).wait_send()
                 send(idx, way, step).start()
         if step == 0:
             for idx in range(slices):
                 slice_own(idx).start()
                 for hop in range(1, 8):
                     slice_out(idx, hop).start()
-            for idx in range(sums):
-                sum_own(idx).start()
-                for hop in range(1, 32):
-                    sum_copy(idx, hop, False).start()
-            for idx in range(count):
+            for idx in range(count + sums):
                 for way in range(2):
                     own(idx, way).start()
-    for idx in range(count):
+    for idx in range(count + sums):
         for way in range(2):
             landed(idx, way, 6).wait_recv()
             own(idx, way).wait()
@@ -153,39 +156,178 @@
         for hop in range(1, 8):
             slice_in(idx, hop).wait_recv()
             slice_out(idx, hop).wait_send()
-    for idx in range(sums):
-        sum_own(idx).wait()
-        for hop in range(1, 32):
-            sum_copy(idx, hop, True).wait_recv()
-            sum_copy(idx, hop, False).wait_send()
-
-
-def ring_gather(collective_id, arrays, dims, slices=(), sums=()):
+
+
+def ring_gather(collective_id, arrays, dims, slices=(), sums=(), spans=None):
     shapes = []
     sent = 0
-    for array, dim in zip(arrays, dims):
-        shape = list(array.shape)
-        shape[dim] *= 8
-        shapes.append(jax.ShapeDtypeStruct(tuple(shape), array.dtype))
-        sent += 7 * array.size * 2
+    spans = spans or [(0, array.shape[0]) for array in arrays]
+    for array, dim, span in zip(arrays, dims, spans):
+        rows, cols = span[1], array.shape[1]
+        shapes.append(jax.ShapeDtypeStruct((8 * rows, cols) if dim == 0 else (rows, 8 * cols), array.dtype))
+        sent += 7 * rows * cols * 2
     for array in slices:
         shapes.append(jax.ShapeDtypeStruct((8,) + array.shape[:2] + (array.shape[2] // 8,), array.dtype))
     for array in sums:
-        shapes.append(jax.ShapeDtypeStruct((32,) + array.shape, array.dtype))
+        shapes.append(jax.ShapeDtypeStruct((8, 4) + array.shape, array.dtype))
+    n_in = len(shapes)
+    for array in sums:
+        shapes.append(jax.ShapeDtypeStruct((4,) + array.shape, array.dtype))
     count, n_slices, n_sums = len(arrays), len(slices), len(sums)
     dma = pltpu.SemaphoreType.DMA
     return pl.pallas_call(
-        functools.partial(ring_kernel, tuple(dims), n_slices, n_sums),
+        functools.partial(ring_kernel, tuple(dims), tuple(spans), n_slices, n_sums),
         out_shape=shapes,
-        in_specs=[pl.BlockSpec(memory_space=pl.ANY)] * len(shapes),
+        in_specs=[pl.BlockSpec(memory_space=pl.ANY)] * n_in,
         out_specs=[pl.BlockSpec(memory_space=pl.ANY)] * len(shapes),
-        scratch_shapes=[dma((count, 2, 7)), dma((count, 2, 7)), dma((count, 2)),
+        scratch_shapes=[dma((count + n_sums, 2, 7)), dma((count + n_sums, 2, 7)), dma((count + n_sums, 2)),
                         dma((max(n_slices, 1), 8)), dma((max(n_slices, 1), 8)), dma((max(n_slices, 1),)),
-                        dma((max(n_sums, 1), 32)), dma((max(n_sums, 1), 32)), dma((max(n_sums, 1),))],
+                        dma((4,)), dma((4,)), dma],
         compiler_params=pltpu.CompilerParams(collective_id=collective_id, has_side_effects=True),
         cost_estimate=pl.CostEstimate(flops=sent * 3000, bytes_accessed=2 * sent, transcendentals=0),
         name=f'ring_gather_{collective_id}',
     )(*arrays, *slices, *sums)
+
+
+TILE = 512
+
+
+def mlp_kernel(gate_sh, up_sh, down_a, down_b, h_ref, dy_ref, act_ref, d_gate_ref, d_up_ref, y_part_ref, dh_part_ref,
+               w_gate, w_up, w_down, gate_acc, up_acc, d_act, send_sem, recv_sem, local_sem, down_sem):
+    f32, bf16 = jnp.float32, jnp.bfloat16
+    me = lax.axis_index('fsdp')
+    place = ring_place(me)
+    targets = (ring_device((place + 1) % 8), ring_device((place + 7) % 8))
+    barrier = pltpu.get_barrier_semaphore()
+    for target in targets:
+        pl.semaphore_signal(barrier, inc=1, device_id={'fsdp': target}, device_id_type=MESH)
+    pl.semaphore_wait(barrier, 2)
+    shards, weights, accs = (gate_sh, up_sh), (w_gate, w_up), (gate_acc, up_acc)
+    rows, width = gate_sh.shape
+    half = rows // 2
+
+    def start_of(owner, way):
+        return pl.multiple_of(owner * rows + way * half, half)
+
+    def send(idx, way, step):
+        owner = ring_device((place + (8 - step if way == 0 else step)) % 8)
+        dst = weights[idx].at[pl.ds(start_of(owner, way), half), :]
+        src = shards[idx].at[pl.ds(way * half, half), :] if isinstance(step, int) and step == 0 else dst
+        return pltpu.make_async_remote_copy(
+            src_ref=src, dst_ref=dst, send_sem=send_sem.at[idx, way, step], recv_sem=recv_sem.at[idx, way, step],
+            device_id={'fsdp': targets[way]}, device_id_type=MESH)
+
+    def landed(idx, way, step):
+        owner = ring_device((place + (7 - step if way == 0 else step + 1)) % 8)
+        dst = weights[idx].at[pl.ds(start_of(owner, way), half), :]
+        return pltpu.make_async_remote_copy(
+            src_ref=dst, dst_ref=dst, send_sem=send_sem.at[idx, way, step], recv_sem=recv_sem.at[idx, way, step],
+            device_id={'fsdp': targets[way]}, device_id_type=MESH)
+
+    def own(idx, way):
+        return pltpu.make_async_copy(shards[idx].at[pl.ds(way * half, half), :],
+                                     weights[idx].at[pl.ds(start_of(me, way), half), :], local_sem.at[idx, way])
+
+    def fetch_down(part):
+        src = (down_a, down_b)[part]
+        return pltpu.make_async_copy(src, w_down.at[pl.ds(part * src.shape[0], src.shape[0]), :], down_sem.at[part])
+
+    def accumulate(step):
+        for way in range(2):
+            start = start_of(ring_device((place + (8 - step if way == 0 else step)) % 8), way)
+            h_block = h_ref[:, pl.ds(start, half)]
+            for idx in range(2):
+                @pl.loop(0, width // TILE)
+                def _(tile):
+                    cols = pl.ds(pl.multiple_of(tile * TILE, TILE), TILE)
+                    accs[idx][:, cols] += jnp.dot(h_block, weights[idx][pl.ds(start, half), cols],
+                                                  preferred_element_type=f32)
+
+    def across(left, right):
+        return lax.dot_general(left, right, (((1,), (1,)), ((), ())), preferred_element_type=f32)
+
+    for idx in range(2):
+        for way in range(2):
+            send(idx, way, 0).start()
+    for part in range(2):
+        fetch_down(part).start()
+    for idx in range(2):
+        for way in range(2):
+            own(idx, way).start()
+    for acc in accs:
+        acc[...] = jnp.zeros_like(acc)
+    for part in range(2):
+        fetch_down(part).wait()
+
+    @pl.loop(0, width // TILE)
+    def _(tile):
+        cols = pl.ds(pl.multiple_of(tile * TILE, TILE), TILE)
+        d_act[:, cols] = across(dy_ref[...], w_down[cols, :]).astype(bf16)
+
+    for idx in range(2):
+        for way in range(2):
+            own(idx, way).wait()
+    accumulate(0)
+
+    @pl.loop(1, 7)
+    def _(step):
+        for idx in range(2):
+            for way in range(2):
+                landed(idx, way, step - 1).wait_recv()
+                send(idx, way, step).start()
+        accumulate(step)
+
+    for idx in range(2):
+        for way in range(2):
+            landed(idx, way, 6).wait_recv()
+    accumulate(7)
+
+    @pl.loop(0, width // 256)
+    def _(tile):
+        cols = pl.ds(pl.multiple_of(tile * 256, 256), 256)
+        gate, up_proj = gate_acc[:, cols], up_acc[:, cols]
+        d_val = d_act[:, cols].astype(f32)
+        sig_gate = jax.nn.sigmoid(gate)
+        silu_gate = gate * sig_gate
+        act_ref[:, cols] = (silu_gate * up_proj).astype(bf16)
+        d_gate_ref[:, cols] = (d_val * up_proj * sig_gate * (1.0 + gate * (1.0 - sig_gate))).astype(bf16)
+        d_up_ref[:, cols] = (d_val * silu_gate).astype(bf16)
+
+    @pl.loop(0, width // TILE)
+    def _(tile):
+        cols = pl.ds(pl.multiple_of(tile * TILE, TILE), TILE)
+        dh_part_ref[:, cols] = across(d_gate_ref[...], w_gate[cols, :]) + across(d_up_ref[...], w_up[cols, :])
+        y_part_ref[:, cols] = jnp.dot(act_ref[...], w_down[:, cols], preferred_element_type=f32)
+
+    for idx in range(2):
+        for way in range(2):
+            for step in range(7):
+                send(idx, way, step).wait_send()
+
+
+def ring_mlp(collective_id, gate_sh, up_sh, down_a, down_b, h_full, dy_full):
+    tokens, d_model = h_full.shape
+    width = gate_sh.shape[1]
+    sent = 14 * gate_sh.size * 2
+    dma = pltpu.SemaphoreType.DMA
+    vmem = pl.BlockSpec(memory_space=pltpu.VMEM)
+    hbm = pl.BlockSpec(memory_space=pl.ANY)
+    hidden = jax.ShapeDtypeStruct((tokens, width), jnp.bfloat16)
+    partial_sum = jax.ShapeDtypeStruct((tokens, d_model), jnp.float32)
+    return pl.pallas_call(
+        mlp_kernel,
+        out_shape=[hidden, hidden, hidden, partial_sum, partial_sum],
+        in_specs=[hbm, hbm, hbm, hbm, vmem, vmem],
+        out_specs=[vmem] * 5,
+        scratch_shapes=[pltpu.VMEM((d_model, width), jnp.bfloat16), pltpu.VMEM((d_model, width), jnp.bfloat16),
+                        pltpu.VMEM((width, d_model), jnp.bfloat16), pltpu.VMEM((tokens, width), jnp.float32),
+                        pltpu.VMEM((tokens, width), jnp.float32), pltpu.VMEM((tokens, width), jnp.bfloat16),
+                        dma((2, 2, 7)), dma((2, 2, 7)), dma((2, 2)), dma((2,))],
+        compiler_params=pltpu.CompilerParams(collective_id=collective_id, has_side_effects=True,
+                                             vmem_limit_bytes=60 * 1024 * 1024),
+        cost_estimate=pl.CostEstimate(flops=sent * 3000, bytes_accessed=2 * sent, transcendentals=0),
+        name=f'ring_mlp_{collective_id}',
+    )(gate_sh, up_sh, down_a, down_b, h_full, dy_full)
 
 
 def after(values, *deps):
@@ -239,37 +381,30 @@
         attn_flat = attn.astype(bf16).reshape(rows, seq_full, local_heads * head_dim)
         attn_part = jnp.einsum('bsh,hd->bsd', attn_flat, w_out, preferred_element_type=f32)
         attn_red = scatter_seq(attn_part)
-        w_gate, w_up = ring_gather(1, after([wgate_sh, wup_sh], attn_part), [0, 0])
-        attn_red, = after([attn_red], w_gate)
+        half_down = wdown_sh.shape[0] // 2
+        down_a, = ring_gather(1, after([wdown_sh], attn_part), [1], spans=[(0, half_down)])
+        attn_red, = after([attn_red], down_a)
         mid_f32 = (x_f32 + attn_red.astype(bf16).astype(f32)).astype(bf16).astype(f32)
         h_mlp_f, norm_back_mlp = jax.vjp(rms_scale, mid_f32, gain_mlp)
         h_mlp_loc = h_mlp_f.astype(bf16)
         h_mlp = gather_seq(h_mlp_loc)
         wdown_sh, h_mlp_src = after([wdown_sh, h_mlp_loc])
-        w_down, h_mlp_cols = ring_gather(2, [wdown_sh], [1], [h_mlp_src])
-        h_mlp, = after([h_mlp], w_down)
-        gate = jnp.einsum('bsd,df->bsf', h_mlp, w_gate, preferred_element_type=f32)
-        up_proj = jnp.einsum('bsd,df->bsf', h_mlp, w_up, preferred_element_type=f32)
-        sig_gate = jax.nn.sigmoid(gate)
-        silu_gate = gate * sig_gate
-        gated_act = (silu_gate * up_proj).astype(bf16)
-        mlp_part = jnp.einsum('bsf,fd->bsd', gated_act, w_down, preferred_element_type=f32)
-
-        d_act = jnp.einsum('bsd,fd->bsf', dy_full, w_down, preferred_element_type=f32).astype(bf16).astype(f32)
-        d_gate = (d_act * up_proj * sig_gate * (1.0 + gate * (1.0 - sig_gate))).astype(bf16)
-        d_up = (d_act * silu_gate).astype(bf16)
-        dh_part = (jnp.einsum('bsf,df->bsd', d_gate, w_gate, preferred_element_type=f32)
-                   + jnp.einsum('bsf,df->bsd', d_up, w_up, preferred_element_type=f32))
+        down_b, h_mlp_cols = ring_gather(2, [wdown_sh], [1], [h_mlp_src], spans=[(half_down, half_down)])
+        h_mlp, = after([h_mlp], down_b)
+        gated_act, d_gate, d_up, mlp_part, dh_part = ring_mlp(
+            7, wgate_sh, wup_sh, down_a, down_b, h_mlp.reshape(tokens, -1), dy_full.reshape(tokens, -1))
+        mlp_part = mlp_part.reshape(rows, seq_full, -1)
+        dh_part = dh_part.reshape(rows, seq_full, -1)
         dh_mlp = scatter_seq(dh_part)
         mlp_red = scatter_seq(mlp_part)
-        act_all, = ring_gather(3, after([gated_act.reshape(tokens, -1)], dh_part, mlp_part), [0])
+        act_all, = ring_gather(3, [gated_act], [0])
         dh_mlp, mlp_red = after([dh_mlp, mlp_red], act_all)
         y_loc = (mid_f32 + mlp_red.astype(bf16).astype(f32)).astype(bf16)
         d_mid_norm, d_gain_mlp = norm_back_mlp(dh_mlp.astype(bf16).astype(f32))
         d_mid = (dy_loc.astype(f32) + d_mid_norm).astype(bf16)
 
         d_mid_full = gather_seq(d_mid)
-        flat_gate, flat_attn, d_mid_src = after([d_gate.reshape(tokens, -1), attn_flat.reshape(tokens, -1), d_mid])
+        flat_gate, flat_attn, d_mid_src = after([d_gate, attn_flat.reshape(tokens, -1), d_mid])
         d_gate_all, attn_all, d_mid_cols = ring_gather(4, [flat_gate, flat_attn], [0, 0], [d_mid_src])
         d_mid_full, = after([d_mid_full], d_gate_all)
         d_attn = jnp.einsum('bsd,hd->bsh', d_mid_full, w_out, preferred_element_type=f32).astype(bf16)
@@ -286,14 +421,14 @@
         d_qkv = d_qkv.astype(bf16).reshape(rows, seq_full, -1)
         dh_attn_part = jnp.einsum('bsc,dc->bsd', d_qkv, w_qkv, preferred_element_type=f32)
         dh_attn = scatter_seq(dh_attn_part)
-        d_up_all, = ring_gather(5, after([d_up.reshape(tokens, -1)], dh_attn_part), [0])
+        d_up_all, = ring_gather(5, after([d_up], dh_attn_part), [0])
         dh_attn, = after([dh_attn], d_up_all)
         d_x_norm, d_gain_attn = norm_back_attn(dh_attn.astype(bf16).astype(f32))
         dx_loc = (d_mid.astype(f32) + d_x_norm).astype(bf16)
         gains = jnp.stack([d_gain_attn, d_gain_mlp]).reshape(16, -1)
         flat_qkv, gains = after([d_qkv.reshape(tokens, -1), gains])
-        d_qkv_all, gains_all = ring_gather(6, [flat_qkv], [0], (), [gains])
-        gain_grads = jnp.sum(gains_all, axis=0).reshape(2, -1)
+        d_qkv_all, gains_all, _ = ring_gather(6, [flat_qkv], [0], (), [gains])
+        gain_grads = jnp.sum(gains_all, axis=(0, 1)).reshape(2, -1)
 
         def spread(pieces):
             pieces = lax.all_gather(pieces, 'model', axis=0)

time: 849 us -> 829 us (0.976)
  matrix products: 84.5 us -> 49.2 us
  waiting for transfers between devices: 2.37 us -> 16.8 us
    dot_general x6 -> x0, matrix products: 35.3 us -> none  [the longest x1 7.45 us: device_fn(): jnp.einsum('bsf,df->bsd', d_up, w_up, preferred_element_type=f32)]
    all_gather x4, waiting for transfers between devices: 0.03 us -> 14.1 us  [spread(): pieces = lax.all_gather(pieces, 'model', axis=0)]
    pallas_call x7 -> x8, Pallas kernels: 706 us -> 713 us  [the longest x7 546 us: ring_gather(): pl.pallas_call(functools.partial(ring_kernel, tuple(dims), tuple(spans),...]
  transfers between devices with their start and end apart: 12 -> 12, of which waited for: 0 -> 1; matrix products, arithmetic and copies ran while one was open for 9% -> 6% of each run, Pallas kernels for 74% -> 58%
where the time goes in v3:
time: 829 us; the launch traced here: 828 us
  Pallas kernels  713 us (86%)
  matrix products  49.2 us (6%)
  local copies, waits for them, and re-layouts  19.2 us (2%)
  waiting for transfers between devices  16.8 us (2%)
  between operations  14.7 us (2%)
  other arithmetic  14.2 us (2%)
    pallas_call x7, Pallas kernels, ring_gather(): pl.pallas_call(functools.partial(ring_kernel, tuple(dims), tuple(spans),...  546 us
    pallas_call x1, Pallas kernels, ring_mlp(): pl.pallas_call(mlp_kernel, out_shape=[hidden, hidden, hidden, partial_sum...  167 us
    dot_general x5, matrix products, pair(): lax.dot_general(left, right, (((0,), (0,)), ((), ())), preferred_element_...  29.4 us
  transfers between devices with their start and end apart: 12, of which 1 were waited for; matrix products, arithmetic and copies ran while one was open for 6% of the time, Pallas kernels for 58%

profile of v3, /device:TPU:0, one launch (start us, length us, event | category | flops | bytes accessed | tf_op | source)
XLA Modules:
  0.0 828.0 jit_solution(13420539779877051820)
XLA Ops:
  9.4 1.8 fusion.18.refs_2_
  13.0 96.2 %ring_gather_0.1 = (bf16[2048,1536]{1,0:T(8,128)(2,1)}, bf16[512,2048]{1,0:T(8,128)(2,1)}, bf16[8,2,32,256]{3,2,1,0:T(8,128)(2,1)}, bf16[8,2,32,256]{3,2,1,0:T(8,128)(2,1)}) custom-call(bf16[256,1536]{1,0:T(8,128)(2,1)} %refs_0_.1, bf16[512,256]{1,0:T(8,128)(2,1)} %refs_1_.1, bf16[2,32,2048]{2,1,0:T(8,128)(2,1)} %fusion.18.refs_2_, bf16[2,32,2048]{2,1,0:T(8,128)(2,1)} %refs_3_.1), custom_call_target="tpu_custom_call" | custom-call | flops 22020096000 | bytes 14680064 | tf_op jit(solution)/shard_map/ring_gather_0/pallas_call | solution.py:178
  109.2 4.9 fusion.2
  116.9 1.4 convolution_convert_fusion
  118.3 2.0 fusion.6
  120.4 54.0 %ring_gather_1.1.down_a = bf16[1024,2048]{1,0:T(8,128)(2,1)} custom-call(bf16[2048,256]{1,0:T(8,128)(2,1)} %refs_0_.3), custom_call_target="tpu_custom_call" | custom-call | flops 11010048000 | bytes 7340032 | tf_op jit(solution)/shard_map/ring_gather_1/pallas_call | solution.py:178
  174.5 1.2 fusion.28
  177.2 54.1 %ring_gather_2.1 = (bf16[1024,2048]{1,0:T(8,128)(2,1)}, bf16[8,2,32,256]{3,2,1,0:T(8,128)(2,1)}) custom-call(bf16[2048,256]{1,0:T(8,128)(2,1)} %refs_0_.3, bf16[2,32,2048]{2,1,0:T(8,128)(2,1)} %fusion.17.refs_1_), custom_call_target="tpu_custom_call" | custom-call | flops 11010048000 | bytes 7340032 | tf_op jit(solution)/shard_map/ring_gather_2/pallas_call | solution.py:178
  231.4 167.3 %ring_mlp_7.1 = (bf16[256,2048]{1,0:T(8,128)(2,1)}, bf16[256,2048]{1,0:T(8,128)(2,1)}, bf16[256,2048]{1,0:T(8,128)(2,1)}, f32[256,2048]{1,0:T(8,128)}, f32[256,2048]{1,0:T(8,128)}) custom-call(bf16[256,2048]{1,0:T(8,128)(2,1)} %gate_sh.1, bf16[256,2048]{1,0:T(8,128)(2,1)} %up_sh.1, bf16[1024,2048]{1,0:T(8,128)(2,1)} %ring_gather_1.1.down_a, ...), custom_call_target="tpu_custom_call" | custom-call | flops 44040192000 | bytes 29360128 | tf_op jit(solution)/shard_map/ring_mlp_7/pallas_call | solution.py:317
  400.9 79.5 %ring_gather_3.1 = bf16[2048,2048]{1,0:T(8,128)(2,1)} custom-call(bf16[256,2048]{1,0:T(8,128)(2,1)} %get-tuple-element.50.refs_0_), custom_call_target="tpu_custom_call" | custom-call | flops 22020096000 | bytes 14680064 | tf_op jit(solution)/shard_map/ring_gather_3/pallas_call | solution.py:178
  480.5 1.2 fusion.19
  481.7 2.2 fusion.22
  484.0 1.3 copy.128
  485.3 14.1 %all-gather.27.cloned.1.call-done = bf16[32,2,32,256]{3,2,1,0:T(8,128)(2,1)} async-done(((bf16[8,2,32,256]{3,2,1,0:T(8,128)(2,1)}), bf16[32,2,32,256]{3,2,1,0:T(8,128)(2,1)}) %all-gather.27.cloned.1.call-update) | async-done | bytes 1048592 | tf_op jit(solution)/shard_map/all_gather | solution.py:434
  499.5 2.3 copy.131
  502.9 109.3 %ring_gather_4.1 = (bf16[2048,2048]{1,0:T(8,128)(2,1)}, bf16[2048,512]{1,0:T(8,128)(2,1)}, bf16[8,2,32,256]{3,2,1,0:T(8,128)(2,1)}) custom-call(bf16[256,2048]{1,0:T(8,128)(2,1)} %get-tuple-element.54.refs_0_, bf16[256,512]{1,0:T(8,128)(2,1)} %bitcast.143, bf16[2,32,2048]{2,1,0:T(8,128)(2,1)} %get-tuple-element.56.refs_2_), custom_call_target="tpu_custom_call" | custom-call | flops 27525120000 | bytes 18350080 | tf_op jit(solution)/shard_map/ring_gather_4/pallas_call | solution.py:178
  612.4 2.7 fusion.9
  615.2 1.3 multiply_reduce_fusion
  619.0 6.0 fusion
  625.0 1.2 copy-done.7
  626.2 7.2 fusion.57
  633.4 1.3 copy.130
  634.7 7.8 fusion.55
  642.6 1.8 copy.126
  644.4 1.5 copy.129
  646.5 1.5 fusion.54
  648.1 83.7 %ring_gather_5.1 = bf16[2048,2048]{1,0:T(8,128)(2,1)} custom-call(bf16[256,2048]{1,0:T(8,128)(2,1)} %get-tuple-element.60.refs_0_), custom_call_target="tpu_custom_call" | custom-call | flops 22020096000 | bytes 14680064 | tf_op jit(solution)/shard_map/ring_gather_5/pallas_call | solution.py:178
  731.8 7.1 fusion.56
  739.0 1.2 fusion.20
  740.9 1.9 fusion.24
  744.0 69.1 %ring_gather_6.1 = (bf16[2048,1536]{1,0:T(8,128)(2,1)}, f32[8,4,16,256]{3,2,1,0:T(8,128)}, f32[4,16,256]{2,1,0:T(8,128)}) custom-call(bf16[256,1536]{1,0:T(8,128)(2,1)} %copy.127.refs_0_, f32[16,256]{1,0:T(8,128)} %reshape.175.refs_1_), custom_call_target="tpu_custom_call" | custom-call | flops 16515072000 | bytes 11010048 | tf_op jit(solution)/shard_map/ring_gather_6/pallas_call | solution.py:178
  815.4 5.7 fusion.53
  (102 shorter events, 19.2 us)
Async XLA Ops:
  7.2 102.1 %all-gather.13.cloned.1.call-start = ((), (), s32[]{:S(2)}) async-start(), calls=%async_computation.4 | async-start | bytes 1310720 | tf_op jit(solution)/shard_map/all_gather | solution.py:345
  8.3 0.6 copy-start.13
  8.9 0.6 copy-start.11
  11.3 163.2 %reduce-scatter.5.cloned.1.call-start = ((), (), s32[]{:S(2)}) async-start(), calls=%async_computation.5 | async-start | bytes 2621440 | tf_op jit(solution)/shard_map/reduce_scatter | solution.py:348
  114.1 1.1 copy-start.8
  116.4 1.9 copy-start.5
  120.4 54.1 %copy-start = (bf16[2,32,2048]{2,1,0:T(8,128)(2,1)S(1)}, bf16[2,32,2048]{2,1,0:T(8,128)(2,1)}, u32[]{:S(2)}) copy-start(bf16[2,32,2048]{2,1,0:T(8,128)(2,1)} %param.11) | copy-start | bytes 786436
  120.4 55.3 %copy-start.9 = (f32[2048]{0:T(1024)S(1)}, f32[2048]{0:T(1024)}, u32[]{:S(2)}) copy-start(f32[2048]{0:T(1024)} %param.14) | copy-start | bytes 24580
  120.4 111.0 %all-gather.15.cloned.1.call-start = ((), (), s32[]{:S(2)}) async-start(), calls=%async_computation.6 | async-start | bytes 1310720 | tf_op jit(solution)/shard_map/all_gather | solution.py:345
  176.6 54.8 %all-gather.17.cloned.1.call-start = ((), (), s32[]{:S(2)}) async-start(), calls=%async_computation.7 | async-start | bytes 1310720 | tf_op jit(solution)/shard_map/all_gather | solution.py:345
  177.2 303.2 %reduce-scatter.9.cloned.1.call-start = ((), (), s32[]{:S(2)}) async-start(), calls=%async_computation.9 | async-start | bytes 2621440 | tf_op jit(solution)/shard_map/reduce_scatter | solution.py:348
  398.8 81.7 %reduce-scatter.7.cloned.1.call-start = ((), (), s32[]{:S(2)}) async-start(), calls=%async_computation.8 | async-start | bytes 2621440 | tf_op jit(solution)/shard_map/reduce_scatter | solution.py:348
  399.4 84.6 %all-gather.21.cloned.1.call-start = ((), (), s32[]{:S(2)}) async-start(), calls=%async_computation.12 | async-start | bytes 1310720 | tf_op jit(solution)/shard_map/all_gather | solution.py:434
  400.1 99.3 %all-gather.27.cloned.1.call-start = ((), (), s32[]{:S(2)}) async-start(), calls=%async_computation.15 | async-start | bytes 1310720 | tf_op jit(solution)/shard_map/all_gather | solution.py:434
  400.9 211.5 %all-gather.19.cloned.1.call-start = ((), (), s32[]{:S(2)}) async-start(), calls=%async_computation.10 | async-start | bytes 1310720 | tf_op jit(solution)/shard_map/all_gather | solution.py:345
  400.9 80.8 %copy-start.6 = (bf16[2,32,2048]{2,1,0:T(8,128)(2,1)S(1)}, bf16[2,32,2048]{2,1,0:T(8,128)(2,1)}, u32[]{:S(2)}) copy-start(bf16[2,32,2048]{2,1,0:T(8,128)(2,1)} %refs_3_.1) | copy-start | bytes 786436
  483.9 149.5 %all-gather.25.cloned.1.call-start = ((), (), s32[]{:S(2)}) async-start(), calls=%async_computation.14 | async-start | bytes 1310720 | tf_op jit(solution)/shard_map/all_gather | solution.py:434
  502.7 141.7 %all-gather.23.cloned.1.call-start = ((), (), s32[]{:S(2)}) async-start(), calls=%async_computation.13 | async-start | bytes 1310720 | tf_op jit(solution)/shard_map/all_gather | solution.py:434
  612.3 126.7 %reduce-scatter.11.cloned.1.call-start = ((), (), s32[]{:S(2)}) async-start(), calls=%async_computation.11 | async-start | bytes 2621440 | tf_op jit(solution)/shard_map/reduce_scatter | solution.py:348
  625.0 1.2 copy-start.7
  644.4 1.5 copy-start.2
  644.4 2.2 copy-start.4
  731.8 7.2 copy-start.1
  731.8 7.2 copy-start.10
  731.8 7.2 copy-start.12
  731.8 9.0 %copy-start.14 = (f32[2,32]{1,0:T(2,128)S(1)}, f32[2,32]{1,0:T(2,128)}, u32[]{:S(2)}) copy-start(f32[2,32]{1,0:T(2,128)} %copy-done.13) | copy-start | bytes 772
  731.8 9.0 %copy-start.3 = (bf16[2,32,2048]{2,1,0:T(8,128)(2,1)S(1)}, bf16[2,32,2048]{2,1,0:T(8,128)(2,1)}, u32[]{:S(2)}) copy-start(bf16[2,32,2048]{2,1,0:T(8,128)(2,1)} %get-tuple-element.56.refs_2_) | copy-start | bytes 786436
Sparse Core Ops, SparseCore 0:
  11.4 19.4 all-gather.12
  120.5 31.4 reduce-scatter.4
  176.7 15.5 all-gather.14
  193.7 16.6 all-gather.16
  398.9 30.2 reduce-scatter.8
  431.6 31.1 reduce-scatter.6
  464.4 16.7 all-gather.20
  482.7 16.6 all-gather.26
  501.6 16.6 all-gather.18
  519.7 16.6 all-gather.24
  612.4 15.3 all-gather.22
  630.2 31.1 reduce-scatter.10

commit v4 on v3

--- a/solution.py
+++ b/solution.py
@@ -40,12 +40,15 @@
     return 2 * (place + y * (7 - 2 * place)) + y
 
 
-def ring_kernel(dims, spans, slices, sums, *refs):
+def ring_kernel(dims, spans, slices, kinds, sums, *refs):
     count = len(dims)
-    total = count + slices + sums
+    first_model = count + slices
+    last = first_model + len(kinds)
+    total = last + sums
     ins, outs = refs[:total], refs[total:2 * total]
     mix = refs[2 * total] if sums else None
-    send_sem, recv_sem, local_sem, slice_send, slice_recv, slice_local, mix_send, mix_recv, mix_local = refs[-9:]
+    (send_sem, recv_sem, local_sem, slice_send, slice_recv, slice_local, mix_send, mix_recv, mix_local,
+     model_send, model_recv, model_local) = refs[-12:]
     me = lax.axis_index('fsdp')
     me_model = lax.axis_index('model')
     place = ring_place(me)
@@ -55,14 +58,14 @@
     peers = [(me + hop) % 8 for hop in range(1, 8)] if slices else targets
     for peer in peers:
         pl.semaphore_signal(barrier, inc=1, device_id={'fsdp': peer}, device_id_type=MESH)
-    if sums:
+    if sums or kinds:
         for hop in range(1, 4):
             pl.semaphore_signal(barrier, inc=1, device_id={'model': (me_model + hop) % 4}, device_id_type=MESH)
-    pl.semaphore_wait(barrier, len(peers) + 3 * sums)
+    pl.semaphore_wait(barrier, len(peers) + (3 if sums or kinds else 0))
 
     def piece(idx, owner, way):
         if idx == count:
-            return outs[count + slices].at[owner, pl.ds(2 * way, 2)]
+            return outs[last].at[owner, pl.ds(2 * way, 2)]
         half = spans[idx][1] // 2
         cols = ins[idx].shape[1]
         if dims[idx] == 0:
@@ -116,11 +119,42 @@
     def mix_copy(hop, incoming):
         slot = mix.at[(me_model + 4 - hop) % 4 if incoming else me_model]
         return pltpu.make_async_remote_copy(
-            src_ref=slot if incoming else ins[count + slices], dst_ref=slot, send_sem=mix_send.at[hop],
+            src_ref=slot if incoming else ins[last], dst_ref=slot, send_sem=mix_send.at[hop],
             recv_sem=mix_recv.at[hop], device_id={'model': (me_model + hop) % 4}, device_id_type=MESH)
 
     def mix_own():
-        return pltpu.make_async_copy(ins[count + slices], mix.at[me_model], mix_local)
+        return pltpu.make_async_copy(ins[last], mix.at[me_model], mix_local)
+
+    def model_src(idx, peer):
+        src = ins[first_model + idx]
+        if kinds[idx] != 'sum':
+            return src
+        block = src.shape[1] // 4
+        return src.at[:, pl.ds(pl.multiple_of(peer * block, block), block), :]
+
+    def model_dst(idx, member):
+        dst = outs[first_model + idx]
+        if kinds[idx] == 'sum':
+            return dst.at[member]
+        if kinds[idx] == 'cols':
+            return dst.at[:, :, member]
+        block = dst.shape[1] // 4
+        return dst.at[:, pl.ds(pl.multiple_of(member * block, block), block), :]
+
+    def model_out(idx, hop):
+        peer = (me_model + hop) % 4
+        return pltpu.make_async_remote_copy(
+            src_ref=model_src(idx, peer), dst_ref=model_dst(idx, me_model), send_sem=model_send.at[idx, hop],
+            recv_sem=model_recv.at[idx, hop], device_id={'model': peer}, device_id_type=MESH)
+
+    def model_in(idx, hop):
+        slot = model_dst(idx, (me_model + 4 - hop) % 4)
+        return pltpu.make_async_remote_copy(
+            src_ref=slot, dst_ref=slot, send_sem=model_send.at[idx, hop], recv_sem=model_recv.at[idx, hop],
+            device_id={'model': (me_model + hop) % 4}, device_id_type=MESH)
+
+    def model_own(idx):
+        return pltpu.make_async_copy(model_src(idx, me_model), model_dst(idx, me_model), model_local.at[idx])
 
     if sums:
         mix_own().start()
@@ -142,6 +176,10 @@
                 slice_own(idx).start()
                 for hop in range(1, 8):
                     slice_out(idx, hop).start()
+            for idx in range(len(kinds)):
+                for hop in range(1, 4):
+                    model_out(idx, hop).start()
+                model_own(idx).start()
             for idx in range(count + sums):
                 for way in range(2):
                     own(idx, way).start()
@@ -156,9 +194,14 @@
         for hop in range(1, 8):
             slice_in(idx, hop).wait_recv()
             slice_out(idx, hop).wait_send()
-
-
-def ring_gather(collective_id, arrays, dims, slices=(), sums=(), spans=None):
+    for idx in range(len(kinds)):
+        model_own(idx).wait()
+        for hop in range(1, 4):
+            model_in(idx, hop).wait_recv()
+            model_out(idx, hop).wait_send()
+
+
+def ring_gather(collective_id, arrays, dims, slices=(), model=(), sums=(), spans=None):
     shapes = []
     sent = 0
     spans = spans or [(0, array.shape[0]) for array in arrays]
@@ -168,6 +211,14 @@
         sent += 7 * rows * cols * 2
     for array in slices:
         shapes.append(jax.ShapeDtypeStruct((8,) + array.shape[:2] + (array.shape[2] // 8,), array.dtype))
+    for kind, array in model:
+        if kind == 'sum':
+            shape = (4, array.shape[0], array.shape[1] // 4, array.shape[2])
+        elif kind == 'cols':
+            shape = array.shape[:2] + (4,) + array.shape[2:]
+        else:
+            shape = (array.shape[0], 4 * array.shape[1], array.shape[2])
+        shapes.append(jax.ShapeDtypeStruct(shape, array.dtype))
     for array in sums:
         shapes.append(jax.ShapeDtypeStruct((8, 4) + array.shape, array.dtype))
     n_in = len(shapes)
@@ -176,17 +227,18 @@
     count, n_slices, n_sums = len(arrays), len(slices), len(sums)
     dma = pltpu.SemaphoreType.DMA
     return pl.pallas_call(
-        functools.partial(ring_kernel, tuple(dims), tuple(spans), n_slices, n_sums),
+        functools.partial(ring_kernel, tuple(dims), tuple(spans), n_slices, tuple(kind for kind, _ in model), n_sums),
         out_shape=shapes,
         in_specs=[pl.BlockSpec(memory_space=pl.ANY)] * n_in,
         out_specs=[pl.BlockSpec(memory_space=pl.ANY)] * len(shapes),
         scratch_shapes=[dma((count + n_sums, 2, 7)), dma((count + n_sums, 2, 7)), dma((count + n_sums, 2)),
                         dma((max(n_slices, 1), 8)), dma((max(n_slices, 1), 8)), dma((max(n_slices, 1),)),
-                        dma((4,)), dma((4,)), dma],
+                        dma((4,)), dma((4,)), dma, dma((max(len(model), 1), 4)), dma((max(len(model), 1), 4)),
+                        dma((max(len(model), 1),))],
         compiler_params=pltpu.CompilerParams(collective_id=collective_id, has_side_effects=True),
         cost_estimate=pl.CostEstimate(flops=sent * 3000, bytes_accessed=2 * sent, transcendentals=0),
         name=f'ring_gather_{collective_id}',
-    )(*arrays, *slices, *sums)
+    )(*arrays, *slices, *[array for _, array in model], *sums)
 
 
 TILE = 512
@@ -330,8 +382,8 @@
     )(gate_sh, up_sh, down_a, down_b, h_full, dy_full)
 
 
-def after(values, *deps):
-    return lax.optimization_barrier((tuple(values), deps))[0]
+def add_blocks(blocks):
+    return (blocks[0] + blocks[1]) + (blocks[2] + blocks[3])
 
 
 def solution(mesh):
@@ -340,12 +392,6 @@
     cols_spec = P('model', 'fsdp')
     f32 = jnp.float32
     bf16 = jnp.bfloat16
-
-    def gather_seq(tensor):
-        return lax.all_gather(tensor, 'model', axis=1, tiled=True)
-
-    def scatter_seq(tensor):
-        return lax.psum_scatter(tensor, 'model', scatter_dimension=1, tiled=True)
 
     def device_fn(x_loc, dy_loc, gain_attn, gain_mlp, wqkv_sh, wout_sh, wgate_sh, wup_sh, wdown_sh, rope_cos, rope_sin):
         head_dim = 2 * rope_cos.shape[1]
@@ -366,9 +412,8 @@
         x_f32 = x_loc.astype(f32)
         h_attn_f, norm_back_attn = jax.vjp(rms_scale, x_f32, gain_attn)
         h_attn_loc = h_attn_f.astype(bf16)
-        h_attn = gather_seq(h_attn_loc)
-        dy_full = gather_seq(dy_loc)
-        w_qkv, w_out, h_attn_cols, dy_cols = ring_gather(0, [wqkv_sh, wout_sh], [0, 1], [h_attn_loc, dy_loc])
+        w_qkv, w_out, h_attn_cols, dy_cols, h_attn, dy_full = ring_gather(
+            0, [wqkv_sh, wout_sh], [0, 1], [h_attn_loc, dy_loc], [('seq', h_attn_loc), ('seq', dy_loc)])
         qkv = jnp.einsum('bsd,dc->bsc', h_attn, w_qkv, preferred_element_type=f32)
         qkv = qkv.reshape(rows, seq_full, local_kv, group_size + 2, head_dim)
         query = rotate(qkv[:, :, :, :group_size], cos_q, sin_q).astype(bf16)
@@ -380,33 +425,28 @@
         attn = jnp.einsum('bkgqt,btkd->bqkgd', prob_bf, value, preferred_element_type=f32)
         attn_flat = attn.astype(bf16).reshape(rows, seq_full, local_heads * head_dim)
         attn_part = jnp.einsum('bsh,hd->bsd', attn_flat, w_out, preferred_element_type=f32)
-        attn_red = scatter_seq(attn_part)
         half_down = wdown_sh.shape[0] // 2
-        down_a, = ring_gather(1, after([wdown_sh], attn_part), [1], spans=[(0, half_down)])
-        attn_red, = after([attn_red], down_a)
+        down_a, attn_red = ring_gather(1, [wdown_sh], [1], (), [('sum', attn_part)], spans=[(0, half_down)])
+        attn_red = add_blocks(attn_red)
         mid_f32 = (x_f32 + attn_red.astype(bf16).astype(f32)).astype(bf16).astype(f32)
         h_mlp_f, norm_back_mlp = jax.vjp(rms_scale, mid_f32, gain_mlp)
         h_mlp_loc = h_mlp_f.astype(bf16)
-        h_mlp = gather_seq(h_mlp_loc)
-        wdown_sh, h_mlp_src = after([wdown_sh, h_mlp_loc])
-        down_b, h_mlp_cols = ring_gather(2, [wdown_sh], [1], [h_mlp_src], spans=[(half_down, half_down)])
-        h_mlp, = after([h_mlp], down_b)
+        down_b, h_mlp_cols, h_mlp, h_attn_cols, dy_cols = ring_gather(
+            2, [wdown_sh], [1], [h_mlp_loc], [('seq', h_mlp_loc), ('cols', h_attn_cols), ('cols', dy_cols)],
+            spans=[(half_down, half_down)])
         gated_act, d_gate, d_up, mlp_part, dh_part = ring_mlp(
             7, wgate_sh, wup_sh, down_a, down_b, h_mlp.reshape(tokens, -1), dy_full.reshape(tokens, -1))
         mlp_part = mlp_part.reshape(rows, seq_full, -1)
         dh_part = dh_part.reshape(rows, seq_full, -1)
-        dh_mlp = scatter_seq(dh_part)
-        mlp_red = scatter_seq(mlp_part)
-        act_all, = ring_gather(3, [gated_act], [0])
-        dh_mlp, mlp_red = after([dh_mlp, mlp_red], act_all)
+        act_all, dh_mlp, mlp_red, h_mlp_cols = ring_gather(
+            3, [gated_act], [0], (), [('sum', dh_part), ('sum', mlp_part), ('cols', h_mlp_cols)])
+        dh_mlp, mlp_red = add_blocks(dh_mlp), add_blocks(mlp_red)
         y_loc = (mid_f32 + mlp_red.astype(bf16).astype(f32)).astype(bf16)
         d_mid_norm, d_gain_mlp = norm_back_mlp(dh_mlp.astype(bf16).astype(f32))
         d_mid = (dy_loc.astype(f32) + d_mid_norm).astype(bf16)
 
-        d_mid_full = gather_seq(d_mid)
-        flat_gate, flat_attn, d_mid_src = after([d_gate, attn_flat.reshape(tokens, -1), d_mid])
-        d_gate_all, attn_all, d_mid_cols = ring_gather(4, [flat_gate, flat_attn], [0, 0], [d_mid_src])
-        d_mid_full, = after([d_mid_full], d_gate_all)
+        d_gate_all, attn_all, d_mid_cols, d_mid_full = ring_gather(
+            4, [d_gate, attn_flat.reshape(tokens, -1)], [0, 0], [d_mid], [('seq', d_mid)])
         d_attn = jnp.einsum('bsd,hd->bsh', d_mid_full, w_out, preferred_element_type=f32).astype(bf16)
         d_attn = d_attn.reshape(rows, seq_full, local_kv, group_size, head_dim)
         d_prob = jnp.einsum('bqkgd,btkd->bkgqt', d_attn, value, preferred_element_type=f32)
@@ -420,21 +460,16 @@
                                  d_value[:, :, :, None]], axis=3)
         d_qkv = d_qkv.astype(bf16).reshape(rows, seq_full, -1)
         dh_attn_part = jnp.einsum('bsc,dc->bsd', d_qkv, w_qkv, preferred_element_type=f32)
-        dh_attn = scatter_seq(dh_attn_part)
-        d_up_all, = ring_gather(5, after([d_up], dh_attn_part), [0])
-        dh_attn, = after([dh_attn], d_up_all)
+        d_up_all, dh_attn, d_mid_cols = ring_gather(
+            5, [d_up], [0], (), [('sum', dh_attn_part), ('cols', d_mid_cols)])
+        dh_attn = add_blocks(dh_attn)
         d_x_norm, d_gain_attn = norm_back_attn(dh_attn.astype(bf16).astype(f32))
         dx_loc = (d_mid.astype(f32) + d_x_norm).astype(bf16)
         gains = jnp.stack([d_gain_attn, d_gain_mlp]).reshape(16, -1)
-        flat_qkv, gains = after([d_qkv.reshape(tokens, -1), gains])
-        d_qkv_all, gains_all, _ = ring_gather(6, [flat_qkv], [0], (), [gains])
+        d_qkv_all, gains_all, _ = ring_gather(6, [d_qkv.reshape(tokens, -1)], [0], sums=[gains])
         gain_grads = jnp.sum(gains_all, axis=(0, 1)).reshape(2, -1)
-
-        def spread(pieces):
-            pieces = lax.all_gather(pieces, 'model', axis=0)
-            return pieces.transpose(1, 2, 0, 3, 4).reshape(8 * tokens, -1)
-
-        h_attn_cols, dy_cols, h_mlp_cols, d_mid_cols = map(spread, (h_attn_cols, dy_cols, h_mlp_cols, d_mid_cols))
+        h_attn_cols, dy_cols, h_mlp_cols, d_mid_cols = [
+            cols.reshape(8 * tokens, -1) for cols in (h_attn_cols, dy_cols, h_mlp_cols, d_mid_cols)]
 
         def pair(left, right):
             return lax.dot_general(left, right, (((0,), (0,)), ((), ())), preferred_element_type=f32)

time: 829 us -> 814 us (0.982)
  Pallas kernels: 713 us -> 734 us
  waiting for transfers between devices: 16.8 us -> 0 us
  between operations: 14.7 us -> 1 us
  local copies, waits for them, and re-layouts: 19.2 us -> 10.9 us
    pallas_call x7, Pallas kernels: 546 us -> 561 us  [ring_gather(): pl.pallas_call(functools.partial(ring_kernel, tuple(dims), tuple(spans),...]
    all_gather x8 -> x0, waiting for transfers between devices: 14.2 us -> none  [the longest x4 14.1 us: spread(): pieces = lax.all_gather(pieces, 'model', axis=0)]
  transfers between devices with their start and end apart: 12 -> 0, of which waited for: 1 -> 0; matrix products, arithmetic and copies ran while one was open for 6% -> 0% of each run, Pallas kernels for 58% -> 0%
where the time goes in v4:
time: 814 us; the launch traced here: 813 us
  Pallas kernels  734 us (90%)
  matrix products  50.9 us (6%)
  other arithmetic  15.7 us (2%)
  local copies, waits for them, and re-layouts  10.9 us (1%)
    pallas_call x7, Pallas kernels, ring_gather(): pl.pallas_call(functools.partial(ring_kernel, tuple(dims), tuple(spans),...  561 us
    pallas_call x1, Pallas kernels, ring_mlp(): pl.pallas_call(mlp_kernel, out_shape=[hidden, hidden, hidden, partial_sum...  173 us
    dot_general x5, matrix products, pair(): lax.dot_general(left, right, (((0,), (0,)), ((), ())), preferred_element_...  29.8 us

profile of v4, /device:TPU:0, one launch (start us, length us, event | category | flops | bytes accessed | tf_op | source)
XLA Modules:
  0.0 812.7 jit_solution(3550292919037919556)
XLA Ops:
  0.6 1.1 fusion.25
  2.3 0.8 copy.46
  3.2 0.9 copy.47
  4.0 1.8 fusion.18.refs_2_.refs_4_
  5.8 96.3 %ring_gather_0.1 = (bf16[2048,1536]{1,0:T(8,128)(2,1)}, bf16[512,2048]{1,0:T(8,128)(2,1)}, bf16[8,2,32,256]{3,2,1,0:T(8,128)(2,1)}, bf16[8,2,32,256]{3,2,1,0:T(8...) custom-call(bf16[256,1536]{1,0:T(8,128)(2,1)} %refs_0_.3, bf16[512,256]{1,0:T(8,128)(2,1)} %refs_1_.1, ...), custom_call_target="tpu_custom_call" | custom-call | flops 22020096000 | bytes 14680064 | tf_op jit(solution)/shard_map/ring_gather_0/pallas_call | solution.py:229
  102.1 4.9 fusion.2
  107.0 1.1 copy-done.6
  108.6 1.1 fusion.57
  110.8 1.3 convolution_convert_fusion
  113.1 3.6 fusion.6.refs_1_
  116.7 55.8 %ring_gather_1.1 = (bf16[1024,2048]{1,0:T(8,128)(2,1)}, f32[4,2,32,2048]{3,2,1,0:T(8,128)}) custom-call(bf16[2048,256]{1,0:T(8,128)(2,1)} %refs_0_.5, f32[2,128,2048]{2,1,0:T(8,128)} %fusion.6.refs_1_), custom_call_target="tpu_custom_call" | custom-call | flops 11010048000 | bytes 7340032 | tf_op jit(solution)/shard_map/ring_gather_1/pallas_call | solution.py:229
  172.6 1.7 fusion.28
  175.2 56.0 %ring_gather_2.1 = (bf16[1024,2048]{1,0:T(8,128)(2,1)}, bf16[8,2,32,256]{3,2,1,0:T(8,128)(2,1)}, bf16[2,128,2048]{2,1,0:T(8,128)(2,1)}, bf16[8,2,4,32,256]{4,3,2,1,0:T(8,128)(2,1)}, bf16[8,2,4,32,256]{4,3,2,1,0:T(8,128)(2,1)}) custom-call(bf16[2048,256]{1,0:T(8,128)(2,1)} %refs_0_.5, bf16[2,32,2048]{2,1,0:T(8,128)(2,1)} %fusion.17.refs_1_.refs_2_, ...), custom_call_target="tpu_custom_call" | custom-call | flops 11010048000 | bytes 7340032 | tf_op jit(solution)/shard_map/ring_gather_2/pallas_call | solution.py:229
  231.2 173.1 %ring_mlp_7.1 = (bf16[256,2048]{1,0:T(8,128)(2,1)}, bf16[256,2048]{1,0:T(8,128)(2,1)}, bf16[256,2048]{1,0:T(8,128)(2,1)}, f32[256,2048]{1,0:T(8,128)}, f32[256,2048]{1,0:T(8,128)}) custom-call(bf16[256,2048]{1,0:T(8,128)(2,1)} %gate_sh.1, bf16[256,2048]{1,0:T(8,128)(2,1)} %up_sh.1, bf16[1024,2048]{1,0:T(8,128)(2,1)} %get-tuple-element.44.down_a, ...), custom_call_target="tpu_custom_call" | custom-call | flops 44040192000 | bytes 29360128 | tf_op jit(solution)/shard_map/ring_mlp_7/pallas_call | solution.py:369
  404.3 89.5 %ring_gather_3.1 = (bf16[2048,2048]{1,0:T(8,128)(2,1)}, f32[4,2,32,2048]{3,2,1,0:T(8,128)}, f32[4,2,32,2048]{3,2,1,0:T(8,128)}, bf16[8,2,4,32,256]{4,3,2,1,0:T(8,128)(2,1)}) custom-call(bf16[256,2048]{1,0:T(8,128)(2,1)} %get-tuple-element.50.refs_0_, f32[2,128,2048]{2,1,0:T(8,128)} %bitcast.140, f32[2,128,2048]{2,1,0:T(8,128)} %bitcast.139, ...), custom_call_target="tpu_custom_call" | custom-call | flops 22020096000 | bytes 14680064 | tf_op jit(solution)/shard_map/ring_gather_3/pallas_call | solution.py:229
  493.8 1.9 fusion.20
  496.0 1.1 fusion.22
  497.2 7.2 fusion.63
  504.3 106.7 %ring_gather_4.1 = (bf16[2048,2048]{1,0:T(8,128)(2,1)}, bf16[2048,512]{1,0:T(8,128)(2,1)}, bf16[8,2,32,256]{3,2,1,0:T(8,128)(2,1)}, bf16[2,128,2048]{2,1,0:T(8,128)(2,1)}) custom-call(bf16[256,2048]{1,0:T(8,128)(2,1)} %get-tuple-element.57.refs_0_, bf16[256,512]{1,0:T(8,128)(2,1)} %bitcast.132, bf16[2,32,2048]{2,1,0:T(8,128)(2,1)} %get-tuple-element.89.refs_2_.refs_3_, ...), custom_call_target="tpu_custom_call" | custom-call | flops 27525120000 | bytes 18350080 | tf_op jit(solution)/shard_map/ring_gather_4/pallas_call | solution.py:229
  611.1 2.7 fusion.9
  613.9 1.3 multiply_reduce_fusion
  617.7 6.0 fusion.refs_1_
  624.3 1.4 reshape.210.refs_0_
  625.7 7.0 fusion.61
  632.8 87.6 %ring_gather_5.1 = (bf16[2048,2048]{1,0:T(8,128)(2,1)}, f32[4,2,32,2048]{3,2,1,0:T(8,128)}, bf16[8,2,4,32,256]{4,3,2,1,0:T(8,128)(2,1)}) custom-call(bf16[256,2048]{1,0:T(8,128)(2,1)} %get-tuple-element.56.refs_0_, f32[2,128,2048]{2,1,0:T(8,128)} %fusion.refs_1_, bf16[8,2,32,256]{3,2,1,0:T(8,128)(2,1)} %get-tuple-element.59.refs_2_), custom_call_target="tpu_custom_call" | custom-call | flops 22020096000 | bytes 14680064 | tf_op jit(solution)/shard_map/ring_gather_5/pallas_call | solution.py:229
  720.4 2.6 fusion.19
  723.6 1.9 fusion.24
  725.6 2.8 fusion.60
  728.4 7.0 fusion.62
  735.4 69.2 %ring_gather_6.1 = (bf16[2048,1536]{1,0:T(8,128)(2,1)}, f32[8,4,16,256]{3,2,1,0:T(8,128)}, f32[4,16,256]{2,1,0:T(8,128)}) custom-call(bf16[256,1536]{1,0:T(8,128)(2,1)} %reshape.210.refs_0_, f32[16,256]{1,0:T(8,128)} %reshape.199.refs_1_), custom_call_target="tpu_custom_call" | custom-call | flops 16515072000 | bytes 11010048 | tf_op jit(solution)/shard_map/ring_gather_6/pallas_call | solution.py:229
  804.7 1.1 reduce_sum.105
  807.0 5.7 fusion.59
  (61 shorter events, 9.3 us)
Async XLA Ops:
  1.7 0.6 copy-start.12
  2.3 99.8 %copy-start.10 = (f32[2,32]{1,0:T(2,128)}, f32[2,32]{1,0:T(2,128)S(1)}, u32[]{:S(2)}) copy-start(f32[2,32]{1,0:T(2,128)S(1)} %fusion.47) | copy-start | bytes 772
  107.0 1.1 copy-start.6
  116.7 55.9 %copy-start.1 = (bf16[2,32,2048]{2,1,0:T(8,128)(2,1)S(1)}, bf16[2,32,2048]{2,1,0:T(8,128)(2,1)}, u32[]{:S(2)}) copy-start(bf16[2,32,2048]{2,1,0:T(8,128)(2,1)} %param.11) | copy-start | bytes 786436
  172.6 1.8 copy-start.8
  493.8 2.2 copy-start.5
  493.8 2.2 copy-start.7
  495.7 1.4 copy-start.14
  623.6 2.1 copy-start
  632.8 87.6 %copy-start.2 = (bf16[2,32,2048]{2,1,0:T(8,128)(2,1)S(1)}, bf16[2,32,2048]{2,1,0:T(8,128)(2,1)}, u32[]{:S(2)}) copy-start(bf16[2,32,2048]{2,1,0:T(8,128)(2,1)} %param.11) | copy-start | bytes 786436
  632.8 87.6 %copy-start.9 = (f32[2048]{0:T(1024)S(1)}, f32[2048]{0:T(1024)}, u32[]{:S(2)}) copy-start(f32[2048]{0:T(1024)} %param.13) | copy-start | bytes 24580
  632.8 87.6 %copy-start.11 = (f32[2,32]{1,0:T(2,128)S(1)}, f32[2,32]{1,0:T(2,128)}, u32[]{:S(2)}) copy-start(f32[2,32]{1,0:T(2,128)} %copy-done.10) | copy-start | bytes 772
  720.4 3.3 copy-start.13
  720.4 5.2 copy-start.4
  735.4 71.6 %copy-start.3 = (bf16[8,2,4,32,256]{4,3,2,1,0:T(8,128)(2,1)S(1)}, bf16[8,2,4,32,256]{4,3,2,1,0:T(8,128)(2,1)}, u32[]{:S(2)}) copy-start(bf16[8,2,4,32,256]{4,3,2,1,0:T(8,128)(2,1)} %get-tuple-element.62) | copy-start | bytes 3145732

commit v5 on v4

--- a/solution.py
+++ b/solution.py
@@ -244,51 +244,115 @@
 TILE = 512
 
 
-def mlp_kernel(gate_sh, up_sh, down_a, down_b, h_ref, dy_ref, act_ref, d_gate_ref, d_up_ref, y_part_ref, dh_part_ref,
-               w_gate, w_up, w_down, gate_acc, up_acc, d_act, send_sem, recv_sem, local_sem, down_sem):
+def mlp_kernel(down_sh, gate_sh, up_sh, attn_part, cols_a, cols_b, x_ref, gain_ref, dy_ref,
+               act_ref, d_gate_ref, d_up_ref, y_part_ref, dh_part_ref, mid_ref, h_cols, all_a, all_b,
+               w_down, w_gate, w_up, gate_acc, up_acc, d_act, h_full, h_loc, blocks,
+               send_sem, recv_sem, local_sem, block_send, block_recv, block_local, h_send, h_recv, h_local,
+               slice_send, slice_recv, slice_local, cols_send, cols_recv, cols_local):
     f32, bf16 = jnp.float32, jnp.bfloat16
     me = lax.axis_index('fsdp')
+    me_model = lax.axis_index('model')
     place = ring_place(me)
     targets = (ring_device((place + 1) % 8), ring_device((place + 7) % 8))
     barrier = pltpu.get_barrier_semaphore()
-    for target in targets:
-        pl.semaphore_signal(barrier, inc=1, device_id={'fsdp': target}, device_id_type=MESH)
-    pl.semaphore_wait(barrier, 2)
-    shards, weights, accs = (gate_sh, up_sh), (w_gate, w_up), (gate_acc, up_acc)
+    for hop in range(1, 8):
+        pl.semaphore_signal(barrier, inc=1, device_id={'fsdp': (me + hop) % 8}, device_id_type=MESH)
+    for hop in range(1, 4):
+        pl.semaphore_signal(barrier, inc=1, device_id={'model': (me_model + hop) % 4}, device_id_type=MESH)
+    pl.semaphore_wait(barrier, 10)
+    shards, weights, accs = (down_sh, gate_sh, up_sh), (w_down, w_gate, w_up), (None, gate_acc, up_acc)
     rows, width = gate_sh.shape
     half = rows // 2
+    tall = down_sh.shape[0] // 2
+    block_rows = x_ref.shape[1]
+    slice_width = h_cols.shape[3]
 
     def start_of(owner, way):
         return pl.multiple_of(owner * rows + way * half, half)
 
+    def piece(idx, owner, way):
+        if idx == 0:
+            return w_down.at[pl.ds(way * tall, tall), pl.ds(pl.multiple_of(owner * rows, rows), rows)]
+        return weights[idx].at[pl.ds(start_of(owner, way), half), :]
+
+    def source(idx, way):
+        size = shards[idx].shape[0] // 2
+        return shards[idx].at[pl.ds(way * size, size), :]
+
+    def owner_at(way, step):
+        return ring_device((place + (8 - step if way == 0 else step)) % 8)
+
     def send(idx, way, step):
-        owner = ring_device((place + (8 - step if way == 0 else step)) % 8)
-        dst = weights[idx].at[pl.ds(start_of(owner, way), half), :]
-        src = shards[idx].at[pl.ds(way * half, half), :] if isinstance(step, int) and step == 0 else dst
-        return pltpu.make_async_remote_copy(
-            src_ref=src, dst_ref=dst, send_sem=send_sem.at[idx, way, step], recv_sem=recv_sem.at[idx, way, step],
+        dst = piece(idx, owner_at(way, step), way)
+        return pltpu.make_async_remote_copy(
+            src_ref=source(idx, way) if isinstance(step, int) and step == 0 else dst, dst_ref=dst,
+            send_sem=send_sem.at[idx, way, step], recv_sem=recv_sem.at[idx, way, step],
             device_id={'fsdp': targets[way]}, device_id_type=MESH)
 
     def landed(idx, way, step):
-        owner = ring_device((place + (7 - step if way == 0 else step + 1)) % 8)
-        dst = weights[idx].at[pl.ds(start_of(owner, way), half), :]
+        dst = piece(idx, owner_at(way, step + 1), way)
         return pltpu.make_async_remote_copy(
             src_ref=dst, dst_ref=dst, send_sem=send_sem.at[idx, way, step], recv_sem=recv_sem.at[idx, way, step],
             device_id={'fsdp': targets[way]}, device_id_type=MESH)
 
     def own(idx, way):
-        return pltpu.make_async_copy(shards[idx].at[pl.ds(way * half, half), :],
-                                     weights[idx].at[pl.ds(start_of(me, way), half), :], local_sem.at[idx, way])
-
-    def fetch_down(part):
-        src = (down_a, down_b)[part]
-        return pltpu.make_async_copy(src, w_down.at[pl.ds(part * src.shape[0], src.shape[0]), :], down_sem.at[part])
+        return pltpu.make_async_copy(source(idx, way), piece(idx, me, way), local_sem.at[idx, way])
+
+    def to_member(src, dst, send_sems, recv_sems, hop):
+        return pltpu.make_async_remote_copy(
+            src_ref=src, dst_ref=dst, send_sem=send_sems, recv_sem=recv_sems,
+            device_id={'model': (me_model + hop) % 4}, device_id_type=MESH)
+
+    def block_of(member):
+        return attn_part.at[:, pl.ds(pl.multiple_of(member * block_rows, block_rows), block_rows), :]
+
+    def block_out(hop):
+        return to_member(block_of((me_model + hop) % 4), blocks.at[me_model], block_send.at[hop], block_recv.at[hop], hop)
+
+    def block_in(hop):
+        slot = blocks.at[(me_model + 4 - hop) % 4]
+        return to_member(slot, slot, block_send.at[hop], block_recv.at[hop], hop)
+
+    def block_own():
+        return pltpu.make_async_copy(block_of(me_model), blocks.at[me_model], block_local)
+
+    def h_slot(member):
+        return h_full.at[:, pl.ds(pl.multiple_of(member * block_rows, block_rows), block_rows), :]
+
+    def h_out(hop):
+        return to_member(h_loc, h_slot(me_model), h_send.at[hop], h_recv.at[hop], hop)
+
+    def h_in(hop):
+        slot = h_slot((me_model + 4 - hop) % 4)
+        return to_member(slot, slot, h_send.at[hop], h_recv.at[hop], hop)
+
+    def columns(peer):
+        return h_loc.at[:, :, pl.ds(pl.multiple_of(peer * slice_width, slice_width), slice_width)]
+
+    def slice_copy(hop, incoming):
+        peer = (me + hop) % 8
+        slot = h_cols.at[(me + 8 - hop) % 8 if incoming else me]
+        return pltpu.make_async_remote_copy(
+            src_ref=slot if incoming else columns(peer), dst_ref=slot, send_sem=slice_send.at[hop],
+            recv_sem=slice_recv.at[hop], device_id={'fsdp': peer}, device_id_type=MESH)
+
+    def slice_own():
+        return pltpu.make_async_copy(columns(me), h_cols.at[me], slice_local)
+
+    cols_in, cols_all = (cols_a, cols_b), (all_a, all_b)
+
+    def cols_copy(idx, hop, incoming):
+        slot = cols_all[idx].at[:, :, (me_model + 4 - hop) % 4 if incoming else me_model]
+        return to_member(slot if incoming else cols_in[idx], slot, cols_send.at[idx, hop], cols_recv.at[idx, hop], hop)
+
+    def cols_own(idx):
+        return pltpu.make_async_copy(cols_in[idx], cols_all[idx].at[:, :, me_model], cols_local.at[idx])
 
     def accumulate(step):
         for way in range(2):
-            start = start_of(ring_device((place + (8 - step if way == 0 else step)) % 8), way)
-            h_block = h_ref[:, pl.ds(start, half)]
-            for idx in range(2):
+            start = start_of(owner_at(way, step), way)
+            h_block = h_full[:, :, pl.ds(start, half)].reshape(dy_ref.shape[0], half)
+            for idx in (1, 2):
                 @pl.loop(0, width // TILE)
                 def _(tile):
                     cols = pl.ds(pl.multiple_of(tile * TILE, TILE), TILE)
@@ -298,38 +362,77 @@
     def across(left, right):
         return lax.dot_general(left, right, (((1,), (1,)), ((), ())), preferred_element_type=f32)
 
+    for way in range(2):
+        send(0, way, 0).start()
+    for hop in range(1, 4):
+        block_out(hop).start()
+    block_own().start()
+    for idx in range(3):
+        for way in range(2):
+            own(idx, way).start()
     for idx in range(2):
+        for hop in range(1, 4):
+            cols_copy(idx, hop, False).start()
+        cols_own(idx).start()
+    gate_acc[...] = jnp.zeros_like(gate_acc)
+    up_acc[...] = jnp.zeros_like(up_acc)
+
+    for step in range(1, 7):
+        for way in range(2):
+            landed(0, way, step - 1).wait_recv()
+            send(0, way, step).start()
+        if step == 2:
+            block_own().wait()
+            for hop in range(1, 4):
+                block_in(hop).wait_recv()
+                block_out(hop).wait_send()
+
+            @pl.loop(0, block_rows // 16)
+            def _(group):
+                at = pl.ds(pl.multiple_of(group * 16, 16), 16)
+                for seq in range(x_ref.shape[0]):
+                    total = (blocks[0, seq, at, :] + blocks[1, seq, at, :]) + (blocks[2, seq, at, :] + blocks[3, seq, at, :])
+                    mid = (x_ref[seq, at, :].astype(f32) + total.astype(bf16).astype(f32)).astype(bf16)
+                    mid_ref[seq, at, :] = mid
+                    mid = mid.astype(f32)
+                    inv_rms = lax.rsqrt(jnp.mean(mid * mid, axis=-1, keepdims=True) + NORM_EPS)
+                    h_loc[seq, at, :] = (mid * inv_rms * gain_ref[...]).astype(bf16)
+        if step == 3:
+            for hop in range(1, 4):
+                h_out(hop).start()
+            pltpu.make_async_copy(h_loc, h_slot(me_model), h_local).start()
+            slice_own().start()
+            for hop in range(1, 8):
+                slice_copy(hop, False).start()
+    for idx in (1, 2):
         for way in range(2):
             send(idx, way, 0).start()
-    for part in range(2):
-        fetch_down(part).start()
-    for idx in range(2):
-        for way in range(2):
-            own(idx, way).start()
-    for acc in accs:
-        acc[...] = jnp.zeros_like(acc)
-    for part in range(2):
-        fetch_down(part).wait()
+    pltpu.make_async_copy(h_loc, h_slot(me_model), h_local).wait()
+    for hop in range(1, 4):
+        h_in(hop).wait_recv()
+    for way in range(2):
+        landed(0, way, 6).wait_recv()
+        own(0, way).wait()
 
     @pl.loop(0, width // TILE)
     def _(tile):
         cols = pl.ds(pl.multiple_of(tile * TILE, TILE), TILE)
         d_act[:, cols] = across(dy_ref[...], w_down[cols, :]).astype(bf16)
 
-    for idx in range(2):
+    for idx in (1, 2):
         for way in range(2):
             own(idx, way).wait()
     accumulate(0)
 
     @pl.loop(1, 7)
     def _(step):
-        for idx in range(2):
+        for idx in (1, 2):
             for way in range(2):
                 landed(idx, way, step - 1).wait_recv()
                 send(idx, way, step).start()
         accumulate(step)
 
-    for idx in range(2):
+    for idx in (1, 2):
         for way in range(2):
             landed(idx, way, 6).wait_recv()
     accumulate(7)
@@ -351,35 +454,53 @@
         dh_part_ref[:, cols] = across(d_gate_ref[...], w_gate[cols, :]) + across(d_up_ref[...], w_up[cols, :])
         y_part_ref[:, cols] = jnp.dot(act_ref[...], w_down[:, cols], preferred_element_type=f32)
 
-    for idx in range(2):
+    for idx in range(3):
         for way in range(2):
             for step in range(7):
                 send(idx, way, step).wait_send()
-
-
-def ring_mlp(collective_id, gate_sh, up_sh, down_a, down_b, h_full, dy_full):
-    tokens, d_model = h_full.shape
+    slice_own().wait()
+    for hop in range(1, 8):
+        slice_copy(hop, True).wait_recv()
+        slice_copy(hop, False).wait_send()
+    for hop in range(1, 4):
+        h_out(hop).wait_send()
+    for idx in range(2):
+        cols_own(idx).wait()
+        for hop in range(1, 4):
+            cols_copy(idx, hop, True).wait_recv()
+            cols_copy(idx, hop, False).wait_send()
+
+
+def ring_mlp(collective_id, down_sh, gate_sh, up_sh, attn_part, cols_a, cols_b, x_loc, gain, dy_full):
+    tokens, d_model = dy_full.shape
     width = gate_sh.shape[1]
-    sent = 14 * gate_sh.size * 2
+    sent = 21 * gate_sh.size * 2
     dma = pltpu.SemaphoreType.DMA
     vmem = pl.BlockSpec(memory_space=pltpu.VMEM)
     hbm = pl.BlockSpec(memory_space=pl.ANY)
-    hidden = jax.ShapeDtypeStruct((tokens, width), jnp.bfloat16)
-    partial_sum = jax.ShapeDtypeStruct((tokens, d_model), jnp.float32)
+    bf16, f32 = jnp.bfloat16, jnp.float32
+    hidden = jax.ShapeDtypeStruct((tokens, width), bf16)
+    partial_sum = jax.ShapeDtypeStruct((tokens, d_model), f32)
+    sliced = jax.ShapeDtypeStruct(cols_a.shape, bf16)
+    spread = jax.ShapeDtypeStruct(cols_a.shape[:2] + (4,) + cols_a.shape[2:], bf16)
     return pl.pallas_call(
         mlp_kernel,
-        out_shape=[hidden, hidden, hidden, partial_sum, partial_sum],
-        in_specs=[hbm, hbm, hbm, hbm, vmem, vmem],
-        out_specs=[vmem] * 5,
-        scratch_shapes=[pltpu.VMEM((d_model, width), jnp.bfloat16), pltpu.VMEM((d_model, width), jnp.bfloat16),
-                        pltpu.VMEM((width, d_model), jnp.bfloat16), pltpu.VMEM((tokens, width), jnp.float32),
-                        pltpu.VMEM((tokens, width), jnp.float32), pltpu.VMEM((tokens, width), jnp.bfloat16),
-                        dma((2, 2, 7)), dma((2, 2, 7)), dma((2, 2)), dma((2,))],
+        out_shape=[hidden, hidden, hidden, partial_sum, partial_sum, jax.ShapeDtypeStruct(x_loc.shape, bf16),
+                   sliced, spread, spread],
+        in_specs=[hbm] * 6 + [vmem] * 3,
+        out_specs=[vmem] * 6 + [hbm] * 3,
+        scratch_shapes=[pltpu.VMEM((width, d_model), bf16), pltpu.VMEM((d_model, width), bf16),
+                        pltpu.VMEM((d_model, width), bf16), pltpu.VMEM((tokens, width), f32),
+                        pltpu.VMEM((tokens, width), f32), pltpu.VMEM((tokens, width), bf16),
+                        pltpu.VMEM(attn_part.shape, bf16), pltpu.VMEM(x_loc.shape, bf16),
+                        pltpu.VMEM((4,) + x_loc.shape, f32),
+                        dma((3, 2, 7)), dma((3, 2, 7)), dma((3, 2)), dma((4,)), dma((4,)), dma, dma((4,)), dma((4,)), dma,
+                        dma((8,)), dma((8,)), dma, dma((2, 4)), dma((2, 4)), dma((2,))],
         compiler_params=pltpu.CompilerParams(collective_id=collective_id, has_side_effects=True,
                                              vmem_limit_bytes=60 * 1024 * 1024),
         cost_estimate=pl.CostEstimate(flops=sent * 3000, bytes_accessed=2 * sent, transcendentals=0),
         name=f'ring_mlp_{collective_id}',
-    )(gate_sh, up_sh, down_a, down_b, h_full, dy_full)
+    )(down_sh, gate_sh, up_sh, attn_part, cols_a, cols_b, x_loc, gain, dy_full)
 
 
 def add_blocks(blocks):
@@ -425,17 +546,11 @@
         attn = jnp.einsum('bkgqt,btkd->bqkgd', prob_bf, value, preferred_element_type=f32)
         attn_flat = attn.astype(bf16).reshape(rows, seq_full, local_heads * head_dim)
         attn_part = jnp.einsum('bsh,hd->bsd', attn_flat, w_out, preferred_element_type=f32)
-        half_down = wdown_sh.shape[0] // 2
-        down_a, attn_red = ring_gather(1, [wdown_sh], [1], (), [('sum', attn_part)], spans=[(0, half_down)])
-        attn_red = add_blocks(attn_red)
-        mid_f32 = (x_f32 + attn_red.astype(bf16).astype(f32)).astype(bf16).astype(f32)
-        h_mlp_f, norm_back_mlp = jax.vjp(rms_scale, mid_f32, gain_mlp)
-        h_mlp_loc = h_mlp_f.astype(bf16)
-        down_b, h_mlp_cols, h_mlp, h_attn_cols, dy_cols = ring_gather(
-            2, [wdown_sh], [1], [h_mlp_loc], [('seq', h_mlp_loc), ('cols', h_attn_cols), ('cols', dy_cols)],
-            spans=[(half_down, half_down)])
-        gated_act, d_gate, d_up, mlp_part, dh_part = ring_mlp(
-            7, wgate_sh, wup_sh, down_a, down_b, h_mlp.reshape(tokens, -1), dy_full.reshape(tokens, -1))
+        gated_act, d_gate, d_up, mlp_part, dh_part, mid, h_mlp_cols, h_attn_cols, dy_cols = ring_mlp(
+            1, wdown_sh, wgate_sh, wup_sh, attn_part, h_attn_cols, dy_cols, x_loc, gain_mlp.reshape(1, -1),
+            dy_full.reshape(tokens, -1))
+        mid_f32 = mid.astype(f32)
+        _, norm_back_mlp = jax.vjp(rms_scale, mid_f32, gain_mlp)
         mlp_part = mlp_part.reshape(rows, seq_full, -1)
         dh_part = dh_part.reshape(rows, seq_full, -1)
         act_all, dh_mlp, mlp_red, h_mlp_cols = ring_gather(

time: 814 us -> 792 us (0.973)
  Pallas kernels: 734 us -> 714 us
    pallas_call x7 -> x5, Pallas kernels: 561 us -> 447 us  [ring_gather(): pl.pallas_call(functools.partial(ring_kernel, tuple(dims), tuple(spans),...]
    pallas_call x1, Pallas kernels: 173 us -> 268 us  [ring_mlp(): pl.pallas_call(mlp_kernel, out_shape=[hidden, hidden, hidden, partial_sum...]
where the time goes in v5:
time: 792 us; the launch traced here: 791 us
  Pallas kernels  714 us (90%)
  matrix products  51 us (6%)
  other arithmetic  14.2 us (2%)
  local copies, waits for them, and re-layouts  10.8 us (1%)
    pallas_call x5, Pallas kernels, ring_gather(): pl.pallas_call(functools.partial(ring_kernel, tuple(dims), tuple(spans),...  447 us
    pallas_call x1, Pallas kernels, ring_mlp(): pl.pallas_call(mlp_kernel, out_shape=[hidden, hidden, hidden, partial_sum...  268 us
    dot_general x5, matrix products, pair(): lax.dot_general(left, right, (((0,), (0,)), ((), ())), preferred_element_...  29.8 us

profile of v5, /device:TPU:0, one launch (start us, length us, event | category | flops | bytes accessed | tf_op | source)
XLA Modules:
  0.0 791.2 jit_solution(4744229730997743149)
XLA Ops:
  0.6 1.1 fusion.23
  2.3 0.8 copy.46
  3.2 0.9 copy.47
  4.0 1.8 fusion.16.refs_2_.refs_4_
  5.8 96.3 %ring_gather_0.1 = (bf16[2048,1536]{1,0:T(8,128)(2,1)}, bf16[512,2048]{1,0:T(8,128)(2,1)}, bf16[8,2,32,256]{3,2,1,0:T(8,128)(2,1)}, bf16[8,2,32,256]{3,2,1,0:T(8...) custom-call(bf16[256,1536]{1,0:T(8,128)(2,1)} %refs_0_.1, bf16[512,256]{1,0:T(8,128)(2,1)} %refs_1_.1, ...), custom_call_target="tpu_custom_call" | custom-call | flops 22020096000 | bytes 14680064 | tf_op jit(solution)/shard_map/ring_gather_0/pallas_call | solution.py:229
  102.1 4.9 fusion.2
  107.0 1.1 copy-done.6
  108.6 1.1 fusion.52
  110.8 1.3 convolution_convert_fusion
  112.4 0.7 copy.101
  113.1 3.6 fusion.6.attn_part
  116.7 267.6 %ring_mlp_1.1 = (bf16[256,2048]{1,0:T(8,128)(2,1)}, bf16[256,2048]{1,0:T(8,128)(2,1)}, bf16[256,2048]{1,0:T(8,128)(2,1)}, f32[256,2048]{1,0:T(8,128)}, f32[256,2...) custom-call(bf16[2048,256]{1,0:T(8,128)(2,1)} %down_sh.1, ...), custom_call_target="tpu_custom_call" | custom-call | flops 66060288000 | bytes 44040192 | tf_op jit(solution)/shard_map/ring_mlp_1/pallas_call | solution.py:486
  384.4 1.1 fusion.26
  385.5 85.7 %ring_gather_3.1 = (bf16[2048,2048]{1,0:T(8,128)(2,1)}, f32[4,2,32,2048]{3,2,1,0:T(8,128)}, f32[4,2,32,2048]{3,2,1,0:T(8,128)}, bf16[8,2,4,32,256]{4,3,2,1,0:T(8,128)(2,1)}) custom-call(bf16[256,2048]{1,0:T(8,128)(2,1)} %get-tuple-element.44.refs_0_, f32[2,128,2048]{2,1,0:T(8,128)} %bitcast.135, f32[2,128,2048]{2,1,0:T(8,128)} %bitcast.134, ...), custom_call_target="tpu_custom_call" | custom-call | flops 22020096000 | bytes 14680064 | tf_op jit(solution)/shard_map/ring_gather_3/pallas_call | solution.py:229
  471.2 1.9 fusion.18
  473.4 1.1 fusion.20
  474.6 7.2 fusion.58
  481.8 107.6 %ring_gather_4.1 = (bf16[2048,2048]{1,0:T(8,128)(2,1)}, bf16[2048,512]{1,0:T(8,128)(2,1)}, bf16[8,2,32,256]{3,2,1,0:T(8,128)(2,1)}, bf16[2,128,2048]{2,1,0:T(8,128)(2,1)}) custom-call(bf16[256,2048]{1,0:T(8,128)(2,1)} %get-tuple-element.51.refs_0_, bf16[256,512]{1,0:T(8,128)(2,1)} %bitcast.126, bf16[2,32,2048]{2,1,0:T(8,128)(2,1)} %get-tuple-element.81.refs_2_.refs_3_, ...), custom_call_target="tpu_custom_call" | custom-call | flops 27525120000 | bytes 18350080 | tf_op jit(solution)/shard_map/ring_gather_4/pallas_call | solution.py:229
  589.4 2.7 fusion.9
  592.2 1.3 multiply_reduce_fusion
  596.0 6.0 fusion.refs_1_
  602.0 0.7 copy.83
  602.6 1.4 reshape.203.refs_0_
  604.1 7.0 fusion.56
  611.1 85.2 %ring_gather_5.1 = (bf16[2048,2048]{1,0:T(8,128)(2,1)}, f32[4,2,32,2048]{3,2,1,0:T(8,128)}, bf16[8,2,4,32,256]{4,3,2,1,0:T(8,128)(2,1)}) custom-call(bf16[256,2048]{1,0:T(8,128)(2,1)} %get-tuple-element.50.refs_0_, f32[2,128,2048]{2,1,0:T(8,128)} %fusion.refs_1_, bf16[8,2,32,256]{3,2,1,0:T(8,128)(2,1)} %get-tuple-element.53.refs_2_), custom_call_target="tpu_custom_call" | custom-call | flops 22020096000 | bytes 14680064 | tf_op jit(solution)/shard_map/ring_gather_5/pallas_call | solution.py:229
  696.4 2.6 fusion.17
  699.7 1.9 fusion.22
  701.6 2.8 fusion.55
  704.4 7.0 fusion.57
  711.4 71.7 %ring_gather_6.1 = (bf16[2048,1536]{1,0:T(8,128)(2,1)}, f32[8,4,16,256]{3,2,1,0:T(8,128)}, f32[4,16,256]{2,1,0:T(8,128)}) custom-call(bf16[256,1536]{1,0:T(8,128)(2,1)} %reshape.203.refs_0_, f32[16,256]{1,0:T(8,128)} %reshape.193.refs_1_), custom_call_target="tpu_custom_call" | custom-call | flops 16515072000 | bytes 11010048 | tf_op jit(solution)/shard_map/ring_gather_6/pallas_call | solution.py:229
  783.1 1.1 reduce_sum.105
  785.5 5.7 fusion.54
  (58 shorter events, 7.1 us)
Async XLA Ops:
  1.7 0.6 copy-start.12
  2.3 99.8 %copy-start.10 = (f32[2,32]{1,0:T(2,128)}, f32[2,32]{1,0:T(2,128)S(1)}, u32[]{:S(2)}) copy-start(f32[2,32]{1,0:T(2,128)S(1)} %fusion.43) | copy-start | bytes 772
  107.0 1.1 copy-start.6
  385.5 85.8 %copy-start.3 = (bf16[2,32,2048]{2,1,0:T(8,128)(2,1)S(1)}, bf16[2,32,2048]{2,1,0:T(8,128)(2,1)}, u32[]{:S(2)}) copy-start(bf16[2,32,2048]{2,1,0:T(8,128)(2,1)} %get-tuple-element.43) | copy-start | bytes 786436
  385.5 85.8 %copy-start.9 = (f32[2048]{0:T(1024)S(1)}, f32[2048]{0:T(1024)}, u32[]{:S(2)}) copy-start(f32[2048]{0:T(1024)} %param.14) | copy-start | bytes 24580
  471.2 2.2 copy-start.5
  471.2 2.2 copy-start.7
  473.2 1.4 copy-start.14
  602.0 2.1 copy-start
  611.1 85.3 %copy-start.1 = (bf16[2,32,2048]{2,1,0:T(8,128)(2,1)S(1)}, bf16[2,32,2048]{2,1,0:T(8,128)(2,1)}, u32[]{:S(2)}) copy-start(bf16[2,32,2048]{2,1,0:T(8,128)(2,1)} %x_ref.1) | copy-start | bytes 786436
  611.1 85.3 %copy-start.8 = (f32[2048]{0:T(1024)S(1)}, f32[2048]{0:T(1024)}, u32[]{:S(2)}) copy-start(f32[2048]{0:T(1024)} %param.13) | copy-start | bytes 24580
  611.1 85.3 %copy-start.11 = (f32[2,32]{1,0:T(2,128)S(1)}, f32[2,32]{1,0:T(2,128)}, u32[]{:S(2)}) copy-start(f32[2,32]{1,0:T(2,128)} %copy-done.10) | copy-start | bytes 772
  696.4 3.3 copy-start.13
  696.4 5.2 copy-start.4
  711.4 74.0 %copy-start.2 = (bf16[8,2,4,32,256]{4,3,2,1,0:T(8,128)(2,1)S(1)}, bf16[8,2,4,32,256]{4,3,2,1,0:T(8,128)(2,1)}, u32[]{:S(2)}) copy-start(bf16[8,2,4,32,256]{4,3,2,1,0:T(8,128)(2,1)} %get-tuple-element.56) | copy-start | bytes 3145732

commit v6 on v5

--- a/solution.py
+++ b/solution.py
@@ -21,13 +21,6 @@
     first = tensor[..., :half]
     second = tensor[..., half:]
     return jnp.concatenate([first * cos_t - second * sin_t, second * cos_t + first * sin_t], axis=-1)
-
-
-def rotate_back(cotangent, cos_t, sin_t):
-    half = cotangent.shape[-1] // 2
-    first = cotangent[..., :half]
-    second = cotangent[..., half:]
-    return jnp.concatenate([first * cos_t + second * sin_t, second * cos_t - first * sin_t], axis=-1)
 
 
 def ring_place(index):
@@ -503,8 +496,312 @@
     )(down_sh, gate_sh, up_sh, attn_part, cols_a, cols_b, x_loc, gain, dy_full)
 
 
-def add_blocks(blocks):
-    return (blocks[0] + blocks[1]) + (blocks[2] + blocks[3])
+def back_kernel(act, attn, d_gate, d_up, dh_part, y_part, h_cols, w_out_in, w_qkv_in, mid_ref, x_ref, dy_ref, gain_mlp, gain_attn,
+                query, key, value, prob, cos_ref, sin_ref,
+                act_all, attn_all, gate_all, up_all, qkv_all, gains_all, mix, mid_cols, mid_spread, h_spread, y_ref, dx_ref,
+                w_out, w_qkv, d_mid, d_full, d_attn, d_qkv, dh_attn, gains, row_sum, dh_blocks, y_blocks, attn_blocks,
+                send_sem, recv_sem, local_sem, block_send, block_recv, block_local, mid_send, mid_recv, mid_local,
+                slice_send, slice_recv, slice_local, cols_send, cols_recv, cols_local, mix_send, mix_recv, mix_local, fetch_sem):
+    f32, bf16 = jnp.float32, jnp.bfloat16
+    me = lax.axis_index('fsdp')
+    me_model = lax.axis_index('model')
+    place = ring_place(me)
+    targets = (ring_device((place + 1) % 8), ring_device((place + 7) % 8))
+    barrier = pltpu.get_barrier_semaphore()
+    for hop in range(1, 8):
+        pl.semaphore_signal(barrier, inc=1, device_id={'fsdp': (me + hop) % 8}, device_id_type=MESH)
+    for hop in range(1, 4):
+        pl.semaphore_signal(barrier, inc=1, device_id={'model': (me_model + hop) % 4}, device_id_type=MESH)
+    pl.semaphore_wait(barrier, 10)
+    sources = (act, attn, d_gate, d_up, d_qkv)
+    gathered = (act_all, attn_all, gate_all, up_all, qkv_all)
+    seqs, block_rows, d_model = x_ref.shape
+    seq_len = 4 * block_rows
+    slice_width = mid_cols.shape[3]
+    head_dim = query.shape[2]
+    heads = query.shape[0] // seqs
+
+    def piece(idx, owner, way):
+        if idx == 5:
+            return gains_all.at[owner, pl.ds(2 * way, 2)]
+        rows = sources[idx].shape[0]
+        return gathered[idx].at[pl.ds(pl.multiple_of(owner * rows + way * (rows // 2), rows // 2), rows // 2), :]
+
+    def source(idx, way):
+        if idx == 5:
+            return mix.at[pl.ds(2 * way, 2)]
+        half = sources[idx].shape[0] // 2
+        return sources[idx].at[pl.ds(way * half, half), :]
+
+    def owner_at(way, step):
+        return ring_device((place + (8 - step if way == 0 else step)) % 8)
+
+    def send(idx, way, step):
+        dst = piece(idx, owner_at(way, step), way)
+        return pltpu.make_async_remote_copy(
+            src_ref=source(idx, way) if step == 0 else dst, dst_ref=dst, send_sem=send_sem.at[idx, way, step],
+            recv_sem=recv_sem.at[idx, way, step], device_id={'fsdp': targets[way]}, device_id_type=MESH)
+
+    def landed(idx, way, step):
+        dst = piece(idx, owner_at(way, step + 1), way)
+        return pltpu.make_async_remote_copy(
+            src_ref=dst, dst_ref=dst, send_sem=send_sem.at[idx, way, step], recv_sem=recv_sem.at[idx, way, step],
+            device_id={'fsdp': targets[way]}, device_id_type=MESH)
+
+    def own(idx, way):
+        return pltpu.make_async_copy(source(idx, way), piece(idx, me, way), local_sem.at[idx, way])
+
+    def start_ring(ids):
+        for idx in ids:
+            for way in range(2):
+                send(idx, way, 0).start()
+
+    def forward(ids, step):
+        for idx in ids:
+            for way in range(2):
+                landed(idx, way, step - 1).wait_recv()
+                send(idx, way, step).start()
+
+    def to_member(src, dst, send_one, recv_one, hop):
+        return pltpu.make_async_remote_copy(
+            src_ref=src, dst_ref=dst, send_sem=send_one, recv_sem=recv_one,
+            device_id={'model': (me_model + hop) % 4}, device_id_type=MESH)
+
+    block_src, block_dst = (dh_part, y_part, dh_attn), (dh_blocks, y_blocks, attn_blocks)
+
+    def block_of(idx, member):
+        return block_src[idx].at[:, pl.ds(pl.multiple_of(member * block_rows, block_rows), block_rows), :]
+
+    def block_copy(idx, hop, incoming):
+        slot = block_dst[idx].at[(me_model + 4 - hop) % 4 if incoming else me_model]
+        src = slot if incoming else block_of(idx, (me_model + hop) % 4)
+        return to_member(src, slot, block_send.at[idx, hop], block_recv.at[idx, hop], hop)
+
+    def block_own(idx):
+        return pltpu.make_async_copy(block_of(idx, me_model), block_dst[idx].at[me_model], block_local.at[idx])
+
+    def blocks_start(idx):
+        for hop in range(1, 4):
+            block_copy(idx, hop, False).start()
+        block_own(idx).start()
+
+    def blocks_wait(idx):
+        block_own(idx).wait()
+        for hop in range(1, 4):
+            block_copy(idx, hop, True).wait_recv()
+            block_copy(idx, hop, False).wait_send()
+
+    def mid_slot(member):
+        return d_full.at[:, pl.ds(pl.multiple_of(member * block_rows, block_rows), block_rows), :]
+
+    def mid_copy(hop, incoming):
+        slot = mid_slot((me_model + 4 - hop) % 4 if incoming else me_model)
+        return to_member(slot if incoming else d_mid, slot, mid_send.at[hop], mid_recv.at[hop], hop)
+
+    def mid_own():
+        return pltpu.make_async_copy(d_mid, mid_slot(me_model), mid_local)
+
+    def columns(peer):
+        return d_mid.at[:, :, pl.ds(pl.multiple_of(peer * slice_width, slice_width), slice_width)]
+
+    def slice_copy(hop, incoming):
+        peer = (me + hop) % 8
+        slot = mid_cols.at[(me + 8 - hop) % 8 if incoming else me]
+        return pltpu.make_async_remote_copy(
+            src_ref=slot if incoming else columns(peer), dst_ref=slot, send_sem=slice_send.at[hop],
+            recv_sem=slice_recv.at[hop], device_id={'fsdp': peer}, device_id_type=MESH)
+
+    def slice_own():
+        return pltpu.make_async_copy(columns(me), mid_cols.at[me], slice_local)
+
+    cols_in, cols_all = (h_cols, mid_cols), (h_spread, mid_spread)
+
+    def cols_copy(idx, hop, incoming):
+        slot = cols_all[idx].at[:, :, (me_model + 4 - hop) % 4 if incoming else me_model]
+        return to_member(slot if incoming else cols_in[idx], slot, cols_send.at[idx, hop], cols_recv.at[idx, hop], hop)
+
+    def cols_own(idx):
+        return pltpu.make_async_copy(cols_in[idx], cols_all[idx].at[:, :, me_model], cols_local.at[idx])
+
+    def mix_copy(hop, incoming):
+        slot = mix.at[(me_model + 4 - hop) % 4 if incoming else me_model]
+        return to_member(slot if incoming else gains, slot, mix_send.at[hop], mix_recv.at[hop], hop)
+
+    def mix_own():
+        return pltpu.make_async_copy(gains, mix.at[me_model], mix_local)
+
+    def fetch(idx):
+        return pltpu.make_async_copy((w_out_in, w_qkv_in)[idx], (w_out, w_qkv)[idx], fetch_sem.at[idx])
+
+    def across(left, right):
+        return lax.dot_general(left, right, (((1,), (1,)), ((), ())), preferred_element_type=f32)
+
+    def along(left, right):
+        return lax.dot_general(left, right, (((0,), (0,)), ((), ())), preferred_element_type=f32)
+
+    def add_up(parts, seq, at):
+        return ((parts[0, seq, at, :] + parts[1, seq, at, :]) + (parts[2, seq, at, :] + parts[3, seq, at, :])).astype(bf16).astype(f32)
+
+    def norm_back(parts, saved, gain, base, result, first_row):
+        row_sum[...] = jnp.zeros_like(row_sum)
+
+        @pl.loop(0, block_rows // 16)
+        def _(group):
+            at = pl.ds(pl.multiple_of(group * 16, 16), 16)
+            for seq in range(seqs):
+                d_h = add_up(parts, seq, at)
+                val = saved[seq, at, :].astype(f32)
+                inv_rms = lax.rsqrt(jnp.mean(val * val, axis=-1, keepdims=True) + NORM_EPS)
+                scaled = d_h * gain[...]
+                slope = jnp.sum(scaled * val, axis=-1, keepdims=True) * (inv_rms * inv_rms * inv_rms) * (1.0 / d_model)
+                result[seq, at, :] = (base[seq, at, :].astype(f32) + (scaled * inv_rms - val * slope)).astype(bf16)
+                per_row = d_h * val * inv_rms
+                row_sum[...] += per_row[:8] + per_row[8:]
+        total = jnp.sum(row_sum[...], axis=0, keepdims=True)
+        width = gains.shape[1]
+        for row in range(d_model // width):
+            gains[first_row + row:first_row + row + 1, :] = total[:, row * width:(row + 1) * width]
+
+    def attention_back():
+        d_attn[...] = across(d_full[...].reshape(seqs * seq_len, d_model), w_out[...]).astype(bf16)
+        for seq in range(seqs):
+            for head in range(heads):
+                idx = seq * heads + head
+                rows = slice(seq * seq_len, (seq + 1) * seq_len)
+                d_out = d_attn[rows, head * head_dim:(head + 1) * head_dim]
+                weight = prob[idx]
+                d_prob = across(d_out, value[idx])
+                row_dot = jnp.sum(d_prob * weight, axis=-1, keepdims=True)
+                d_scores = (weight * (d_prob - row_dot) * head_dim ** -0.5).astype(bf16)
+                d_query = jnp.dot(d_scores, key[idx], preferred_element_type=f32)
+                d_key = along(d_scores, query[idx])
+                d_value = along(weight.astype(bf16), d_out)
+                for place_in, part in enumerate((d_query, d_key)):
+                    turned = part * cos_ref[...] + pltpu.roll(part, head_dim // 2, 1) * sin_ref[...]
+                    start = (3 * head + place_in) * head_dim
+                    d_qkv[rows, start:start + head_dim] = turned.astype(bf16)
+                d_qkv[rows, (3 * head + 2) * head_dim:(3 * head + 3) * head_dim] = d_value.astype(bf16)
+
+        @pl.loop(0, d_model // TILE)
+        def _(tile):
+            cols = pl.ds(pl.multiple_of(tile * TILE, TILE), TILE)
+            dh_attn[:, :, cols] = across(d_qkv[...], w_qkv[cols, :]).reshape(seqs, seq_len, TILE)
+
+    start_ring((0, 1))
+    blocks_start(0)
+    blocks_start(1)
+    for idx in range(4):
+        for way in range(2):
+            own(idx, way).start()
+    for idx in range(2):
+        fetch(idx).start()
+    for hop in range(1, 4):
+        cols_copy(0, hop, False).start()
+    cols_own(0).start()
+    for step in range(1, 7):
+        forward((0, 1), step)
+        if step == 2:
+            blocks_wait(0)
+            norm_back(dh_blocks, mid_ref, gain_mlp, dy_ref, d_mid, 8)
+        if step == 3:
+            for hop in range(1, 4):
+                mid_copy(hop, False).start()
+            mid_own().start()
+            slice_own().start()
+            for hop in range(1, 8):
+                slice_copy(hop, False).start()
+        if step == 5:
+            blocks_wait(1)
+
+            @pl.loop(0, block_rows // 16)
+            def _(group):
+                at = pl.ds(pl.multiple_of(group * 16, 16), 16)
+                for seq in range(seqs):
+                    y_ref[seq, at, :] = (mid_ref[seq, at, :].astype(f32) + add_up(y_blocks, seq, at)).astype(bf16)
+    start_ring((2, 3))
+    for step in range(1, 7):
+        forward((2, 3), step)
+        if step == 1:
+            mid_own().wait()
+            for hop in range(1, 4):
+                mid_copy(hop, True).wait_recv()
+                mid_copy(hop, False).wait_send()
+            for idx in range(2):
+                fetch(idx).wait()
+            attention_back()
+        if step == 2:
+            blocks_start(2)
+            slice_own().wait()
+            for hop in range(1, 8):
+                slice_copy(hop, True).wait_recv()
+                slice_copy(hop, False).wait_send()
+            for hop in range(1, 4):
+                cols_copy(1, hop, False).start()
+            cols_own(1).start()
+        if step == 4:
+            blocks_wait(2)
+            norm_back(attn_blocks, x_ref, gain_attn, d_mid, dx_ref, 0)
+        if step == 5:
+            mix_own().start()
+            for hop in range(1, 4):
+                mix_copy(hop, False).start()
+    start_ring((4,))
+    mix_own().wait()
+    for hop in range(1, 4):
+        mix_copy(hop, True).wait_recv()
+        mix_copy(hop, False).wait_send()
+    start_ring((5,))
+    for idx in (4, 5):
+        for way in range(2):
+            own(idx, way).start()
+    for step in range(1, 7):
+        forward((4, 5), step)
+    for idx in range(6):
+        for way in range(2):
+            landed(idx, way, 6).wait_recv()
+            own(idx, way).wait()
+            for step in range(7):
+                send(idx, way, step).wait_send()
+    for idx in range(2):
+        cols_own(idx).wait()
+        for hop in range(1, 4):
+            cols_copy(idx, hop, True).wait_recv()
+            cols_copy(idx, hop, False).wait_send()
+
+
+def ring_back(collective_id, *args):
+    act, attn, d_gate, d_up, dh_part, y_part, h_cols, w_out, w_qkv, mid = args[:10]
+    tokens = act.shape[0]
+    seqs, seq_len, d_model = dh_part.shape
+    bf16, f32 = jnp.bfloat16, jnp.float32
+    qkv_cols = w_qkv.shape[1]
+    sent = 7 * (3 * act.size + attn.size + tokens * qkv_cols) * 2
+    dma = pltpu.SemaphoreType.DMA
+    vmem = pl.BlockSpec(memory_space=pltpu.VMEM)
+    hbm = pl.BlockSpec(memory_space=pl.ANY)
+    shape = jax.ShapeDtypeStruct
+    gain_shape = (16, d_model // 8)
+    spread = shape(h_cols.shape[:2] + (4,) + h_cols.shape[2:], bf16)
+    blocks = pltpu.VMEM((4,) + mid.shape, f32)
+    return pl.pallas_call(
+        back_kernel,
+        out_shape=[shape((8 * tokens, array.shape[1]), bf16) for array in (act, attn, d_gate, d_up)]
+        + [shape((8 * tokens, qkv_cols), bf16), shape((8, 4) + gain_shape, f32), shape((4,) + gain_shape, f32),
+           shape(h_cols.shape, bf16), spread, spread, shape(mid.shape, bf16), shape(mid.shape, bf16)],
+        in_specs=[hbm] * 9 + [vmem] * (len(args) - 9),
+        out_specs=[hbm] * 10 + [vmem] * 2,
+        scratch_shapes=[pltpu.VMEM(w_out.shape, bf16), pltpu.VMEM(w_qkv.shape, bf16), pltpu.VMEM(mid.shape, bf16),
+                        pltpu.VMEM(dh_part.shape, bf16), pltpu.VMEM((tokens, w_out.shape[0]), bf16),
+                        pltpu.VMEM((tokens, qkv_cols), bf16), pltpu.VMEM(dh_part.shape, f32), pltpu.VMEM(gain_shape, f32),
+                        pltpu.VMEM((8, d_model), f32), blocks, blocks, blocks,
+                        dma((6, 2, 7)), dma((6, 2, 7)), dma((6, 2)), dma((3, 4)), dma((3, 4)), dma((3,)),
+                        dma((4,)), dma((4,)), dma, dma((8,)), dma((8,)), dma, dma((2, 4)), dma((2, 4)), dma((2,)),
+                        dma((4,)), dma((4,)), dma, dma((2,))],
+        compiler_params=pltpu.CompilerParams(collective_id=collective_id, has_side_effects=True,
+                                             vmem_limit_bytes=60 * 1024 * 1024),
+        cost_estimate=pl.CostEstimate(flops=sent * 3000, bytes_accessed=2 * sent, transcendentals=0),
+        name=f'ring_back_{collective_id}',
+    )(*args)
 
 
 def solution(mesh):
@@ -531,8 +828,7 @@
         sin_k = rope_sin[:, None, :]
 
         x_f32 = x_loc.astype(f32)
-        h_attn_f, norm_back_attn = jax.vjp(rms_scale, x_f32, gain_attn)
-        h_attn_loc = h_attn_f.astype(bf16)
+        h_attn_loc = rms_scale(x_f32, gain_attn).astype(bf16)
         w_qkv, w_out, h_attn_cols, dy_cols, h_attn, dy_full = ring_gather(
             0, [wqkv_sh, wout_sh], [0, 1], [h_attn_loc, dy_loc], [('seq', h_attn_loc), ('seq', dy_loc)])
         qkv = jnp.einsum('bsd,dc->bsc', h_attn, w_qkv, preferred_element_type=f32)
@@ -549,39 +845,15 @@
         gated_act, d_gate, d_up, mlp_part, dh_part, mid, h_mlp_cols, h_attn_cols, dy_cols = ring_mlp(
             1, wdown_sh, wgate_sh, wup_sh, attn_part, h_attn_cols, dy_cols, x_loc, gain_mlp.reshape(1, -1),
             dy_full.reshape(tokens, -1))
-        mid_f32 = mid.astype(f32)
-        _, norm_back_mlp = jax.vjp(rms_scale, mid_f32, gain_mlp)
-        mlp_part = mlp_part.reshape(rows, seq_full, -1)
-        dh_part = dh_part.reshape(rows, seq_full, -1)
-        act_all, dh_mlp, mlp_red, h_mlp_cols = ring_gather(
-            3, [gated_act], [0], (), [('sum', dh_part), ('sum', mlp_part), ('cols', h_mlp_cols)])
-        dh_mlp, mlp_red = add_blocks(dh_mlp), add_blocks(mlp_red)
-        y_loc = (mid_f32 + mlp_red.astype(bf16).astype(f32)).astype(bf16)
-        d_mid_norm, d_gain_mlp = norm_back_mlp(dh_mlp.astype(bf16).astype(f32))
-        d_mid = (dy_loc.astype(f32) + d_mid_norm).astype(bf16)
-
-        d_gate_all, attn_all, d_mid_cols, d_mid_full = ring_gather(
-            4, [d_gate, attn_flat.reshape(tokens, -1)], [0, 0], [d_mid], [('seq', d_mid)])
-        d_attn = jnp.einsum('bsd,hd->bsh', d_mid_full, w_out, preferred_element_type=f32).astype(bf16)
-        d_attn = d_attn.reshape(rows, seq_full, local_kv, group_size, head_dim)
-        d_prob = jnp.einsum('bqkgd,btkd->bkgqt', d_attn, value, preferred_element_type=f32)
-        d_value = jnp.einsum('bkgqt,bqkgd->btkd', prob_bf, d_attn, preferred_element_type=f32)
-        row_dot = jnp.sum(d_prob * attn_prob, axis=-1, keepdims=True)
-        d_scores = (attn_prob * (d_prob - row_dot) * scale).astype(bf16)
-        d_query = jnp.einsum('bkgqt,btkd->bqkgd', d_scores, key_rot, preferred_element_type=f32)
-        d_key = jnp.einsum('bkgqt,bqkgd->btkd', d_scores, query, preferred_element_type=f32)
-        d_qkv = jnp.concatenate([rotate_back(d_query, cos_q, sin_q),
-                                 rotate_back(d_key, cos_k, sin_k)[:, :, :, None],
-                                 d_value[:, :, :, None]], axis=3)
-        d_qkv = d_qkv.astype(bf16).reshape(rows, seq_full, -1)
-        dh_attn_part = jnp.einsum('bsc,dc->bsd', d_qkv, w_qkv, preferred_element_type=f32)
-        d_up_all, dh_attn, d_mid_cols = ring_gather(
-            5, [d_up], [0], (), [('sum', dh_attn_part), ('cols', d_mid_cols)])
-        dh_attn = add_blocks(dh_attn)
-        d_x_norm, d_gain_attn = norm_back_attn(dh_attn.astype(bf16).astype(f32))
-        dx_loc = (d_mid.astype(f32) + d_x_norm).astype(bf16)
-        gains = jnp.stack([d_gain_attn, d_gain_mlp]).reshape(16, -1)
-        d_qkv_all, gains_all, _ = ring_gather(6, [d_qkv.reshape(tokens, -1)], [0], sums=[gains])
+        def by_head(heads):
+            return heads.reshape(rows, seq_full, local_heads, head_dim).transpose(0, 2, 1, 3).reshape(-1, seq_full, head_dim)
+
+        (act_all, attn_all, d_gate_all, d_up_all, d_qkv_all, gains_all, _, _, d_mid_cols, h_mlp_cols, y_loc, dx_loc) = ring_back(
+            2, gated_act, attn_flat.reshape(tokens, -1), d_gate, d_up, dh_part.reshape(rows, seq_full, -1),
+            mlp_part.reshape(rows, seq_full, -1), h_mlp_cols, w_out, w_qkv, mid, x_loc, dy_loc, gain_mlp.reshape(1, -1),
+            gain_attn.reshape(1, -1), by_head(query), by_head(key_rot), by_head(value),
+            attn_prob.reshape(-1, seq_full, seq_full), jnp.concatenate([rope_cos, rope_cos], axis=1),
+            jnp.concatenate([rope_sin, -rope_sin], axis=1))
         gain_grads = jnp.sum(gains_all, axis=(0, 1)).reshape(2, -1)
         h_attn_cols, dy_cols, h_mlp_cols, d_mid_cols = [
             cols.reshape(8 * tokens, -1) for cols in (h_attn_cols, dy_cols, h_mlp_cols, d_mid_cols)]

time: 792 us -> 747 us (0.943)
  matrix products: 51 us -> 27.8 us
  Pallas kernels: 714 us -> 703 us
    pallas_call x5 -> x1, Pallas kernels: 447 us -> 96.3 us  [ring_gather(): pl.pallas_call(functools.partial(ring_kernel, tuple(dims), tuple(spans),...]
    pallas_call x0 -> x1, Pallas kernels: none -> 340 us  [ring_back(): pl.pallas_call(back_kernel, out_shape=[shape((8 * tokens, array.shape[1])...]
    dot_general x5, matrix products: 29.8 us -> 18.7 us  [pair(): lax.dot_general(left, right, (((0,), (0,)), ((), ())), preferred_element_...]
    dot_general x6 -> x0, matrix products: 10.9 us -> none  [the longest x1 5.95 us: device_fn(): jnp.einsum('bsc,dc->bsd', d_qkv, w_qkv, preferred_element_type=f32)]
where the time goes in v6:
time: 747 us; the launch traced here: 746 us
  Pallas kernels  703 us (94%)
  matrix products  27.8 us (4%)
  local copies, waits for them, and re-layouts  7.97 us (1%)
    pallas_call x1, Pallas kernels, ring_back(): pl.pallas_call(back_kernel, out_shape=[shape((8 * tokens, array.shape[1])...  340 us
    pallas_call x1, Pallas kernels, ring_mlp(): pl.pallas_call(mlp_kernel, out_shape=[hidden, hidden, hidden, partial_sum...  268 us
    pallas_call x1, Pallas kernels, ring_gather(): pl.pallas_call(functools.partial(ring_kernel, tuple(dims), tuple(spans),...  96.3 us
    dot_general x5, matrix products, pair(): lax.dot_general(left, right, (((0,), (0,)), ((), ())), preferred_element_...  18.7 us

profile of v6, /device:TPU:0, one launch (start us, length us, event | category | flops | bytes accessed | tf_op | source)
XLA Modules:
  0.0 746.4 jit_solution(11744650043966834696)
XLA Ops:
  0.6 1.1 fusion.6
  1.8 0.8 neg.3
  2.6 0.9 copy.58
  3.5 0.9 copy.59
  4.3 0.8 pad_maximum_fusion.2
  5.1 1.8 fusion.8.refs_2_.refs_4_
  6.9 96.3 %ring_gather_0.1 = (bf16[2048,1536]{1,0:T(8,128)(2,1)}, bf16[512,2048]{1,0:T(8,128)(2,1)}, bf16[8,2,32,256]{3,2,1,0:T(8,128)(2,1)}, bf16[8,2,32,256]{3,2,1,0:T(8...) custom-call(bf16[256,1536]{1,0:T(8,128)(2,1)} %refs_0_.1, bf16[512,256]{1,0:T(8,128)(2,1)} %refs_1_.1, ...), custom_call_target="tpu_custom_call" | custom-call | flops 22020096000 | bytes 14680064 | tf_op jit(solution)/shard_map/ring_gather_0/pallas_call | solution.py:222
  103.1 4.9 fusion
  108.1 0.9 copy.67
  109.0 0.2 copy.76
  109.2 0.3 subtract_convert_fusion.1
  109.5 0.2 copy.78
  109.7 0.2 copy.77
  110.1 0.3 pad_maximum_fusion
  110.4 0.3 fusion.18
  110.9 0.2 convolution_convert_fusion
  111.1 1.0 copy.68
  112.1 0.2 copy.66
  112.3 0.7 copy.90
  113.1 3.6 fusion.2.attn_part
  116.7 267.5 %ring_mlp_1.1 = (bf16[256,2048]{1,0:T(8,128)(2,1)}, bf16[256,2048]{1,0:T(8,128)(2,1)}, bf16[256,2048]{1,0:T(8,128)(2,1)}, f32[256,2048]{1,0:T(8,128)}, f32[256,2...) custom-call(bf16[2048,256]{1,0:T(8,128)(2,1)} %down_sh.1, ...), custom_call_target="tpu_custom_call" | custom-call | flops 66060288000 | bytes 44040192 | tf_op jit(solution)/shard_map/ring_mlp_1/pallas_call | solution.py:479
  384.3 339.6 %ring_back_2.1 = (bf16[2048,2048]{1,0:T(8,128)(2,1)}, bf16[2048,512]{1,0:T(8,128)(2,1)}, bf16[2048,2048]{1,0:T(8,128)(2,1)}, bf16[2048,2048]{1,0:T(8,128)(2,1)},...) custom-call(bf16[256,2048]{1,0:T(8,128)(2,1)} %get-tuple-element.40., ...), custom_call_target="tpu_custom_call" | custom-call | flops 88080384000 | bytes 58720256 | tf_op jit(solution)/shard_map/ring_back_2/pallas_call | solution.py:786
  723.9 1.1 reduce_sum.29
  725.0 0.6 copy.82
  725.6 0.6 copy.81
  726.2 5.9 fusion.19
  732.1 1.5 fusion.20
  733.7 4.0 fusion.23
  737.6 3.7 fusion.22
  741.3 3.7 fusion.21
  745.0 0.7 copy.93
  745.7 0.7 copy.94
  (40 shorter events, 0.6 us)
Async XLA Ops:
  110.4 1.8 copy-start.4
  110.4 1.7 copy-start.5
  384.2 341.9 %copy-start.1 = (bf16[8,2,4,32,256]{4,3,2,1,0:T(8,128)(2,1)S(1)}, bf16[8,2,4,32,256]{4,3,2,1,0:T(8,128)(2,1)}, u32[]{:S(2)}) copy-start(bf16[8,2,4,32,256]{4,3,2,1,0:T(8,128)(2,1)} %get-tuple-element.50) | copy-start | bytes 3145732
  726.2 5.9 copy-start.2
  726.2 5.9 copy-start.3
  726.2 7.5 %copy-start.8 = (bf16[8,2,4,32,256]{4,3,2,1,0:T(8,128)(2,1)S(1)}, bf16[8,2,4,32,256]{4,3,2,1,0:T(8,128)(2,1)}, u32[]{:S(2)}) copy-start(bf16[8,2,4,32,256]{4,3,2,1,0:T(8,128)(2,1)} %get-tuple-element.58) | copy-start | bytes 3145732
  726.2 7.5 copy-start.9
  726.2 11.4 %slice-start.2 = ((s8[8388608]{0:T(1024)(128)(4,1)}), s8[4194304]{0:T(1024)(128)(4,1)S(1)}, s32[]{:S(2)}) async-start(s8[8388608]{0:T(1024)(128)(4,1)} %bitcast.77), calls=%async_computation.2 | async-start | bytes 8388608
  732.1 5.5 slice-start.3
  732.1 9.2 %slice-start = ((s8[8388608]{0:T(1024)(128)(4,1)}), s8[4194304]{0:T(1024)(128)(4,1)S(1)}, s32[]{:S(2)}) async-start(s8[8388608]{0:T(1024)(128)(4,1)} %bitcast.75), calls=%async_computation | async-start | bytes 8388608
  733.7 4.0 copy-start
  733.7 7.7 %slice-start.1 = ((s8[8388608]{0:T(1024)(128)(4,1)}), s8[4194304]{0:T(1024)(128)(4,1)S(1)}, s32[]{:S(2)}) async-start(s8[8388608]{0:T(1024)(128)(4,1)} %bitcast.75), calls=%async_computation.1 | async-start | bytes 8388608
  741.3 3.7 copy-start.7
  741.3 4.4 copy-start.6

commit v7 on v6

v7 whole, which is shorter than its diff:
```python
import functools

import jax
import jax.numpy as jnp
from jax import lax
from jax.experimental import pallas as pl
from jax.experimental.pallas import tpu as pltpu
from jax.sharding import PartitionSpec as P

NORM_EPS = 1e-5
MESH = pl.DeviceIdType.MESH


def ring_place(index):
    z, y = index // 2, index % 2
    return z + y * (7 - 2 * z)


def ring_device(place):
    y = place // 4
    return 2 * (place + y * (7 - 2 * place)) + y


TILE = 512


def front_kernel(qkv_sh, out_sh, down_sh, gate_sh, up_sh, x_ref, dy_in, gain_attn, gain_mlp, cos_ref, sin_ref,
                 w_qkv_all, w_out_all, attn_cols, dy_cols, h_cols, attn_spread, dy_spread,
                 query, key, value, prob, attn_flat, act_ref, d_gate_ref, d_up_ref, y_part_ref, dh_part_ref, mid_ref,
                 w_qkv, w_out, w_down, w_gate, w_up, qkv, attn_part, gate_acc, up_acc, d_act, ha_full, dy_full, h_full,
                 ha_loc, h_loc, blocks,
                 send_sem, recv_sem, local_sem, block_send, block_recv, block_local, seq_send, seq_recv, seq_local,
                 slice_send, slice_recv, slice_local, cols_send, cols_recv, cols_local, fetch_sem):
    f32, bf16 = jnp.float32, jnp.bfloat16
    me = lax.axis_index('fsdp')
    me_model = lax.axis_index('model')
    place = ring_place(me)
    targets = (ring_device((place + 1) % 8), ring_device((place + 7) % 8))
    barrier = pltpu.get_barrier_semaphore()
    for hop in range(1, 8):
        pl.semaphore_signal(barrier, inc=1, device_id={'fsdp': (me + hop) % 8}, device_id_type=MESH)
    for hop in range(1, 4):
        pl.semaphore_signal(barrier, inc=1, device_id={'model': (me_model + hop) % 4}, device_id_type=MESH)
    pl.semaphore_wait(barrier, 10)
    shards, weights = (qkv_sh, out_sh, down_sh, gate_sh, up_sh), (w_qkv_all, w_out_all, w_down, w_gate, w_up)
    accs = {3: gate_acc, 4: up_acc}
    rows, width = gate_sh.shape
    half = rows // 2
    seqs, block_rows, d_model = x_ref.shape
    seq_len = 4 * block_rows
    tokens = seqs * seq_len
    slice_width = h_cols.shape[3]
    head_dim = query.shape[2]
    heads = query.shape[0] // seqs

    def start_of(owner, way):
        return pl.multiple_of(owner * rows + way * half, half)

    def piece(idx, owner, way):
        if idx in (1, 2):
            tall = shards[idx].shape[0] // 2
            return weights[idx].at[pl.ds(way * tall, tall), pl.ds(pl.multiple_of(owner * rows, rows), rows)]
        return weights[idx].at[pl.ds(start_of(owner, way), half), :]

    def source(idx, way):
        size = shards[idx].shape[0] // 2
        return shards[idx].at[pl.ds(way * size, size), :]

    def owner_at(way, step):
        return ring_device((place + (8 - step if way == 0 else step)) % 8)

    def send(idx, way, step):
        dst = piece(idx, owner_at(way, step), way)
        return pltpu.make_async_remote_copy(
            src_ref=source(idx, way) if isinstance(step, int) and step == 0 else dst, dst_ref=dst,
            send_sem=send_sem.at[idx, way, step], recv_sem=recv_sem.at[idx, way, step],
            device_id={'fsdp': targets[way]}, device_id_type=MESH)

    def landed(idx, way, step):
        dst = piece(idx, owner_at(way, step + 1), way)
        return pltpu.make_async_remote_copy(
            src_ref=dst, dst_ref=dst, send_sem=send_sem.at[idx, way, step], recv_sem=recv_sem.at[idx, way, step],
            device_id={'fsdp': targets[way]}, device_id_type=MESH)

    def own(idx, way):
        return pltpu.make_async_copy(source(idx, way), piece(idx, me, way), local_sem.at[idx, way])

    def start_ring(ids):
        for idx in ids:
            for way in range(2):
                send(idx, way, 0).start()

    def forward(ids, step):
        for idx in ids:
            for way in range(2):
                landed(idx, way, step - 1).wait_recv()
                send(idx, way, step).start()

    def finish_ring(ids):
        for idx in ids:
            for way in range(2):
                landed(idx, way, 6).wait_recv()
                own(idx, way).wait()

    def to_member(src, dst, send_one, recv_one, hop):
        return pltpu.make_async_remote_copy(
            src_ref=src, dst_ref=dst, send_sem=send_one, recv_sem=recv_one,
            device_id={'model': (me_model + hop) % 4}, device_id_type=MESH)

    def rows_of(ref, member):
        return ref.at[:, pl.ds(pl.multiple_of(member * block_rows, block_rows), block_rows), :]

    def block_copy(hop, incoming):
        slot = blocks.at[(me_model + 4 - hop) % 4 if incoming else me_model]
        src = slot if incoming else rows_of(attn_part, (me_model + hop) % 4)
        return to_member(src, slot, block_send.at[hop], block_recv.at[hop], hop)

    def block_own():
        return pltpu.make_async_copy(rows_of(attn_part, me_model), blocks.at[me_model], block_local)

    seq_src, seq_dst = (ha_loc, dy_in, h_loc), (ha_full, dy_full, h_full)
    slice_dst, spread_dst = (attn_cols, dy_cols, h_cols), (attn_spread, dy_spread)

    def seq_copy(idx, hop, incoming):
        slot = rows_of(seq_dst[idx], (me_model + 4 - hop) % 4 if incoming else me_model)
        return to_member(slot if incoming else seq_src[idx], slot, seq_send.at[idx, hop], seq_recv.at[idx, hop], hop)

    def seq_own(idx):
        return pltpu.make_async_copy(seq_src[idx], rows_of(seq_dst[idx], me_model), seq_local.at[idx])

    def columns(idx, peer):
        return seq_src[idx].at[:, :, pl.ds(pl.multiple_of(peer * slice_width, slice_width), slice_width)]

    def slice_copy(idx, hop, incoming):
        peer = (me + hop) % 8
        slot = slice_dst[idx].at[(me + 8 - hop) % 8 if incoming else me]
        return pltpu.make_async_remote_copy(
            src_ref=slot if incoming else columns(idx, peer), dst_ref=slot, send_sem=slice_send.at[idx, hop],
            recv_sem=slice_recv.at[idx, hop], device_id={'fsdp': peer}, device_id_type=MESH)

    def slice_own(idx):
        return pltpu.make_async_copy(columns(idx, me), slice_dst[idx].at[me], slice_local.at[idx])

    def hand_out(idx):
        for hop in range(1, 4):
            seq_copy(idx, hop, False).start()
        seq_own(idx).start()
        slice_own(idx).start()
        for hop in range(1, 8):
            slice_copy(idx, hop, False).start()

    def seq_wait(idx):
        seq_own(idx).wait()
        for hop in range(1, 4):
            seq_copy(idx, hop, True).wait_recv()
            seq_copy(idx, hop, False).wait_send()

    def slice_wait(idx):
        slice_own(idx).wait()
        for hop in range(1, 8):
            slice_copy(idx, hop, True).wait_recv()
            slice_copy(idx, hop, False).wait_send()

    def cols_copy(idx, hop, incoming):
        slot = spread_dst[idx].at[:, :, (me_model + 4 - hop) % 4 if incoming else me_model]
        return to_member(slot if incoming else slice_dst[idx], slot, cols_send.at[idx, hop], cols_recv.at[idx, hop], hop)

    def cols_own(idx):
        return pltpu.make_async_copy(slice_dst[idx], spread_dst[idx].at[:, :, me_model], cols_local.at[idx])

    def fetch(idx):
        return pltpu.make_async_copy(weights[idx], (w_qkv, w_out)[idx], fetch_sem.at[idx])

    def normed(val, gain):
        return (val * lax.rsqrt(jnp.mean(val * val, axis=-1, keepdims=True) + NORM_EPS) * gain[...]).astype(bf16)

    def attention():
        @pl.loop(0, qkv.shape[1] // TILE)
        def _(tile):
            cols = pl.ds(pl.multiple_of(tile * TILE, TILE), TILE)
            qkv[:, cols] = jnp.dot(ha_full[...].reshape(tokens, d_model), w_qkv[:, cols], preferred_element_type=f32)
        causal = (lax.broadcasted_iota(jnp.int32, (seq_len, seq_len), 0)
                  >= lax.broadcasted_iota(jnp.int32, (seq_len, seq_len), 1))
        for seq in range(seqs):
            for head in range(heads):
                idx = seq * heads + head
                at = slice(seq * seq_len, (seq + 1) * seq_len)
                start = 3 * head * head_dim
                for place_in, turned_ref in enumerate((query, key)):
                    part = qkv[at, start + place_in * head_dim:start + (place_in + 1) * head_dim]
                    turned = part * cos_ref[...] - pltpu.roll(part, head_dim // 2, 1) * sin_ref[...]
                    turned_ref[idx] = turned.astype(bf16)
                value[idx] = qkv[at, start + 2 * head_dim:start + 3 * head_dim].astype(bf16)
                scores = jnp.where(causal, across(query[idx], key[idx]) * head_dim ** -0.5, -1e30)
                unnormed = jnp.exp(scores - jnp.max(scores, axis=-1, keepdims=True))
                weight = unnormed / jnp.sum(unnormed, axis=-1, keepdims=True)
                prob[idx] = weight
                mixed = jnp.dot(weight.astype(bf16), value[idx], preferred_element_type=f32)
                attn_flat[at, head * head_dim:(head + 1) * head_dim] = mixed.astype(bf16)

        @pl.loop(0, d_model // TILE)
        def _(tile):
            cols = pl.ds(pl.multiple_of(tile * TILE, TILE), TILE)
            attn_part[:, :, cols] = jnp.dot(attn_flat[...], w_out[:, cols],
                                            preferred_element_type=f32).reshape(seqs, seq_len, TILE)

    def accumulate(step):
        for way in range(2):
            start = start_of(owner_at(way, step), way)
            h_block = h_full[:, :, pl.ds(start, half)].reshape(tokens, half)
            for idx in (3, 4):
                @pl.loop(0, width // TILE)
                def _(tile):
                    cols = pl.ds(pl.multiple_of(tile * TILE, TILE), TILE)
                    accs[idx][:, cols] += jnp.dot(h_block, weights[idx][pl.ds(start, half), cols],
                                                  preferred_element_type=f32)

    def across(left, right):
        return lax.dot_general(left, right, (((1,), (1,)), ((), ())), preferred_element_type=f32)

    start_ring((0, 1))
    for idx in range(5):
        for way in range(2):
            own(idx, way).start()
    hand_out(1)

    @pl.loop(0, block_rows // 16)
    def _(group):
        at = pl.ds(pl.multiple_of(group * 16, 16), 16)
        for seq in range(seqs):
            ha_loc[seq, at, :] = normed(x_ref[seq, at, :].astype(f32), gain_attn)
    gate_acc[...] = jnp.zeros_like(gate_acc)
    up_acc[...] = jnp.zeros_like(up_acc)
    for step in range(1, 7):
        forward((0, 1), step)
        if step == 1:
            hand_out(0)
    start_ring((2,))
    finish_ring((0, 1))
    for idx in range(2):
        fetch(idx).start()
    for step in range(1, 7):
        forward((2,), step)
        if step == 1:
            seq_wait(0)
            for idx in range(2):
                fetch(idx).wait()
            attention()
        if step == 2:
            for hop in range(1, 4):
                block_copy(hop, False).start()
            block_own().start()
        if step == 4:
            block_own().wait()
            for hop in range(1, 4):
                block_copy(hop, True).wait_recv()
                block_copy(hop, False).wait_send()

            @pl.loop(0, block_rows // 16)
            def _(group):
                at = pl.ds(pl.multiple_of(group * 16, 16), 16)
                for seq in range(seqs):
                    total = (blocks[0, seq, at, :] + blocks[1, seq, at, :]) + (blocks[2, seq, at, :] + blocks[3, seq, at, :])
                    mid = (x_ref[seq, at, :].astype(f32) + total.astype(bf16).astype(f32)).astype(bf16)
                    mid_ref[seq, at, :] = mid
                    h_loc[seq, at, :] = normed(mid.astype(f32), gain_mlp)
        if step == 5:
            hand_out(2)
    start_ring((3, 4))
    seq_wait(1)
    for idx in range(2):
        slice_wait(idx)
        for hop in range(1, 4):
            cols_copy(idx, hop, False).start()
        cols_own(idx).start()
    finish_ring((2,))

    @pl.loop(0, width // TILE)
    def _(tile):
        cols = pl.ds(pl.multiple_of(tile * TILE, TILE), TILE)
        d_act[:, cols] = across(dy_full[...].reshape(tokens, d_model), w_down[cols, :]).astype(bf16)

    seq_wait(2)
    for idx in (3, 4):
        for way in range(2):
            own(idx, way).wait()
    accumulate(0)

    @pl.loop(1, 7)
    def _(step):
        forward((3, 4), step)
        accumulate(step)

    for idx in (3, 4):
        for way in range(2):
            landed(idx, way, 6).wait_recv()
    accumulate(7)

    @pl.loop(0, width // 256)
    def _(tile):
        cols = pl.ds(pl.multiple_of(tile * 256, 256), 256)
        gate, up_proj = gate_acc[:, cols], up_acc[:, cols]
        d_val = d_act[:, cols].astype(f32)
        sig_gate = jax.nn.sigmoid(gate)
        silu_gate = gate * sig_gate
        act_ref[:, cols] = (silu_gate * up_proj).astype(bf16)
        d_gate_ref[:, cols] = (d_val * up_proj * sig_gate * (1.0 + gate * (1.0 - sig_gate))).astype(bf16)
        d_up_ref[:, cols] = (d_val * silu_gate).astype(bf16)

    @pl.loop(0, width // TILE)
    def _(tile):
        cols = pl.ds(pl.multiple_of(tile * TILE, TILE), TILE)
        dh_part_ref[:, cols] = across(d_gate_ref[...], w_gate[cols, :]) + across(d_up_ref[...], w_up[cols, :])
        y_part_ref[:, cols] = jnp.dot(act_ref[...], w_down[:, cols], preferred_element_type=f32)

    for idx in range(5):
        for way in range(2):
            for step in range(7):
                send(idx, way, step).wait_send()
    slice_wait(2)
    for idx in range(2):
        cols_own(idx).wait()
        for hop in range(1, 4):
            cols_copy(idx, hop, True).wait_recv()
            cols_copy(idx, hop, False).wait_send()


def ring_front(collective_id, *args):
    qkv_sh, out_sh, down_sh, gate_sh, up_sh, x_loc, dy_loc = args[:7]
    seqs, block_rows, d_model = x_loc.shape
    seq_len, head_dim = args[9].shape
    tokens = seqs * seq_len
    width, qkv_cols, attn_cols = gate_sh.shape[1], qkv_sh.shape[1], out_sh.shape[0]
    sent = 7 * (qkv_sh.size + out_sh.size + 3 * gate_sh.size) * 2
    dma = pltpu.SemaphoreType.DMA
    vmem = pl.BlockSpec(memory_space=pltpu.VMEM)
    hbm = pl.BlockSpec(memory_space=pl.ANY)
    bf16, f32 = jnp.bfloat16, jnp.float32
    shape, buf = jax.ShapeDtypeStruct, pltpu.VMEM
    sliced = shape((8, seqs, block_rows, d_model // 8), bf16)
    spread = shape((8, seqs, 4, block_rows, d_model // 8), bf16)
    per_head = shape((seqs * attn_cols // head_dim, seq_len, head_dim), bf16)
    hidden = shape((tokens, width), bf16)
    partial_sum = shape((tokens, d_model), f32)
    whole = (seqs, seq_len, d_model)
    return pl.pallas_call(
        front_kernel,
        out_shape=[shape((d_model, qkv_cols), bf16), shape((attn_cols, d_model), bf16), sliced, sliced, sliced, spread, spread,
                   per_head, per_head, per_head, shape((per_head.shape[0], seq_len, seq_len), f32),
                   shape((tokens, attn_cols), bf16), hidden, hidden, hidden, partial_sum, partial_sum, shape(x_loc.shape, bf16)],
        in_specs=[hbm] * 5 + [vmem] * 6,
        out_specs=[hbm] * 7 + [vmem] * 11,
        scratch_shapes=[buf((d_model, qkv_cols), bf16), buf((attn_cols, d_model), bf16), buf((width, d_model), bf16),
                        buf((d_model, width), bf16), buf((d_model, width), bf16), buf((tokens, qkv_cols), f32), buf(whole, f32),
                        buf((tokens, width), f32), buf((tokens, width), f32), buf((tokens, width), bf16),
                        buf(whole, bf16), buf(whole, bf16), buf(whole, bf16), buf(x_loc.shape, bf16), buf(x_loc.shape, bf16),
                        buf((4,) + x_loc.shape, f32),
                        dma((5, 2, 7)), dma((5, 2, 7)), dma((5, 2)), dma((4,)), dma((4,)), dma, dma((3, 4)), dma((3, 4)), dma((3,)),
                        dma((3, 8)), dma((3, 8)), dma((3,)), dma((2, 4)), dma((2, 4)), dma((2,)), dma((2,))],
        compiler_params=pltpu.CompilerParams(collective_id=collective_id, has_side_effects=True,
                                             vmem_limit_bytes=63 * 1024 * 1024),
        cost_estimate=pl.CostEstimate(flops=sent * 3000, bytes_accessed=2 * sent, transcendentals=0),
        name=f'ring_front_{collective_id}',
    )(*args)


def back_kernel(act, attn, d_gate, d_up, dh_part, y_part, h_cols, w_out_in, w_qkv_in, mid_ref, x_ref, dy_ref, gain_mlp, gain_attn,
                query, key, value, prob, cos_ref, sin_ref,
                act_all, attn_all, gate_all, up_all, qkv_all, gains_all, mix, mid_cols, mid_spread, h_spread, y_ref, dx_ref,
                w_out, w_qkv, d_mid, d_full, d_attn, d_qkv, dh_attn, gains, row_sum, dh_blocks, y_blocks, attn_blocks,
                send_sem, recv_sem, local_sem, block_send, block_recv, block_local, mid_send, mid_recv, mid_local,
                slice_send, slice_recv, slice_local, cols_send, cols_recv, cols_local, mix_send, mix_recv, mix_local, fetch_sem):
    f32, bf16 = jnp.float32, jnp.bfloat16
    me = lax.axis_index('fsdp')
    me_model = lax.axis_index('model')
    place = ring_place(me)
    targets = (ring_device((place + 1) % 8), ring_device((place + 7) % 8))
    barrier = pltpu.get_barrier_semaphore()
    for hop in range(1, 8):
        pl.semaphore_signal(barrier, inc=1, device_id={'fsdp': (me + hop) % 8}, device_id_type=MESH)
    for hop in range(1, 4):
        pl.semaphore_signal(barrier, inc=1, device_id={'model': (me_model + hop) % 4}, device_id_type=MESH)
    pl.semaphore_wait(barrier, 10)
    sources = (act, attn, d_gate, d_up, d_qkv)
    gathered = (act_all, attn_all, gate_all, up_all, qkv_all)
    seqs, block_rows, d_model = x_ref.shape
    seq_len = 4 * block_rows
    slice_width = mid_cols.shape[3]
    head_dim = query.shape[2]
    heads = query.shape[0] // seqs

    def piece(idx, owner, way):
        if idx == 5:
            return gains_all.at[owner, pl.ds(2 * way, 2)]
        rows = sources[idx].shape[0]
        return gathered[idx].at[pl.ds(pl.multiple_of(owner * rows + way * (rows // 2), rows // 2), rows // 2), :]

    def source(idx, way):
        if idx == 5:
            return mix.at[pl.ds(2 * way, 2)]
        half = sources[idx].shape[0] // 2
        return sources[idx].at[pl.ds(way * half, half), :]

    def owner_at(way, step):
        return ring_device((place + (8 - step if way == 0 else step)) % 8)

    def send(idx, way, step):
        dst = piece(idx, owner_at(way, step), way)
        return pltpu.make_async_remote_copy(
            src_ref=source(idx, way) if step == 0 else dst, dst_ref=dst, send_sem=send_sem.at[idx, way, step],
            recv_sem=recv_sem.at[idx, way, step], device_id={'fsdp': targets[way]}, device_id_type=MESH)

    def landed(idx, way, step):
        dst = piece(idx, owner_at(way, step + 1), way)
        return pltpu.make_async_remote_copy(
            src_ref=dst, dst_ref=dst, send_sem=send_sem.at[idx, way, step], recv_sem=recv_sem.at[idx, way, step],
            device_id={'fsdp': targets[way]}, device_id_type=MESH)

    def own(idx, way):
        return pltpu.make_async_copy(source(idx, way), piece(idx, me, way), local_sem.at[idx, way])

    def start_ring(ids):
        for idx in ids:
            for way in range(2):
                send(idx, way, 0).start()

    def forward(ids, step):
        for idx in ids:
            for way in range(2):
                landed(idx, way, step - 1).wait_recv()
                send(idx, way, step).start()

    def to_member(src, dst, send_one, recv_one, hop):
        return pltpu.make_async_remote_copy(
            src_ref=src, dst_ref=dst, send_sem=send_one, recv_sem=recv_one,
            device_id={'model': (me_model + hop) % 4}, device_id_type=MESH)

    block_src, block_dst = (dh_part, y_part, dh_attn), (dh_blocks, y_blocks, attn_blocks)

    def block_of(idx, member):
        return block_src[idx].at[:, pl.ds(pl.multiple_of(member * block_rows, block_rows), block_rows), :]

    def block_copy(idx, hop, incoming):
        slot = block_dst[idx].at[(me_model + 4 - hop) % 4 if incoming else me_model]
        src = slot if incoming else block_of(idx, (me_model + hop) % 4)
        return to_member(src, slot, block_send.at[idx, hop], block_recv.at[idx, hop], hop)

    def block_own(idx):
        return pltpu.make_async_copy(block_of(idx, me_model), block_dst[idx].at[me_model], block_local.at[idx])

    def blocks_start(idx):
        for hop in range(1, 4):
            block_copy(idx, hop, False).start()
        block_own(idx).start()

    def blocks_wait(idx):
        block_own(idx).wait()
        for hop in range(1, 4):
            block_copy(idx, hop, True).wait_recv()
            block_copy(idx, hop, False).wait_send()

    def mid_slot(member):
        return d_full.at[:, pl.ds(pl.multiple_of(member * block_rows, block_rows), block_rows), :]

    def mid_copy(hop, incoming):
        slot = mid_slot((me_model + 4 - hop) % 4 if incoming else me_model)
        return to_member(slot if incoming else d_mid, slot, mid_send.at[hop], mid_recv.at[hop], hop)

    def mid_own():
        return pltpu.make_async_copy(d_mid, mid_slot(me_model), mid_local)

    def columns(peer):
        return d_mid.at[:, :, pl.ds(pl.multiple_of(peer * slice_width, slice_width), slice_width)]

    def slice_copy(hop, incoming):
        peer = (me + hop) % 8
        slot = mid_cols.at[(me + 8 - hop) % 8 if incoming else me]
        return pltpu.make_async_remote_copy(
            src_ref=slot if incoming else columns(peer), dst_ref=slot, send_sem=slice_send.at[hop],
            recv_sem=slice_recv.at[hop], device_id={'fsdp': peer}, device_id_type=MESH)

    def slice_own():
        return pltpu.make_async_copy(columns(me), mid_cols.at[me], slice_local)

    cols_in, cols_all = (h_cols, mid_cols), (h_spread, mid_spread)

    def cols_copy(idx, hop, incoming):
        slot = cols_all[idx].at[:, :, (me_model + 4 - hop) % 4 if incoming else me_model]
        return to_member(slot if incoming else cols_in[idx], slot, cols_send.at[idx, hop], cols_recv.at[idx, hop], hop)

    def cols_own(idx):
        return pltpu.make_async_copy(cols_in[idx], cols_all[idx].at[:, :, me_model], cols_local.at[idx])

    def mix_copy(hop, incoming):
        slot = mix.at[(me_model + 4 - hop) % 4 if incoming else me_model]
        return to_member(slot if incoming else gains, slot, mix_send.at[hop], mix_recv.at[hop], hop)

    def mix_own():
        return pltpu.make_async_copy(gains, mix.at[me_model], mix_local)

    def fetch(idx):
        return pltpu.make_async_copy((w_out_in, w_qkv_in)[idx], (w_out, w_qkv)[idx], fetch_sem.at[idx])

    def across(left, right):
        return lax.dot_general(left, right, (((1,), (1,)), ((), ())), preferred_element_type=f32)

    def along(left, right):
        return lax.dot_general(left, right, (((0,), (0,)), ((), ())), preferred_element_type=f32)

    def add_up(parts, seq, at):
        return ((parts[0, seq, at, :] + parts[1, seq, at, :]) + (parts[2, seq, at, :] + parts[3, seq, at, :])).astype(bf16).astype(f32)

    def norm_back(parts, saved, gain, base, result, first_row):
        row_sum[...] = jnp.zeros_like(row_sum)

        @pl.loop(0, block_rows // 16)
        def _(group):
            at = pl.ds(pl.multiple_of(group * 16, 16), 16)
            for seq in range(seqs):
                d_h = add_up(parts, seq, at)
                val = saved[seq, at, :].astype(f32)
                inv_rms = lax.rsqrt(jnp.mean(val * val, axis=-1, keepdims=True) + NORM_EPS)
                scaled = d_h * gain[...]
                slope = jnp.sum(scaled * val, axis=-1, keepdims=True) * (inv_rms * inv_rms * inv_rms) * (1.0 / d_model)
                result[seq, at, :] = (base[seq, at, :].astype(f32) + (scaled * inv_rms - val * slope)).astype(bf16)
                per_row = d_h * val * inv_rms
                row_sum[...] += per_row[:8] + per_row[8:]
        total = jnp.sum(row_sum[...], axis=0, keepdims=True)
        width = gains.shape[1]
        for row in range(d_model // width):
            gains[first_row + row:first_row + row + 1, :] = total[:, row * width:(row + 1) * width]

    def attention_back():
        d_attn[...] = across(d_full[...].reshape(seqs * seq_len, d_model), w_out[...]).astype(bf16)
        for seq in range(seqs):
            for head in range(heads):
                idx = seq * heads + head
                rows = slice(seq * seq_len, (seq + 1) * seq_len)
                d_out = d_attn[rows, head * head_dim:(head + 1) * head_dim]
                weight = prob[idx]
                d_prob = across(d_out, value[idx])
                row_dot = jnp.sum(d_prob * weight, axis=-1, keepdims=True)
                d_scores = (weight * (d_prob - row_dot) * head_dim ** -0.5).astype(bf16)
                d_query = jnp.dot(d_scores, key[idx], preferred_element_type=f32)
                d_key = along(d_scores, query[idx])
                d_value = along(weight.astype(bf16), d_out)
                for place_in, part in enumerate((d_query, d_key)):
                    turned = part * cos_ref[...] + pltpu.roll(part, head_dim // 2, 1) * sin_ref[...]
                    start = (3 * head + place_in) * head_dim
                    d_qkv[rows, start:start + head_dim] = turned.astype(bf16)
                d_qkv[rows, (3 * head + 2) * head_dim:(3 * head + 3) * head_dim] = d_value.astype(bf16)

        @pl.loop(0, d_model // TILE)
        def _(tile):
            cols = pl.ds(pl.multiple_of(tile * TILE, TILE), TILE)
            dh_attn[:, :, cols] = across(d_qkv[...], w_qkv[cols, :]).reshape(seqs, seq_len, TILE)

    start_ring((0, 1))
    blocks_start(0)
    blocks_start(1)
    for idx in range(4):
        for way in range(2):
            own(idx, way).start()
    for idx in range(2):
        fetch(idx).start()
    for hop in range(1, 4):
        cols_copy(0, hop, False).start()
    cols_own(0).start()
    for step in range(1, 7):
        forward((0, 1), step)
        if step == 2:
            blocks_wait(0)
            norm_back(dh_blocks, mid_ref, gain_mlp, dy_ref, d_mid, 8)
        if step == 3:
            for hop in range(1, 4):
                mid_copy(hop, False).start()
            mid_own().start()
            slice_own().start()
            for hop in range(1, 8):
                slice_copy(hop, False).start()
        if step == 5:
            blocks_wait(1)

            @pl.loop(0, block_rows // 16)
            def _(group):
                at = pl.ds(pl.multiple_of(group * 16, 16), 16)
                for seq in range(seqs):
                    y_ref[seq, at, :] = (mid_ref[seq, at, :].astype(f32) + add_up(y_blocks, seq, at)).astype(bf16)
    start_ring((2, 3))
    for step in range(1, 7):
        forward((2, 3), step)
        if step == 1:
            mid_own().wait()
            for hop in range(1, 4):
                mid_copy(hop, True).wait_recv()
                mid_copy(hop, False).wait_send()
            for idx in range(2):
                fetch(idx).wait()
            attention_back()
        if step == 2:
            blocks_start(2)
            slice_own().wait()
            for hop in range(1, 8):
                slice_copy(hop, True).wait_recv()
                slice_copy(hop, False).wait_send()
            for hop in range(1, 4):
                cols_copy(1, hop, False).start()
            cols_own(1).start()
        if step == 4:
            blocks_wait(2)
            norm_back(attn_blocks, x_ref, gain_attn, d_mid, dx_ref, 0)
        if step == 5:
            mix_own().start()
            for hop in range(1, 4):
                mix_copy(hop, False).start()
    start_ring((4,))
    mix_own().wait()
    for hop in range(1, 4):
        mix_copy(hop, True).wait_recv()
        mix_copy(hop, False).wait_send()
    start_ring((5,))
    for idx in (4, 5):
        for way in range(2):
            own(idx, way).start()
    for step in range(1, 7):
        forward((4, 5), step)
    for idx in range(6):
        for way in range(2):
            landed(idx, way, 6).wait_recv()
            own(idx, way).wait()
            for step in range(7):
                send(idx, way, step).wait_send()
    for idx in range(2):
        cols_own(idx).wait()
        for hop in range(1, 4):
            cols_copy(idx, hop, True).wait_recv()
            cols_copy(idx, hop, False).wait_send()


def ring_back(collective_id, *args):
    act, attn, d_gate, d_up, dh_part, y_part, h_cols, w_out, w_qkv, mid = args[:10]
    tokens = act.shape[0]
    seqs, seq_len, d_model = dh_part.shape
    bf16, f32 = jnp.bfloat16, jnp.float32
    qkv_cols = w_qkv.shape[1]
    sent = 7 * (3 * act.size + attn.size + tokens * qkv_cols) * 2
    dma = pltpu.SemaphoreType.DMA
    vmem = pl.BlockSpec(memory_space=pltpu.VMEM)
    hbm = pl.BlockSpec(memory_space=pl.ANY)
    shape = jax.ShapeDtypeStruct
    gain_shape = (16, d_model // 8)
    spread = shape(h_cols.shape[:2] + (4,) + h_cols.shape[2:], bf16)
    blocks = pltpu.VMEM((4,) + mid.shape, f32)
    return pl.pallas_call(
        back_kernel,
        out_shape=[shape((8 * tokens, array.shape[1]), bf16) for array in (act, attn, d_gate, d_up)]
        + [shape((8 * tokens, qkv_cols), bf16), shape((8, 4) + gain_shape, f32), shape((4,) + gain_shape, f32),
           shape(h_cols.shape, bf16), spread, spread, shape(mid.shape, bf16), shape(mid.shape, bf16)],
        in_specs=[hbm] * 9 + [vmem] * (len(args) - 9),
        out_specs=[hbm] * 10 + [vmem] * 2,
        scratch_shapes=[pltpu.VMEM(w_out.shape, bf16), pltpu.VMEM(w_qkv.shape, bf16), pltpu.VMEM(mid.shape, bf16),
                        pltpu.VMEM(dh_part.shape, bf16), pltpu.VMEM((tokens, w_out.shape[0]), bf16),
                        pltpu.VMEM((tokens, qkv_cols), bf16), pltpu.VMEM(dh_part.shape, f32), pltpu.VMEM(gain_shape, f32),
                        pltpu.VMEM((8, d_model), f32), blocks, blocks, blocks,
                        dma((6, 2, 7)), dma((6, 2, 7)), dma((6, 2)), dma((3, 4)), dma((3, 4)), dma((3,)),
                        dma((4,)), dma((4,)), dma, dma((8,)), dma((8,)), dma, dma((2, 4)), dma((2, 4)), dma((2,)),
                        dma((4,)), dma((4,)), dma, dma((2,))],
        compiler_params=pltpu.CompilerParams(collective_id=collective_id, has_side_effects=True,
                                             vmem_limit_bytes=60 * 1024 * 1024),
        cost_estimate=pl.CostEstimate(flops=sent * 3000, bytes_accessed=2 * sent, transcendentals=0),
        name=f'ring_back_{collective_id}',
    )(*args)


def solution(mesh):
    act_spec = P('fsdp', 'model', None)
    rows_spec = P('fsdp', 'model')
    cols_spec = P('model', 'fsdp')
    f32 = jnp.float32

    def device_fn(x_loc, dy_loc, gain_attn, gain_mlp, wqkv_sh, wout_sh, wgate_sh, wup_sh, wdown_sh, rope_cos, rope_sin):
        tokens = x_loc.shape[0] * rope_cos.shape[0]
        cos_two = jnp.concatenate([rope_cos, rope_cos], axis=1)
        sin_two = jnp.concatenate([rope_sin, -rope_sin], axis=1)
        gain_a, gain_m = gain_attn.reshape(1, -1), gain_mlp.reshape(1, -1)
        (w_qkv, w_out, _, _, h_mlp_cols, h_attn_cols, dy_cols, query, key_rot, value, prob, attn_flat, gated_act, d_gate, d_up,
         mlp_part, dh_part, mid) = ring_front(
            1, wqkv_sh, wout_sh, wdown_sh, wgate_sh, wup_sh, x_loc, dy_loc, gain_a, gain_m, cos_two, sin_two)
        whole = (x_loc.shape[0], rope_cos.shape[0], x_loc.shape[2])
        (act_all, attn_all, d_gate_all, d_up_all, d_qkv_all, gains_all, _, _, d_mid_cols, h_mlp_cols, y_loc, dx_loc) = ring_back(
            2, gated_act, attn_flat, d_gate, d_up, dh_part.reshape(whole), mlp_part.reshape(whole), h_mlp_cols, w_out, w_qkv,
            mid, x_loc, dy_loc, gain_m, gain_a, query, key_rot, value, prob, cos_two, sin_two)
        gain_grads = jnp.sum(gains_all, axis=(0, 1)).reshape(2, -1)
        h_attn_cols, dy_cols, h_mlp_cols, d_mid_cols = [
            cols.reshape(8 * tokens, -1) for cols in (h_attn_cols, dy_cols, h_mlp_cols, d_mid_cols)]

        def pair(left, right):
            return lax.dot_general(left, right, (((0,), (0,)), ((), ())), preferred_element_type=f32)

        return (y_loc, dx_loc, gain_grads[0], gain_grads[1],
                pair(h_attn_cols, d_qkv_all), pair(attn_all, d_mid_cols),
                pair(h_mlp_cols, d_gate_all), pair(h_mlp_cols, d_up_all), pair(act_all, dy_cols))

    in_specs = (act_spec, act_spec, P(), P(), rows_spec, cols_spec, rows_spec, rows_spec, cols_spec, P(), P())
    out_specs = (act_spec, act_spec, P(), P(), rows_spec, cols_spec, rows_spec, rows_spec, cols_spec)
    return jax.shard_map(device_fn, mesh=mesh, in_specs=in_specs, out_specs=out_specs, check_vma=False)
```

time: 747 us -> 719 us (0.963)
  Pallas kernels: 703 us -> 692 us
  matrix products: 27.8 us -> 18.7 us
    dot_general x4 -> x0, matrix products: 9.07 us -> none  [the longest x1 4.89 us: device_fn(): qkv = jnp.einsum('bsd,dc->bsc', h_attn, w_qkv, preferred_element_type=f32)]
    pallas_call x2 -> x1, Pallas kernels: 364 us -> 356 us  [ring_front(): pl.pallas_call(front_kernel, out_shape=[shape((d_model, qkv_cols), bf16),...]
where the time goes in v7:
time: 719 us; the launch traced here: 718 us
  Pallas kernels  692 us (96%)
  matrix products  18.7 us (3%)
    pallas_call x1, Pallas kernels, ring_front(): pl.pallas_call(front_kernel, out_shape=[shape((d_model, qkv_cols), bf16),...  356 us
    pallas_call x1, Pallas kernels, ring_back(): pl.pallas_call(back_kernel, out_shape=[shape((8 * tokens, array.shape[1])...  335 us
    dot_general x5, matrix products, pair(): lax.dot_general(left, right, (((0,), (0,)), ((), ())), preferred_element_...  18.7 us

profile of v7, /device:TPU:0, one launch (start us, length us, event | category | flops | bytes accessed | tf_op | source)
XLA Modules:
  0.0 718.3 jit_solution(4588861581885991092)
XLA Ops:
  0.6 0.8 neg.3
  1.4 0.1 copy.27
  1.5 0.9 copy.24
  2.4 0.9 copy.26
  3.2 0.8 pad_maximum_fusion
  4.0 356.4 %ring_front_1.1 = (bf16[2048,1536]{1,0:T(8,128)(2,1)}, bf16[512,2048]{1,0:T(8,128)(2,1)}, bf16[8,2,32,256]{3,2,1,0:T(8,128)(2,1)}, bf16[8,2,32,256]{3,2,1,0:T(8,...) custom-call(bf16[256,1536]{1,0:T(8,128)(2,1)} %qkv_sh.1, ...), custom_call_target="tpu_custom_call" | custom-call | flops 88080384000 | bytes 58720256 | tf_op jit(solution)/shard_map/ring_front_1/pallas_call | solution.py:346
  360.4 0.0 copy-start.1
  360.4 335.4 %ring_back_2.1 = (bf16[2048,2048]{1,0:T(8,128)(2,1)}, bf16[2048,512]{1,0:T(8,128)(2,1)}, bf16[2048,2048]{1,0:T(8,128)(2,1)}, bf16[2048,2048]{1,0:T(8,128)(2,1)},...) custom-call(bf16[256,2048]{1,0:T(8,128)(2,1)} %get-tuple-element.35., ...), custom_call_target="tpu_custom_call" | custom-call | flops 88080384000 | bytes 58720256 | tf_op jit(solution)/shard_map/ring_back_2/pallas_call | solution.py:654
  695.8 1.1 reduce_sum.9
  696.9 0.6 copy.29
  697.5 0.6 copy.28
  698.1 0.0 copy-done.1
  698.1 0.0 copy-start.7
  698.1 0.0 slice-start.2
  698.1 5.9 fusion
  704.0 0.0 copy-done.2
  704.0 0.0 copy-done.3
  704.0 1.5 fusion.1
  705.6 0.0 copy-done.6
  705.6 0.0 copy-done.7
  705.6 4.0 fusion.4
  709.5 0.0 slice-done.2
  709.5 0.0 slice-done.3
  709.5 0.0 copy-done
  709.6 3.7 fusion.3
  713.2 0.0 slice-done
  713.2 0.0 slice-done.1
  713.2 0.0 copy-start.4
  713.2 3.7 fusion.2
  716.9 0.7 copy.32
  717.6 0.0 copy-done.4
  717.6 0.7 copy.33
  (12 shorter events, 0.0 us)
Async XLA Ops:
  360.4 337.7 %copy-start.1 = (bf16[8,2,4,32,256]{4,3,2,1,0:T(8,128)(2,1)S(1)}, bf16[8,2,4,32,256]{4,3,2,1,0:T(8,128)(2,1)}, u32[]{:S(2)}) copy-start(bf16[8,2,4,32,256]{4,3,2,1,0:T(8,128)(2,1)} %get-tuple-element.52) | copy-start | bytes 3145732
  698.1 5.9 copy-start.2
  698.1 5.9 copy-start.3
  698.1 7.5 %copy-start.6 = (bf16[8,2,4,32,256]{4,3,2,1,0:T(8,128)(2,1)S(1)}, bf16[8,2,4,32,256]{4,3,2,1,0:T(8,128)(2,1)}, u32[]{:S(2)}) copy-start(bf16[8,2,4,32,256]{4,3,2,1,0:T(8,128)(2,1)} %get-tuple-element.60) | copy-start | bytes 3145732
  698.1 7.5 %copy-start.7 = (bf16[2048,2048]{1,0:T(8,128)(2,1)S(1)}, bf16[2048,2048]{1,0:T(8,128)(2,1)}, u32[]{:S(2)}) copy-start(bf16[2048,2048]{1,0:T(8,128)(2,1)} %get-tuple-element.59) | copy-start | bytes 25165828
  698.1 11.4 %slice-start.2 = ((s8[8388608]{0:T(1024)(128)(4,1)}), s8[4194304]{0:T(1024)(128)(4,1)S(1)}, s32[]{:S(2)}) async-start(s8[8388608]{0:T(1024)(128)(4,1)} %bitcast.26), calls=%async_computation.2 | async-start | bytes 8388608
  704.0 5.5 slice-start.3
  704.0 9.2 %slice-start = ((s8[8388608]{0:T(1024)(128)(4,1)}), s8[4194304]{0:T(1024)(128)(4,1)S(1)}, s32[]{:S(2)}) async-start(s8[8388608]{0:T(1024)(128)(4,1)} %bitcast.24), calls=%async_computation | async-start | bytes 8388608
  705.6 4.0 copy-start
  705.6 7.6 %slice-start.1 = ((s8[8388608]{0:T(1024)(128)(4,1)}), s8[4194304]{0:T(1024)(128)(4,1)S(1)}, s32[]{:S(2)}) async-start(s8[8388608]{0:T(1024)(128)(4,1)} %bitcast.24), calls=%async_computation.1 | async-start | bytes 8388608
  713.2 3.7 copy-start.5
  713.2 4.4 copy-start.4

commit v8 on v7

--- a/solution.py
+++ b/solution.py
@@ -9,6 +9,11 @@
 
 NORM_EPS = 1e-5
 MESH = pl.DeviceIdType.MESH
+WAYS, STEPS, LATER = range(2), range(7), range(1, 7)
+MATES, OTHERS = range(1, 4), range(1, 8)
+DMA = pltpu.SemaphoreType.DMA
+MATE_SEMS, OTHER_SEMS, PAIR, TRIO = DMA((4,)), DMA((8,)), DMA((2,)), DMA((3,))
+PAIR_MATES, TRIO_MATES, TRIO_OTHERS = DMA((2, 4)), DMA((3, 4)), DMA((3, 8))
 
 
 def ring_place(index):
@@ -21,7 +26,52 @@
     return 2 * (place + y * (7 - 2 * place)) + y
 
 
-TILE = 512
+def neighbours(place):
+    return ring_device((place + 1) % 8), ring_device((place + 7) % 8)
+
+
+def owner_of(place, way, step):
+    return ring_device((place + (8 - step if way == 0 else step)) % 8)
+
+
+def enter(me, me_model):
+    barrier = pltpu.get_barrier_semaphore()
+    for hop in OTHERS:
+        pl.semaphore_signal(barrier, inc=1, device_id={'fsdp': (me + hop) % 8}, device_id_type=MESH)
+    for hop in MATES:
+        pl.semaphore_signal(barrier, inc=1, device_id={'model': (me_model + hop) % 4}, device_id_type=MESH)
+    pl.semaphore_wait(barrier, 10)
+
+
+def member(me_model, hop, incoming):
+    return (me_model + 4 - hop) % 4 if incoming else me_model
+
+
+def across(left, right):
+    return lax.dot_general(left, right, (((1,), (1,)), ((), ())), preferred_element_type=jnp.float32)
+
+
+def along(left, right):
+    return lax.dot_general(left, right, (((0,), (0,)), ((), ())), preferred_element_type=jnp.float32)
+
+
+def tiles(width, tile_width, body):
+    @pl.loop(0, width // tile_width)
+    def _(tile):
+        body(pl.ds(pl.multiple_of(tile * tile_width, tile_width), tile_width))
+
+
+def wide_tables(cos_ref, sin_ref):
+    cos_t, sin_t = cos_ref[...], sin_ref[...]
+    return jnp.concatenate([cos_t, cos_t], axis=1), jnp.concatenate([sin_t, -sin_t], axis=1)
+
+
+def sum_blocks(parts, seq, at):
+    total = (parts[0, seq, at, :] + parts[1, seq, at, :]) + (parts[2, seq, at, :] + parts[3, seq, at, :])
+    return total.astype(jnp.bfloat16).astype(jnp.float32)
+
+
+TILE, GROUP = 512, 16
 
 
 def front_kernel(qkv_sh, out_sh, down_sh, gate_sh, up_sh, x_ref, dy_in, gain_attn, gain_mlp, cos_ref, sin_ref,
@@ -35,13 +85,8 @@
     me = lax.axis_index('fsdp')
     me_model = lax.axis_index('model')
     place = ring_place(me)
-    targets = (ring_device((place + 1) % 8), ring_device((place + 7) % 8))
-    barrier = pltpu.get_barrier_semaphore()
-    for hop in range(1, 8):
-        pl.semaphore_signal(barrier, inc=1, device_id={'fsdp': (me + hop) % 8}, device_id_type=MESH)
-    for hop in range(1, 4):
-        pl.semaphore_signal(barrier, inc=1, device_id={'model': (me_model + hop) % 4}, device_id_type=MESH)
-    pl.semaphore_wait(barrier, 10)
+    targets = neighbours(place)
+    enter(me, me_model)
     shards, weights = (qkv_sh, out_sh, down_sh, gate_sh, up_sh), (w_qkv_all, w_out_all, w_down, w_gate, w_up)
     accs = {3: gate_acc, 4: up_acc}
     rows, width = gate_sh.shape
@@ -67,7 +112,7 @@
         return shards[idx].at[pl.ds(way * size, size), :]
 
     def owner_at(way, step):
-        return ring_device((place + (8 - step if way == 0 else step)) % 8)
+        return owner_of(place, way, step)
 
     def send(idx, way, step):
         dst = piece(idx, owner_at(way, step), way)
@@ -87,18 +132,18 @@
 
     def start_ring(ids):
         for idx in ids:
-            for way in range(2):
+            for way in WAYS:
                 send(idx, way, 0).start()
 
     def forward(ids, step):
         for idx in ids:
-            for way in range(2):
+            for way in WAYS:
                 landed(idx, way, step - 1).wait_recv()
                 send(idx, way, step).start()
 
     def finish_ring(ids):
         for idx in ids:
-            for way in range(2):
+            for way in WAYS:
                 landed(idx, way, 6).wait_recv()
                 own(idx, way).wait()
 
@@ -107,11 +152,11 @@
             src_ref=src, dst_ref=dst, send_sem=send_one, recv_sem=recv_one,
             device_id={'model': (me_model + hop) % 4}, device_id_type=MESH)
 
-    def rows_of(ref, member):
-        return ref.at[:, pl.ds(pl.multiple_of(member * block_rows, block_rows), block_rows), :]
+    def rows_of(ref, who):
+        return ref.at[:, pl.ds(pl.multiple_of(who * block_rows, block_rows), block_rows), :]
 
     def block_copy(hop, incoming):
-        slot = blocks.at[(me_model + 4 - hop) % 4 if incoming else me_model]
+        slot = blocks.at[member(me_model, hop, incoming)]
         src = slot if incoming else rows_of(attn_part, (me_model + hop) % 4)
         return to_member(src, slot, block_send.at[hop], block_recv.at[hop], hop)
 
@@ -122,7 +167,7 @@
     slice_dst, spread_dst = (attn_cols, dy_cols, h_cols), (attn_spread, dy_spread)
 
     def seq_copy(idx, hop, incoming):
-        slot = rows_of(seq_dst[idx], (me_model + 4 - hop) % 4 if incoming else me_model)
+        slot = rows_of(seq_dst[idx], member(me_model, hop, incoming))
         return to_member(slot if incoming else seq_src[idx], slot, seq_send.at[idx, hop], seq_recv.at[idx, hop], hop)
 
     def seq_own(idx):
@@ -142,27 +187,27 @@
         return pltpu.make_async_copy(columns(idx, me), slice_dst[idx].at[me], slice_local.at[idx])
 
     def hand_out(idx):
-        for hop in range(1, 4):
+        for hop in MATES:
             seq_copy(idx, hop, False).start()
         seq_own(idx).start()
         slice_own(idx).start()
-        for hop in range(1, 8):
+        for hop in OTHERS:
             slice_copy(idx, hop, False).start()
 
     def seq_wait(idx):
         seq_own(idx).wait()
-        for hop in range(1, 4):
+        for hop in MATES:
             seq_copy(idx, hop, True).wait_recv()
             seq_copy(idx, hop, False).wait_send()
 
     def slice_wait(idx):
         slice_own(idx).wait()
-        for hop in range(1, 8):
+        for hop in OTHERS:
             slice_copy(idx, hop, True).wait_recv()
             slice_copy(idx, hop, False).wait_send()
 
     def cols_copy(idx, hop, incoming):
-        slot = spread_dst[idx].at[:, :, (me_model + 4 - hop) % 4 if incoming else me_model]
+        slot = spread_dst[idx].at[:, :, member(me_model, hop, incoming)]
         return to_member(slot if incoming else slice_dst[idx], slot, cols_send.at[idx, hop], cols_recv.at[idx, hop], hop)
 
     def cols_own(idx):
@@ -175,9 +220,9 @@
         return (val * lax.rsqrt(jnp.mean(val * val, axis=-1, keepdims=True) + NORM_EPS) * gain[...]).astype(bf16)
 
     def attention():
-        @pl.loop(0, qkv.shape[1] // TILE)
-        def _(tile):
-            cols = pl.ds(pl.multiple_of(tile * TILE, TILE), TILE)
+        cos_two, sin_two = wide_tables(cos_ref, sin_ref)
+        @functools.partial(tiles, qkv.shape[1], TILE)
+        def _(cols):
             qkv[:, cols] = jnp.dot(ha_full[...].reshape(tokens, d_model), w_qkv[:, cols], preferred_element_type=f32)
         causal = (lax.broadcasted_iota(jnp.int32, (seq_len, seq_len), 0)
                   >= lax.broadcasted_iota(jnp.int32, (seq_len, seq_len), 1))
@@ -188,7 +233,7 @@
                 start = 3 * head * head_dim
                 for place_in, turned_ref in enumerate((query, key)):
                     part = qkv[at, start + place_in * head_dim:start + (place_in + 1) * head_dim]
-                    turned = part * cos_ref[...] - pltpu.roll(part, head_dim // 2, 1) * sin_ref[...]
+                    turned = part * cos_two - pltpu.roll(part, head_dim // 2, 1) * sin_two
                     turned_ref[idx] = turned.astype(bf16)
                 value[idx] = qkv[at, start + 2 * head_dim:start + 3 * head_dim].astype(bf16)
                 scores = jnp.where(causal, across(query[idx], key[idx]) * head_dim ** -0.5, -1e30)
@@ -198,91 +243,82 @@
                 mixed = jnp.dot(weight.astype(bf16), value[idx], preferred_element_type=f32)
                 attn_flat[at, head * head_dim:(head + 1) * head_dim] = mixed.astype(bf16)
 
-        @pl.loop(0, d_model // TILE)
-        def _(tile):
-            cols = pl.ds(pl.multiple_of(tile * TILE, TILE), TILE)
+        @functools.partial(tiles, d_model, TILE)
+        def _(cols):
             attn_part[:, :, cols] = jnp.dot(attn_flat[...], w_out[:, cols],
                                             preferred_element_type=f32).reshape(seqs, seq_len, TILE)
 
     def accumulate(step):
-        for way in range(2):
+        for way in WAYS:
             start = start_of(owner_at(way, step), way)
             h_block = h_full[:, :, pl.ds(start, half)].reshape(tokens, half)
             for idx in (3, 4):
-                @pl.loop(0, width // TILE)
-                def _(tile):
-                    cols = pl.ds(pl.multiple_of(tile * TILE, TILE), TILE)
+                @functools.partial(tiles, width, TILE)
+                def _(cols):
                     accs[idx][:, cols] += jnp.dot(h_block, weights[idx][pl.ds(start, half), cols],
                                                   preferred_element_type=f32)
 
-    def across(left, right):
-        return lax.dot_general(left, right, (((1,), (1,)), ((), ())), preferred_element_type=f32)
-
     start_ring((0, 1))
     for idx in range(5):
-        for way in range(2):
+        for way in WAYS:
             own(idx, way).start()
     hand_out(1)
 
-    @pl.loop(0, block_rows // 16)
-    def _(group):
-        at = pl.ds(pl.multiple_of(group * 16, 16), 16)
+    @functools.partial(tiles, block_rows, GROUP)
+    def _(at):
         for seq in range(seqs):
             ha_loc[seq, at, :] = normed(x_ref[seq, at, :].astype(f32), gain_attn)
     gate_acc[...] = jnp.zeros_like(gate_acc)
     up_acc[...] = jnp.zeros_like(up_acc)
-    for step in range(1, 7):
+    for step in LATER:
         forward((0, 1), step)
         if step == 1:
             hand_out(0)
     start_ring((2,))
     finish_ring((0, 1))
-    for idx in range(2):
+    for idx in WAYS:
         fetch(idx).start()
-    for step in range(1, 7):
+    for step in LATER:
         forward((2,), step)
         if step == 1:
             seq_wait(0)
-            for idx in range(2):
+            for idx in WAYS:
                 fetch(idx).wait()
             attention()
         if step == 2:
-            for hop in range(1, 4):
+            for hop in MATES:
                 block_copy(hop, False).start()
             block_own().start()
         if step == 4:
             block_own().wait()
-            for hop in range(1, 4):
+            for hop in MATES:
                 block_copy(hop, True).wait_recv()
                 block_copy(hop, False).wait_send()
 
-            @pl.loop(0, block_rows // 16)
-            def _(group):
-                at = pl.ds(pl.multiple_of(group * 16, 16), 16)
+            @functools.partial(tiles, block_rows, GROUP)
+            def _(at):
                 for seq in range(seqs):
-                    total = (blocks[0, seq, at, :] + blocks[1, seq, at, :]) + (blocks[2, seq, at, :] + blocks[3, seq, at, :])
-                    mid = (x_ref[seq, at, :].astype(f32) + total.astype(bf16).astype(f32)).astype(bf16)
+                    mid = (x_ref[seq, at, :].astype(f32) + sum_blocks(blocks, seq, at)).astype(bf16)
                     mid_ref[seq, at, :] = mid
                     h_loc[seq, at, :] = normed(mid.astype(f32), gain_mlp)
         if step == 5:
             hand_out(2)
     start_ring((3, 4))
     seq_wait(1)
-    for idx in range(2):
+    for idx in WAYS:
         slice_wait(idx)
-        for hop in range(1, 4):
+        for hop in MATES:
             cols_copy(idx, hop, False).start()
         cols_own(idx).start()
     finish_ring((2,))
 
-    @pl.loop(0, width // TILE)
-    def _(tile):
-        cols = pl.ds(pl.multiple_of(tile * TILE, TILE), TILE)
+    @functools.partial(tiles, width, TILE)
+    def _(cols):
         d_act[:, cols] = across(dy_full[...].reshape(tokens, d_model), w_down[cols, :]).astype(bf16)
 
     seq_wait(2)
     for idx in (3, 4):
-        for way in range(2):
+        for way in WAYS:
             own(idx, way).wait()
     accumulate(0)
 
@@ -292,13 +328,12 @@
         accumulate(step)
 
     for idx in (3, 4):
-        for way in range(2):
+        for way in WAYS:
             landed(idx, way, 6).wait_recv()
     accumulate(7)
 
-    @pl.loop(0, width // 256)
-    def _(tile):
-        cols = pl.ds(pl.multiple_of(tile * 256, 256), 256)
+    @functools.partial(tiles, width, 256)
+    def _(cols):
         gate, up_proj = gate_acc[:, cols], up_acc[:, cols]
         d_val = d_act[:, cols].astype(f32)
         sig_gate = jax.nn.sigmoid(gate)
@@ -307,20 +342,19 @@
         d_gate_ref[:, cols] = (d_val * up_proj * sig_gate * (1.0 + gate * (1.0 - sig_gate))).astype(bf16)
         d_up_ref[:, cols] = (d_val * silu_gate).astype(bf16)
 
-    @pl.loop(0, width // TILE)
-    def _(tile):
-        cols = pl.ds(pl.multiple_of(tile * TILE, TILE), TILE)
+    @functools.partial(tiles, width, TILE)
+    def _(cols):
         dh_part_ref[:, cols] = across(d_gate_ref[...], w_gate[cols, :]) + across(d_up_ref[...], w_up[cols, :])
         y_part_ref[:, cols] = jnp.dot(act_ref[...], w_down[:, cols], preferred_element_type=f32)
 
     for idx in range(5):
-        for way in range(2):
-            for step in range(7):
+        for way in WAYS:
+            for step in STEPS:
                 send(idx, way, step).wait_send()
     slice_wait(2)
-    for idx in range(2):
+    for idx in WAYS:
         cols_own(idx).wait()
-        for hop in range(1, 4):
+        for hop in MATES:
             cols_copy(idx, hop, True).wait_recv()
             cols_copy(idx, hop, False).wait_send()
 
@@ -328,11 +362,10 @@
 def ring_front(collective_id, *args):
     qkv_sh, out_sh, down_sh, gate_sh, up_sh, x_loc, dy_loc = args[:7]
     seqs, block_rows, d_model = x_loc.shape
-    seq_len, head_dim = args[9].shape
+    seq_len, head_dim = args[9].shape[0], 2 * args[9].shape[1]
     tokens = seqs * seq_len
     width, qkv_cols, attn_cols = gate_sh.shape[1], qkv_sh.shape[1], out_sh.shape[0]
     sent = 7 * (qkv_sh.size + out_sh.size + 3 * gate_sh.size) * 2
-    dma = pltpu.SemaphoreType.DMA
     vmem = pl.BlockSpec(memory_space=pltpu.VMEM)
     hbm = pl.BlockSpec(memory_space=pl.ANY)
     bf16, f32 = jnp.bfloat16, jnp.float32
@@ -355,8 +388,8 @@
                         buf((tokens, width), f32), buf((tokens, width), f32), buf((tokens, width), bf16),
                         buf(whole, bf16), buf(whole, bf16), buf(whole, bf16), buf(x_loc.shape, bf16), buf(x_loc.shape, bf16),
                         buf((4,) + x_loc.shape, f32),
-                        dma((5, 2, 7)), dma((5, 2, 7)), dma((5, 2)), dma((4,)), dma((4,)), dma, dma((3, 4)), dma((3, 4)), dma((3,)),
-                        dma((3, 8)), dma((3, 8)), dma((3,)), dma((2, 4)), dma((2, 4)), dma((2,)), dma((2,))],
+                        DMA((5, 2, 7)), DMA((5, 2, 7)), DMA((5, 2)), MATE_SEMS, MATE_SEMS, DMA, TRIO_MATES, TRIO_MATES, TRIO,
+                        TRIO_OTHERS, TRIO_OTHERS, TRIO, PAIR_MATES, PAIR_MATES, PAIR, PAIR],
         compiler_params=pltpu.CompilerParams(collective_id=collective_id, has_side_effects=True,
                                              vmem_limit_bytes=63 * 1024 * 1024),
         cost_estimate=pl.CostEstimate(flops=sent * 3000, bytes_accessed=2 * sent, transcendentals=0),
@@ -374,13 +407,8 @@
     me = lax.axis_index('fsdp')
     me_model = lax.axis_index('model')
     place = ring_place(me)
-    targets = (ring_device((place + 1) % 8), ring_device((place + 7) % 8))
-    barrier = pltpu.get_barrier_semaphore()
-    for hop in range(1, 8):
-        pl.semaphore_signal(barrier, inc=1, device_id={'fsdp': (me + hop) % 8}, device_id_type=MESH)
-    for hop in range(1, 4):
-        pl.semaphore_signal(barrier, inc=1, device_id={'model': (me_model + hop) % 4}, device_id_type=MESH)
-    pl.semaphore_wait(barrier, 10)
+    targets = neighbours(place)
+    enter(me, me_model)
     sources = (act, attn, d_gate, d_up, d_qkv)
     gathered = (act_all, attn_all, gate_all, up_all, qkv_all)
     seqs, block_rows, d_model = x_ref.shape
@@ -402,7 +430,7 @@
         return sources[idx].at[pl.ds(way * half, half), :]
 
     def owner_at(way, step):
-        return ring_device((place + (8 - step if way == 0 else step)) % 8)
+        return owner_of(place, way, step)
 
     def send(idx, way, step):
         dst = piece(idx, owner_at(way, step), way)
@@ -421,12 +449,12 @@
 
     def start_ring(ids):
         for idx in ids:
-            for way in range(2):
+            for way in WAYS:
                 send(idx, way, 0).start()
 
     def forward(ids, step):
         for idx in ids:
-            for way in range(2):
+            for way in WAYS:
                 landed(idx, way, step - 1).wait_recv()
                 send(idx, way, step).start()
 
@@ -437,11 +465,11 @@
 
     block_src, block_dst = (dh_part, y_part, dh_attn), (dh_blocks, y_blocks, attn_blocks)
 
-    def block_of(idx, member):
-        return block_src[idx].at[:, pl.ds(pl.multiple_of(member * block_rows, block_rows), block_rows), :]
+    def block_of(idx, who):
+        return block_src[idx].at[:, pl.ds(pl.multiple_of(who * block_rows, block_rows), block_rows), :]
 
     def block_copy(idx, hop, incoming):
-        slot = block_dst[idx].at[(me_model + 4 - hop) % 4 if incoming else me_model]
+        slot = block_dst[idx].at[member(me_model, hop, incoming)]
         src = slot if incoming else block_of(idx, (me_model + hop) % 4)
         return to_member(src, slot, block_send.at[idx, hop], block_recv.at[idx, hop], hop)
 
@@ -449,21 +477,21 @@
         return pltpu.make_async_copy(block_of(idx, me_model), block_dst[idx].at[me_model], block_local.at[idx])
 
     def blocks_start(idx):
-        for hop in range(1, 4):
+        for hop in MATES:
             block_copy(idx, hop, False).start()
         block_own(idx).start()
 
     def blocks_wait(idx):
         block_own(idx).wait()
-        for hop in range(1, 4):
+        for hop in MATES:
             block_copy(idx, hop, True).wait_recv()
             block_copy(idx, hop, False).wait_send()
 
-    def mid_slot(member):
-        return d_full.at[:, pl.ds(pl.multiple_of(member * block_rows, block_rows), block_rows), :]
+    def mid_slot(who):
+        return d_full.at[:, pl.ds(pl.multiple_of(who * block_rows, block_rows), block_rows), :]
 
     def mid_copy(hop, incoming):
-        slot = mid_slot((me_model + 4 - hop) % 4 if incoming else me_model)
+        slot = mid_slot(member(me_model, hop, incoming))
         return to_member(slot if incoming else d_mid, slot, mid_send.at[hop], mid_recv.at[hop], hop)
 
     def mid_own():
@@ -485,14 +513,14 @@
     cols_in, cols_all = (h_cols, mid_cols), (h_spread, mid_spread)
 
     def cols_copy(idx, hop, incoming):
-        slot = cols_all[idx].at[:, :, (me_model + 4 - hop) % 4 if incoming else me_model]
+        slot = cols_all[idx].at[:, :, member(me_model, hop, incoming)]
         return to_member(slot if incoming else cols_in[idx], slot, cols_send.at[idx, hop], cols_recv.at[idx, hop], hop)
 
     def cols_own(idx):
         return pltpu.make_async_copy(cols_in[idx], cols_all[idx].at[:, :, me_model], cols_local.at[idx])
 
     def mix_copy(hop, incoming):
-        slot = mix.at[(me_model + 4 - hop) % 4 if incoming else me_model]
+        slot = mix.at[member(me_model, hop, incoming)]
         return to_member(slot if incoming else gains, slot, mix_send.at[hop], mix_recv.at[hop], hop)
 
     def mix_own():
@@ -501,23 +529,13 @@
     def fetch(idx):
         return pltpu.make_async_copy((w_out_in, w_qkv_in)[idx], (w_out, w_qkv)[idx], fetch_sem.at[idx])
 
-    def across(left, right):
-        return lax.dot_general(left, right, (((1,), (1,)), ((), ())), preferred_element_type=f32)
-
-    def along(left, right):
-        return lax.dot_general(left, right, (((0,), (0,)), ((), ())), preferred_element_type=f32)
-
-    def add_up(parts, seq, at):
-        return ((parts[0, seq, at, :] + parts[1, seq, at, :]) + (parts[2, seq, at, :] + parts[3, seq, at, :])).astype(bf16).astype(f32)
-
     def norm_back(parts, saved, gain, base, result, first_row):
         row_sum[...] = jnp.zeros_like(row_sum)
 
-        @pl.loop(0, block_rows // 16)
-        def _(group):
-            at = pl.ds(pl.multiple_of(group * 16, 16), 16)
+        @functools.partial(tiles, block_rows, GROUP)
+        def _(at):
             for seq in range(seqs):
-                d_h = add_up(parts, seq, at)
+                d_h = sum_blocks(parts, seq, at)
                 val = saved[seq, at, :].astype(f32)
                 inv_rms = lax.rsqrt(jnp.mean(val * val, axis=-1, keepdims=True) + NORM_EPS)
                 scaled = d_h * gain[...]
@@ -531,6 +549,7 @@
             gains[first_row + row:first_row + row + 1, :] = total[:, row * width:(row + 1) * width]
 
     def attention_back():
+        cos_two, sin_two = wide_tables(cos_ref, sin_ref)
         d_attn[...] = across(d_full[...].reshape(seqs * seq_len, d_model), w_out[...]).astype(bf16)
         for seq in range(seqs):
             for head in range(heads):
@@ -545,65 +564,63 @@
                 d_key = along(d_scores, query[idx])
                 d_value = along(weight.astype(bf16), d_out)
                 for place_in, part in enumerate((d_query, d_key)):
-                    turned = part * cos_ref[...] + pltpu.roll(part, head_dim // 2, 1) * sin_ref[...]
+                    turned = part * cos_two + pltpu.roll(part, head_dim // 2, 1) * sin_two
                     start = (3 * head + place_in) * head_dim
                     d_qkv[rows, start:start + head_dim] = turned.astype(bf16)
                 d_qkv[rows, (3 * head + 2) * head_dim:(3 * head + 3) * head_dim] = d_value.astype(bf16)
 
-        @pl.loop(0, d_model // TILE)
-        def _(tile):
-            cols = pl.ds(pl.multiple_of(tile * TILE, TILE), TILE)
+        @functools.partial(tiles, d_model, TILE)
+        def _(cols):
             dh_attn[:, :, cols] = across(d_qkv[...], w_qkv[cols, :]).reshape(seqs, seq_len, TILE)
 
     start_ring((0, 1))
     blocks_start(0)
     blocks_start(1)
     for idx in range(4):
-        for way in range(2):
+        for way in WAYS:
             own(idx, way).start()
-    for idx in range(2):
+    for idx in WAYS:
         fetch(idx).start()
-    for hop in range(1, 4):
+    for hop in MATES:
         cols_copy(0, hop, False).start()
     cols_own(0).start()
-    for step in range(1, 7):
+    for step in LATER:
         forward((0, 1), step)
         if step == 2:
             blocks_wait(0)
             norm_back(dh_blocks, mid_ref, gain_mlp, dy_ref, d_mid, 8)
         if step == 3:
-            for hop in range(1, 4):
+            for hop in MATES:
                 mid_copy(hop, False).start()
             mid_own().start()
             slice_own().start()
-            for hop in range(1, 8):
+            for hop in OTHERS:
                 slice_copy(hop, False).start()
         if step == 5:
             blocks_wait(1)
 
-            @pl.loop(0, block_rows // 16)
-            def _(group):
-                at = pl.ds(pl.multiple_of(group * 16, 16), 16)
+            @functools.partial(tiles, block_rows, GROUP)
+            def _(at):
                 for seq in range(seqs):
-                    y_ref[seq, at, :] = (mid_ref[seq, at, :].astype(f32) + add_up(y_blocks, seq, at)).astype(bf16)
+                    y_ref[seq, at, :] = (mid_ref[seq, at, :].astype(f32) + sum_blocks(y_blocks, seq, at)).astype(bf16)
     start_ring((2, 3))
-    for step in range(1, 7):
+    for step in LATER:
         forward((2, 3), step)
         if step == 1:
             mid_own().wait()
-            for hop in range(1, 4):
+            for hop in MATES:
                 mid_copy(hop, True).wait_recv()
                 mid_copy(hop, False).wait_send()
-            for idx in range(2):
+            for idx in WAYS:
                 fetch(idx).wait()
             attention_back()
         if step == 2:
             blocks_start(2)
             slice_own().wait()
-            for hop in range(1, 8):
+            for hop in OTHERS:
                 slice_copy(hop, True).wait_recv()
                 slice_copy(hop, False).wait_send()
-            for hop in range(1, 4):
+            for hop in MATES:
                 cols_copy(1, hop, False).start()
             cols_own(1).start()
         if step == 4:
@@ -611,28 +628,28 @@
             norm_back(attn_blocks, x_ref, gain_attn, d_mid, dx_ref, 0)
         if step == 5:
             mix_own().start()
-            for hop in range(1, 4):
+            for hop in MATES:
                 mix_copy(hop, False).start()
     start_ring((4,))
     mix_own().wait()
-    for hop in range(1, 4):
+    for hop in MATES:
         mix_copy(hop, True).wait_recv()
         mix_copy(hop, False).wait_send()
     start_ring((5,))
     for idx in (4, 5):
-        for way in range(2):
+        for way in WAYS:
             own(idx, way).start()
-    for step in range(1, 7):
+    for step in LATER:
         forward((4, 5), step)
     for idx in range(6):
-        for way in range(2):
+        for way in WAYS:
             landed(idx, way, 6).wait_recv()
             own(idx, way).wait()
-            for step in range(7):
+            for step in STEPS:
                 send(idx, way, step).wait_send()
-    for idx in range(2):
+    for idx in WAYS:
         cols_own(idx).wait()
-        for hop in range(1, 4):
+        for hop in MATES:
             cols_copy(idx, hop, True).wait_recv()
             cols_copy(idx, hop, False).wait_send()
 
@@ -644,7 +661,6 @@
     bf16, f32 = jnp.bfloat16, jnp.float32
     qkv_cols = w_qkv.shape[1]
     sent = 7 * (3 * act.size + attn.size + tokens * qkv_cols) * 2
-    dma = pltpu.SemaphoreType.DMA
     vmem = pl.BlockSpec(memory_space=pltpu.VMEM)
     hbm = pl.BlockSpec(memory_space=pl.ANY)
     shape = jax.ShapeDtypeStruct
@@ -662,9 +678,9 @@
                         pltpu.VMEM(dh_part.shape, bf16), pltpu.VMEM((tokens, w_out.shape[0]), bf16),
                         pltpu.VMEM((tokens, qkv_cols), bf16), pltpu.VMEM(dh_part.shape, f32), pltpu.VMEM(gain_shape, f32),
                         pltpu.VMEM((8, d_model), f32), blocks, blocks, blocks,
-                        dma((6, 2, 7)), dma((6, 2, 7)), dma((6, 2)), dma((3, 4)), dma((3, 4)), dma((3,)),
-                        dma((4,)), dma((4,)), dma, dma((8,)), dma((8,)), dma, dma((2, 4)), dma((2, 4)), dma((2,)),
-                        dma((4,)), dma((4,)), dma, dma((2,))],
+                        DMA((6, 2, 7)), DMA((6, 2, 7)), DMA((6, 2)), TRIO_MATES, TRIO_MATES, TRIO,
+                        MATE_SEMS, MATE_SEMS, DMA, OTHER_SEMS, OTHER_SEMS, DMA, PAIR_MATES, PAIR_MATES, PAIR,
+                        MATE_SEMS, MATE_SEMS, DMA, PAIR],
         compiler_params=pltpu.CompilerParams(collective_id=collective_id, has_side_effects=True,
                                              vmem_limit_bytes=60 * 1024 * 1024),
         cost_estimate=pl.CostEstimate(flops=sent * 3000, bytes_accessed=2 * sent, transcendentals=0),
@@ -680,16 +696,14 @@
 
     def device_fn(x_loc, dy_loc, gain_attn, gain_mlp, wqkv_sh, wout_sh, wgate_sh, wup_sh, wdown_sh, rope_cos, rope_sin):
         tokens = x_loc.shape[0] * rope_cos.shape[0]
-        cos_two = jnp.concatenate([rope_cos, rope_cos], axis=1)
-        sin_two = jnp.concatenate([rope_sin, -rope_sin], axis=1)
         gain_a, gain_m = gain_attn.reshape(1, -1), gain_mlp.reshape(1, -1)
         (w_qkv, w_out, _, _, h_mlp_cols, h_attn_cols, dy_cols, query, key_rot, value, prob, attn_flat, gated_act, d_gate, d_up,
          mlp_part, dh_part, mid) = ring_front(
-            1, wqkv_sh, wout_sh, wdown_sh, wgate_sh, wup_sh, x_loc, dy_loc, gain_a, gain_m, cos_two, sin_two)
+            1, wqkv_sh, wout_sh, wdown_sh, wgate_sh, wup_sh, x_loc, dy_loc, gain_a, gain_m, rope_cos, rope_sin)
         whole = (x_loc.shape[0], rope_cos.shape[0], x_loc.shape[2])
         (act_all, attn_all, d_gate_all, d_up_all, d_qkv_all, gains_all, _, _, d_mid_cols, h_mlp_cols, y_loc, dx_loc) = ring_back(
             2, gated_act, attn_flat, d_gate, d_up, dh_part.reshape(whole), mlp_part.reshape(whole), h_mlp_cols, w_out, w_qkv,
-            mid, x_loc, dy_loc, gain_m, gain_a, query, key_rot, value, prob, cos_two, sin_two)
+            mid, x_loc, dy_loc, gain_m, gain_a, query, key_rot, value, prob, rope_cos, rope_sin)
         gain_grads = jnp.sum(gains_all, axis=(0, 1)).reshape(2, -1)
         h_attn_cols, dy_cols, h_mlp_cols, d_mid_cols = [
             cols.reshape(8 * tokens, -1) for cols in (h_attn_cols, dy_cols, h_mlp_cols, d_mid_cols)]

time: 719 us -> 718 us (level)
  no operation moved by 1% of the time
where the time goes in v8:
time: 718 us
  Pallas kernels  692 us (96%)
  matrix products  18.7 us (3%)
    pallas_call x1, Pallas kernels, ring_front(): pl.pallas_call(front_kernel, out_shape=[shape((d_model, qkv_cols), bf16),...  356 us
    pallas_call x1, Pallas kernels, ring_back(): pl.pallas_call(back_kernel, out_shape=[shape((8 * tokens, array.shape[1])...  335 us
    dot_general x5, matrix products, pair(): lax.dot_general(left, right, (((0,), (0,)), ((), ())), preferred_element_...  18.7 us

profile of v8, /device:TPU:0, one launch (start us, length us, event | category | flops | bytes accessed | tf_op | source)
XLA Modules:
  0.0 717.9 jit_solution(3330201644904599476)
XLA Ops:
  0.6 1.5 copy.20.cos_ref
  2.1 1.5 copy.21.sin_ref
  3.6 356.4 %ring_front_1.1 = (bf16[2048,1536]{1,0:T(8,128)(2,1)}, bf16[512,2048]{1,0:T(8,128)(2,1)}, bf16[8,2,32,256]{3,2,1,0:T(8,128)(2,1)}, bf16[8,2,32,256]{3,2,1,0:T(8,...) custom-call(bf16[256,1536]{1,0:T(8,128)(2,1)} %qkv_sh.1, ...), custom_call_target="tpu_custom_call" | custom-call | flops 88080384000 | bytes 58720256 | tf_op jit(solution)/shard_map/ring_front_1/pallas_call | solution.py:379
  360.1 0.0 copy-start.1
  360.1 335.3 %ring_back_2.1 = (bf16[2048,2048]{1,0:T(8,128)(2,1)}, bf16[2048,512]{1,0:T(8,128)(2,1)}, bf16[2048,2048]{1,0:T(8,128)(2,1)}, bf16[2048,2048]{1,0:T(8,128)(2,1)},...) custom-call(bf16[256,2048]{1,0:T(8,128)(2,1)} %get-tuple-element.35., ...), custom_call_target="tpu_custom_call" | custom-call | flops 88080384000 | bytes 58720256 | tf_op jit(solution)/shard_map/ring_back_2/pallas_call | solution.py:670
  695.4 1.1 reduce_sum.9
  696.5 0.6 copy.25
  697.1 0.6 copy.24
  697.7 0.0 copy-done.1
  697.7 0.0 copy-start.2
  697.7 0.0 copy-start.3
  697.7 0.0 copy-start.7
  697.7 0.0 slice-start.2
  697.7 5.9 fusion
  703.6 0.0 copy-done.2
  703.6 0.0 copy-done.3
  703.6 1.5 fusion.1
  705.2 0.0 copy-done.6
  705.2 0.0 copy-done.7
  705.2 4.0 fusion.4
  709.2 0.0 slice-done.2
  709.2 0.0 slice-done.3
  709.2 0.0 copy-done
  709.2 3.7 fusion.3
  712.8 0.0 slice-done
  712.8 0.0 slice-done.1
  712.9 0.0 copy-start.4
  712.9 3.7 fusion.2
  716.5 0.0 copy-done.5
  716.5 0.7 copy.28
  717.2 0.0 copy-done.4
  717.2 0.7 copy.29
  (9 shorter events, 0.0 us)
Async XLA Ops:
  360.1 337.7 %copy-start.1 = (bf16[8,2,4,32,256]{4,3,2,1,0:T(8,128)(2,1)S(1)}, bf16[8,2,4,32,256]{4,3,2,1,0:T(8,128)(2,1)}, u32[]{:S(2)}) copy-start(bf16[8,2,4,32,256]{4,3,2,1,0:T(8,128)(2,1)} %get-tuple-element.52) | copy-start | bytes 3145732
  697.7 5.9 copy-start.2
  697.7 5.9 copy-start.3
  697.7 7.5 %copy-start.6 = (bf16[8,2,4,32,256]{4,3,2,1,0:T(8,128)(2,1)S(1)}, bf16[8,2,4,32,256]{4,3,2,1,0:T(8,128)(2,1)}, u32[]{:S(2)}) copy-start(bf16[8,2,4,32,256]{4,3,2,1,0:T(8,128)(2,1)} %get-tuple-element.60) | copy-start | bytes 3145732
  697.7 7.5 %copy-start.7 = (bf16[2048,2048]{1,0:T(8,128)(2,1)S(1)}, bf16[2048,2048]{1,0:T(8,128)(2,1)}, u32[]{:S(2)}) copy-start(bf16[2048,2048]{1,0:T(8,128)(2,1)} %get-tuple-element.59) | copy-start | bytes 25165828
  697.7 11.4 %slice-start.2 = ((s8[8388608]{0:T(1024)(128)(4,1)}), s8[4194304]{0:T(1024)(128)(4,1)S(1)}, s32[]{:S(2)}) async-start(s8[8388608]{0:T(1024)(128)(4,1)} %bitcast.26), calls=%async_computation.2 | async-start | bytes 8388608
  703.6 5.5 slice-start.3
  703.6 9.2 %slice-start = ((s8[8388608]{0:T(1024)(128)(4,1)}), s8[4194304]{0:T(1024)(128)(4,1)S(1)}, s32[]{:S(2)}) async-start(s8[8388608]{0:T(1024)(128)(4,1)} %bitcast.24), calls=%async_computation | async-start | bytes 8388608
  705.2 4.0 copy-start
  705.2 7.7 %slice-start.1 = ((s8[8388608]{0:T(1024)(128)(4,1)}), s8[4194304]{0:T(1024)(128)(4,1)S(1)}, s32[]{:S(2)}) async-start(s8[8388608]{0:T(1024)(128)(4,1)} %bitcast.24), calls=%async_computation.1 | async-start | bytes 8388608
  712.8 3.7 copy-start.5
  712.9 4.4 copy-start.4

commit v9 on v8

--- a/solution.py
+++ b/solution.py
@@ -398,11 +398,12 @@
 
 
 def back_kernel(act, attn, d_gate, d_up, dh_part, y_part, h_cols, w_out_in, w_qkv_in, mid_ref, x_ref, dy_ref, gain_mlp, gain_attn,
-                query, key, value, prob, cos_ref, sin_ref,
-                act_all, attn_all, gate_all, up_all, qkv_all, gains_all, mix, mid_cols, mid_spread, h_spread, y_ref, dx_ref,
+                query, key, value, prob, cos_ref, sin_ref, dy_spread,
+                dw_down, dw_out, dw_gate, dw_up, act_all, attn_all, gate_all, up_all, qkv_all, gains_all, mix, mid_cols, mid_spread, h_spread, y_ref, dx_ref,
                 w_out, w_qkv, d_mid, d_full, d_attn, d_qkv, dh_attn, gains, row_sum, dh_blocks, y_blocks, attn_blocks,
                 send_sem, recv_sem, local_sem, block_send, block_recv, block_local, mid_send, mid_recv, mid_local,
-                slice_send, slice_recv, slice_local, cols_send, cols_recv, cols_local, mix_send, mix_recv, mix_local, fetch_sem):
+                slice_send, slice_recv, slice_local, cols_send, cols_recv, cols_local, mix_send, mix_recv, mix_local, fetch_sem,
+                small, big, tall, flat, small_sem, big_sem, product_sem):
     f32, bf16 = jnp.float32, jnp.bfloat16
     me = lax.axis_index('fsdp')
     me_model = lax.axis_index('model')
@@ -518,6 +519,18 @@
 
     def cols_own(idx):
         return pltpu.make_async_copy(cols_in[idx], cols_all[idx].at[:, :, me_model], cols_local.at[idx])
+
+    def finish_ring(ids):
+        for idx in ids:
+            for way in WAYS:
+                landed(idx, way, 6).wait_recv()
+                own(idx, way).wait()
+
+    def cols_wait(idx):
+        cols_own(idx).wait()
+        for hop in MATES:
+            cols_copy(idx, hop, True).wait_recv()
+            cols_copy(idx, hop, False).wait_send()
 
     def mix_copy(hop, incoming):
         slot = mix.at[member(me_model, hop, incoming)]
@@ -573,6 +586,41 @@
         def _(cols):
             dh_attn[:, :, cols] = across(d_qkv[...], w_qkv[cols, :]).reshape(seqs, seq_len, TILE)
 
+    bigs, smalls, products = (act_all, attn_all, gate_all, up_all), (dy_spread, mid_spread, h_spread), (dw_down, dw_out, dw_gate, dw_up)
+
+    def span(tile):
+        return pl.ds(tile * TILE, TILE)
+
+    def small_copy(which):
+        return pltpu.make_async_copy(smalls[which], small.at[which], small_sem.at[which])
+
+    def big_copy(kind, tile, slot):
+        return pltpu.make_async_copy(bigs[kind].at[:, span(tile)], big.at[slot], big_sem.at[slot])
+
+    def product_copy(kind, tile, slot):
+        if kind < 2:
+            return pltpu.make_async_copy(tall.at[slot], products[kind].at[span(tile), :], product_sem.at[slot])
+        return pltpu.make_async_copy(flat.at[slot], products[kind].at[:, span(tile)], product_sem.at[slot])
+
+    def begin(jobs, done=()):
+        for slot, job in enumerate(done):
+            product_copy(*job, slot).wait()
+        for slot, job in enumerate(jobs):
+            big_copy(*job, slot).start()
+
+    def multiply(jobs):
+        for slot, (kind, tile) in enumerate(jobs):
+            big_copy(kind, tile, slot).wait()
+            side = small[min(kind, 2)].reshape(big.shape[1], slice_width)
+            if kind < 2:
+                tall[slot] = along(big[slot], side)
+            else:
+                flat[slot] = along(side, big[slot])
+            product_copy(kind, tile, slot).start()
+
+    early = {3: ((0, 0), (0, 1)), 5: ((0, 2), (0, 3)), 6: ((1, 0),)}
+    late = {2: ((2, 0), (2, 1)), 3: ((2, 2), (2, 3)), 4: ((3, 0), (3, 1)), 5: ((3, 2), (3, 3))}
+    small_copy(0).start()
     start_ring((0, 1))
     blocks_start(0)
     blocks_start(1)
@@ -604,8 +652,25 @@
                 for seq in range(seqs):
                     y_ref[seq, at, :] = (mid_ref[seq, at, :].astype(f32) + sum_blocks(y_blocks, seq, at)).astype(bf16)
     start_ring((2, 3))
+    past = ()
     for step in LATER:
+        if step == 3:
+            small_copy(0).wait()
+            finish_ring((0, 1))
+        if step == 5:
+            cols_wait(0)
+            small_copy(2).start()
+        if step == 6:
+            cols_wait(1)
+            small_copy(1).start()
+        if step in early:
+            begin(early[step], past)
+            past = early[step]
         forward((2, 3), step)
+        if step == 6:
+            small_copy(1).wait()
+        if step in early:
+            multiply(early[step])
         if step == 1:
             mid_own().wait()
             for hop in MATES:
@@ -640,18 +705,21 @@
         for way in WAYS:
             own(idx, way).start()
     for step in LATER:
+        if step == 2:
+            small_copy(2).wait()
+            finish_ring((2, 3))
+        if step in late:
+            begin(late[step], past)
+            past = late[step]
         forward((4, 5), step)
+        if step in late:
+            multiply(late[step])
+    begin((), past)
+    finish_ring((4, 5))
     for idx in range(6):
         for way in WAYS:
-            landed(idx, way, 6).wait_recv()
-            own(idx, way).wait()
             for step in STEPS:
                 send(idx, way, step).wait_send()
-    for idx in WAYS:
-        cols_own(idx).wait()
-        for hop in MATES:
-            cols_copy(idx, hop, True).wait_recv()
-            cols_copy(idx, hop, False).wait_send()
 
 
 def ring_back(collective_id, *args):
@@ -665,22 +733,27 @@
     hbm = pl.BlockSpec(memory_space=pl.ANY)
     shape = jax.ShapeDtypeStruct
     gain_shape = (16, d_model // 8)
+    side = d_model // 8
     spread = shape(h_cols.shape[:2] + (4,) + h_cols.shape[2:], bf16)
     blocks = pltpu.VMEM((4,) + mid.shape, f32)
     return pl.pallas_call(
         back_kernel,
-        out_shape=[shape((8 * tokens, array.shape[1]), bf16) for array in (act, attn, d_gate, d_up)]
+        out_shape=[shape((act.shape[1], side), f32), shape((attn.shape[1], side), f32), shape((side, act.shape[1]), f32),
+                   shape((side, act.shape[1]), f32)]
+        + [shape((8 * tokens, array.shape[1]), bf16) for array in (act, attn, d_gate, d_up)]
         + [shape((8 * tokens, qkv_cols), bf16), shape((8, 4) + gain_shape, f32), shape((4,) + gain_shape, f32),
            shape(h_cols.shape, bf16), spread, spread, shape(mid.shape, bf16), shape(mid.shape, bf16)],
-        in_specs=[hbm] * 9 + [vmem] * (len(args) - 9),
-        out_specs=[hbm] * 10 + [vmem] * 2,
+        in_specs=[hbm] * 9 + [vmem] * (len(args) - 10) + [hbm],
+        out_specs=[hbm] * 14 + [vmem] * 2,
         scratch_shapes=[pltpu.VMEM(w_out.shape, bf16), pltpu.VMEM(w_qkv.shape, bf16), pltpu.VMEM(mid.shape, bf16),
                         pltpu.VMEM(dh_part.shape, bf16), pltpu.VMEM((tokens, w_out.shape[0]), bf16),
                         pltpu.VMEM((tokens, qkv_cols), bf16), pltpu.VMEM(dh_part.shape, f32), pltpu.VMEM(gain_shape, f32),
                         pltpu.VMEM((8, d_model), f32), blocks, blocks, blocks,
                         DMA((6, 2, 7)), DMA((6, 2, 7)), DMA((6, 2)), TRIO_MATES, TRIO_MATES, TRIO,
                         MATE_SEMS, MATE_SEMS, DMA, OTHER_SEMS, OTHER_SEMS, DMA, PAIR_MATES, PAIR_MATES, PAIR,
-                        MATE_SEMS, MATE_SEMS, DMA, PAIR],
+                        MATE_SEMS, MATE_SEMS, DMA, PAIR,
+                        pltpu.VMEM((3,) + spread.shape, bf16), pltpu.VMEM((2, 8 * tokens, TILE), bf16),
+                        pltpu.VMEM((2, TILE, side), f32), pltpu.VMEM((2, side, TILE), f32), TRIO, PAIR, PAIR],
         compiler_params=pltpu.CompilerParams(collective_id=collective_id, has_side_effects=True,
                                              vmem_limit_bytes=60 * 1024 * 1024),
         cost_estimate=pl.CostEstimate(flops=sent * 3000, bytes_accessed=2 * sent, transcendentals=0),
@@ -701,19 +774,12 @@
          mlp_part, dh_part, mid) = ring_front(
             1, wqkv_sh, wout_sh, wdown_sh, wgate_sh, wup_sh, x_loc, dy_loc, gain_a, gain_m, rope_cos, rope_sin)
         whole = (x_loc.shape[0], rope_cos.shape[0], x_loc.shape[2])
-        (act_all, attn_all, d_gate_all, d_up_all, d_qkv_all, gains_all, _, _, d_mid_cols, h_mlp_cols, y_loc, dx_loc) = ring_back(
+        (dw_down, dw_out, dw_gate, dw_up, _, _, _, _, d_qkv_all, gains_all, _, _, _, _, y_loc, dx_loc) = ring_back(
             2, gated_act, attn_flat, d_gate, d_up, dh_part.reshape(whole), mlp_part.reshape(whole), h_mlp_cols, w_out, w_qkv,
-            mid, x_loc, dy_loc, gain_m, gain_a, query, key_rot, value, prob, rope_cos, rope_sin)
+            mid, x_loc, dy_loc, gain_m, gain_a, query, key_rot, value, prob, rope_cos, rope_sin, dy_cols)
         gain_grads = jnp.sum(gains_all, axis=(0, 1)).reshape(2, -1)
-        h_attn_cols, dy_cols, h_mlp_cols, d_mid_cols = [
-            cols.reshape(8 * tokens, -1) for cols in (h_attn_cols, dy_cols, h_mlp_cols, d_mid_cols)]
-
-        def pair(left, right):
-            return lax.dot_general(left, right, (((0,), (0,)), ((), ())), preferred_element_type=f32)
-
-        return (y_loc, dx_loc, gain_grads[0], gain_grads[1],
-                pair(h_attn_cols, d_qkv_all), pair(attn_all, d_mid_cols),
-                pair(h_mlp_cols, d_gate_all), pair(h_mlp_cols, d_up_all), pair(act_all, dy_cols))
+        dw_qkv = along(h_attn_cols.reshape(8 * tokens, -1), d_qkv_all)
+        return (y_loc, dx_loc, gain_grads[0], gain_grads[1], dw_qkv, dw_out, dw_gate, dw_up, dw_down)
 
     in_specs = (act_spec, act_spec, P(), P(), rows_spec, cols_spec, rows_spec, rows_spec, cols_spec, P(), P())
     out_specs = (act_spec, act_spec, P(), P(), rows_spec, cols_spec, rows_spec, rows_spec, cols_spec)

time: 718 us -> 712 us (level)
  matrix products: 18.7 us -> 5.88 us
    dot_general x5 -> x1, matrix products: 18.7 us -> 5.88 us  [along(): lax.dot_general(left, right, (((0,), (0,)), ((), ())), preferred_element_...]
where the time goes in v9:
time: 712 us
  Pallas kernels  692 us (97%)
  local copies, waits for them, and re-layouts  12.4 us (2%)
    pallas_call x1, Pallas kernels, ring_front(): pl.pallas_call(front_kernel, out_shape=[shape((d_model, qkv_cols), bf16),...  356 us
    pallas_call x1, Pallas kernels, ring_back(): pl.pallas_call(back_kernel, out_shape=[shape((act.shape[1], side), f32),...  336 us

profile of v9, /device:TPU:0, one launch (start us, length us, event | category | flops | bytes accessed | tf_op | source)
XLA Modules:
  0.0 712.0 jit_solution(14895679314996743641)
XLA Ops:
  0.6 1.5 copy.20.cos_ref
  2.1 1.5 copy.21.sin_ref
  3.6 356.4 %ring_front_1.1 = (bf16[2048,1536]{1,0:T(8,128)(2,1)}, bf16[512,2048]{1,0:T(8,128)(2,1)}, bf16[8,2,32,256]{3,2,1,0:T(8,128)(2,1)}, bf16[8,2,32,256]{3,2,1,0:T(8,...) custom-call(bf16[256,1536]{1,0:T(8,128)(2,1)} %qkv_sh.1, ...), custom_call_target="tpu_custom_call" | custom-call | flops 88080384000 | bytes 58720256 | tf_op jit(solution)/shard_map/ring_front_1/pallas_call | solution.py:379
  360.0 0.0 copy-start
  360.0 335.5 %ring_back_2.1 = (f32[2048,256]{1,0:T(8,128)}, f32[512,256]{1,0:T(8,128)}, f32[256,2048]{1,0:T(8,128)}, f32[256,2048]{1,0:T(8,128)}, bf16[2048,2048]{1,0:T(8,128...) custom-call(bf16[256,2048]{1,0:T(8,128)(2,1)} %get-tuple-element.33., ...), custom_call_target="tpu_custom_call" | custom-call | flops 88080384000 | bytes 58720256 | tf_op jit(solution)/shard_map/ring_back_2/pallas_call | solution.py:739
  695.5 1.1 reduce_sum.9
  696.6 0.6 copy.25
  697.2 0.6 copy.24
  697.9 0.0 copy-done
  697.9 0.0 copy-start.6
  697.9 0.0 copy-start.5
  697.9 0.0 copy-start.4
  697.9 0.0 copy-start.3
  697.9 5.9 fusion
  703.8 0.0 copy-done.6
  703.8 0.7 copy.32
  704.5 0.0 copy-done.5
  704.5 0.7 copy.33
  705.2 0.0 copy-done.4
  705.2 0.8 copy.34
  706.0 0.0 copy-done.3
  706.0 0.0 copy-start.2
  706.0 1.3 copy.35
  707.3 1.0 copy-done.2
  708.3 0.0 copy-start.1
  708.3 1.3 copy.36
  709.6 1.0 copy-done.1
  710.7 1.3 copy.37
  (1 shorter events, 0.0 us)
Async XLA Ops:
  360.0 337.8 %copy-start = (bf16[8,2,4,32,256]{4,3,2,1,0:T(8,128)(2,1)S(1)}, bf16[8,2,4,32,256]{4,3,2,1,0:T(8,128)(2,1)}, u32[]{:S(2)}) copy-start(bf16[8,2,4,32,256]{4,3,2,1,0:T(8,128)(2,1)} %get-tuple-element.51) | copy-start | bytes 3145732
  697.9 5.9 copy-start.6
  697.9 6.6 copy-start.5
  697.9 7.3 %copy-start.4 = (f32[512,256]{1,0:T(8,128)S(1)}, f32[512,256]{1,0:T(8,128)}, u32[]{:S(2)}) copy-start(f32[512,256]{1,0:T(8,128)} %get-tuple-element.73) | copy-start | bytes 1572868
  697.9 8.1 %copy-start.3 = (f32[256,2048]{1,0:T(8,128)S(1)}, f32[256,2048]{1,0:T(8,128)}, u32[]{:S(2)}) copy-start(f32[256,2048]{1,0:T(8,128)} %get-tuple-element.74) | copy-start | bytes 6291460
  706.0 2.3 copy-start.2
  708.3 2.3 copy-start.1

commit v10 on v9

--- a/solution.py
+++ b/solution.py
@@ -63,7 +63,7 @@
 
 def wide_tables(cos_ref, sin_ref):
     cos_t, sin_t = cos_ref[...], sin_ref[...]
-    return jnp.concatenate([cos_t, cos_t], axis=1), jnp.concatenate([sin_t, -sin_t], axis=1)
+    return jnp.concatenate([cos_t, cos_t], axis=0).T, jnp.concatenate([sin_t, -sin_t], axis=0).T
 
 
 def sum_blocks(parts, seq, at):
@@ -362,7 +362,7 @@
 def ring_front(collective_id, *args):
     qkv_sh, out_sh, down_sh, gate_sh, up_sh, x_loc, dy_loc = args[:7]
     seqs, block_rows, d_model = x_loc.shape
-    seq_len, head_dim = args[9].shape[0], 2 * args[9].shape[1]
+    seq_len, head_dim = args[9].shape[1], 2 * args[9].shape[0]
     tokens = seqs * seq_len
     width, qkv_cols, attn_cols = gate_sh.shape[1], qkv_sh.shape[1], out_sh.shape[0]
     sent = 7 * (qkv_sh.size + out_sh.size + 3 * gate_sh.size) * 2
@@ -398,12 +398,12 @@
 
 
 def back_kernel(act, attn, d_gate, d_up, dh_part, y_part, h_cols, w_out_in, w_qkv_in, mid_ref, x_ref, dy_ref, gain_mlp, gain_attn,
-                query, key, value, prob, cos_ref, sin_ref, dy_spread,
-                dw_down, dw_out, dw_gate, dw_up, act_all, attn_all, gate_all, up_all, qkv_all, gains_all, mix, mid_cols, mid_spread, h_spread, y_ref, dx_ref,
+                query, key, value, prob, cos_ref, sin_ref, dy_spread, attn_spread,
+                dw_qkv, dw_down, dw_out, dw_gate, dw_up, act_all, attn_all, gate_all, up_all, gains_all, mix, mid_cols, mid_spread, h_spread, y_ref, dx_ref,
                 w_out, w_qkv, d_mid, d_full, d_attn, d_qkv, dh_attn, gains, row_sum, dh_blocks, y_blocks, attn_blocks,
                 send_sem, recv_sem, local_sem, block_send, block_recv, block_local, mid_send, mid_recv, mid_local,
                 slice_send, slice_recv, slice_local, cols_send, cols_recv, cols_local, mix_send, mix_recv, mix_local, fetch_sem,
-                small, big, tall, flat, small_sem, big_sem, product_sem):
+                small, big, tall, flat, qkv_all, qkv_acc, small_sem, big_sem, product_sem):
     f32, bf16 = jnp.float32, jnp.bfloat16
     me = lax.axis_index('fsdp')
     me_model = lax.axis_index('model')
@@ -586,7 +586,7 @@
         def _(cols):
             dh_attn[:, :, cols] = across(d_qkv[...], w_qkv[cols, :]).reshape(seqs, seq_len, TILE)
 
-    bigs, smalls, products = (act_all, attn_all, gate_all, up_all), (dy_spread, mid_spread, h_spread), (dw_down, dw_out, dw_gate, dw_up)
+    bigs, smalls, products = (act_all, attn_all, gate_all, up_all), (dy_spread, mid_spread, h_spread, attn_spread), (dw_down, dw_out, dw_gate, dw_up)
 
     def span(tile):
         return pl.ds(tile * TILE, TILE)
@@ -618,9 +618,24 @@
                 flat[slot] = along(side, big[slot])
             product_copy(kind, tile, slot).start()
 
+    def accumulate(step):
+        for way in WAYS:
+            owner = owner_at(way, step)
+            side = small[3, owner, way].reshape(seq_len, slice_width)
+
+            @functools.partial(tiles, qkv_acc.shape[1], TILE)
+            def _(cols):
+                if step == 0:
+                    block = d_qkv[way * seq_len:(way + 1) * seq_len, cols]
+                else:
+                    block = qkv_all[pl.ds(pl.multiple_of((2 * owner + way) * seq_len, seq_len), seq_len), cols]
+                qkv_acc[:, cols] += along(side, block)
+
     early = {3: ((0, 0), (0, 1)), 5: ((0, 2), (0, 3)), 6: ((1, 0),)}
     late = {2: ((2, 0), (2, 1)), 3: ((2, 2), (2, 3)), 4: ((3, 0), (3, 1)), 5: ((3, 2), (3, 3))}
     small_copy(0).start()
+    small_copy(3).start()
+    qkv_acc[...] = jnp.zeros_like(qkv_acc)
     start_ring((0, 1))
     blocks_start(0)
     blocks_start(1)
@@ -704,6 +719,8 @@
     for idx in (4, 5):
         for way in WAYS:
             own(idx, way).start()
+    small_copy(3).wait()
+    accumulate(0)
     for step in LATER:
         if step == 2:
             small_copy(2).wait()
@@ -714,12 +731,17 @@
         forward((4, 5), step)
         if step in late:
             multiply(late[step])
+        accumulate(step)
     begin((), past)
     finish_ring((4, 5))
+    accumulate(7)
+    result = pltpu.make_async_copy(qkv_acc, dw_qkv, fetch_sem.at[0])
+    result.start()
     for idx in range(6):
         for way in WAYS:
             for step in STEPS:
                 send(idx, way, step).wait_send()
+    result.wait()
 
 
 def ring_back(collective_id, *args):
@@ -738,12 +760,12 @@
     blocks = pltpu.VMEM((4,) + mid.shape, f32)
     return pl.pallas_call(
         back_kernel,
-        out_shape=[shape((act.shape[1], side), f32), shape((attn.shape[1], side), f32), shape((side, act.shape[1]), f32),
+        out_shape=[shape((side, qkv_cols), f32), shape((act.shape[1], side), f32), shape((attn.shape[1], side), f32), shape((side, act.shape[1]), f32),
                    shape((side, act.shape[1]), f32)]
         + [shape((8 * tokens, array.shape[1]), bf16) for array in (act, attn, d_gate, d_up)]
-        + [shape((8 * tokens, qkv_cols), bf16), shape((8, 4) + gain_shape, f32), shape((4,) + gain_shape, f32),
+        + [shape((8, 4) + gain_shape, f32), shape((4,) + gain_shape, f32),
            shape(h_cols.shape, bf16), spread, spread, shape(mid.shape, bf16), shape(mid.shape, bf16)],
-        in_specs=[hbm] * 9 + [vmem] * (len(args) - 10) + [hbm],
+        in_specs=[hbm] * 9 + [vmem] * (len(args) - 11) + [hbm] * 2,
         out_specs=[hbm] * 14 + [vmem] * 2,
         scratch_shapes=[pltpu.VMEM(w_out.shape, bf16), pltpu.VMEM(w_qkv.shape, bf16), pltpu.VMEM(mid.shape, bf16),
                         pltpu.VMEM(dh_part.shape, bf16), pltpu.VMEM((tokens, w_out.shape[0]), bf16),
@@ -752,8 +774,9 @@
                         DMA((6, 2, 7)), DMA((6, 2, 7)), DMA((6, 2)), TRIO_MATES, TRIO_MATES, TRIO,
                         MATE_SEMS, MATE_SEMS, DMA, OTHER_SEMS, OTHER_SEMS, DMA, PAIR_MATES, PAIR_MATES, PAIR,
                         MATE_SEMS, MATE_SEMS, DMA, PAIR,
-                        pltpu.VMEM((3,) + spread.shape, bf16), pltpu.VMEM((2, 8 * tokens, TILE), bf16),
-                        pltpu.VMEM((2, TILE, side), f32), pltpu.VMEM((2, side, TILE), f32), TRIO, PAIR, PAIR],
+                        pltpu.VMEM((4,) + spread.shape, bf16), pltpu.VMEM((2, 8 * tokens, TILE), bf16),
+                        pltpu.VMEM((2, TILE, side), f32), pltpu.VMEM((2, side, TILE), f32), pltpu.VMEM((8 * tokens, qkv_cols), bf16),
+                        pltpu.VMEM((side, qkv_cols), f32), MATE_SEMS, PAIR, PAIR],
         compiler_params=pltpu.CompilerParams(collective_id=collective_id, has_side_effects=True,
                                              vmem_limit_bytes=60 * 1024 * 1024),
         cost_estimate=pl.CostEstimate(flops=sent * 3000, bytes_accessed=2 * sent, transcendentals=0),
@@ -768,17 +791,16 @@
     f32 = jnp.float32
 
     def device_fn(x_loc, dy_loc, gain_attn, gain_mlp, wqkv_sh, wout_sh, wgate_sh, wup_sh, wdown_sh, rope_cos, rope_sin):
-        tokens = x_loc.shape[0] * rope_cos.shape[0]
         gain_a, gain_m = gain_attn.reshape(1, -1), gain_mlp.reshape(1, -1)
+        rope_cos_t, rope_sin_t = rope_cos.T, rope_sin.T
         (w_qkv, w_out, _, _, h_mlp_cols, h_attn_cols, dy_cols, query, key_rot, value, prob, attn_flat, gated_act, d_gate, d_up,
          mlp_part, dh_part, mid) = ring_front(
-            1, wqkv_sh, wout_sh, wdown_sh, wgate_sh, wup_sh, x_loc, dy_loc, gain_a, gain_m, rope_cos, rope_sin)
+            1, wqkv_sh, wout_sh, wdown_sh, wgate_sh, wup_sh, x_loc, dy_loc, gain_a, gain_m, rope_cos_t, rope_sin_t)
         whole = (x_loc.shape[0], rope_cos.shape[0], x_loc.shape[2])
-        (dw_down, dw_out, dw_gate, dw_up, _, _, _, _, d_qkv_all, gains_all, _, _, _, _, y_loc, dx_loc) = ring_back(
+        (dw_qkv, dw_down, dw_out, dw_gate, dw_up, _, _, _, _, gains_all, _, _, _, _, y_loc, dx_loc) = ring_back(
             2, gated_act, attn_flat, d_gate, d_up, dh_part.reshape(whole), mlp_part.reshape(whole), h_mlp_cols, w_out, w_qkv,
-            mid, x_loc, dy_loc, gain_m, gain_a, query, key_rot, value, prob, rope_cos, rope_sin, dy_cols)
+            mid, x_loc, dy_loc, gain_m, gain_a, query, key_rot, value, prob, rope_cos_t, rope_sin_t, dy_cols, h_attn_cols)
         gain_grads = jnp.sum(gains_all, axis=(0, 1)).reshape(2, -1)
-        dw_qkv = along(h_attn_cols.reshape(8 * tokens, -1), d_qkv_all)
         return (y_loc, dx_loc, gain_grads[0], gain_grads[1], dw_qkv, dw_out, dw_gate, dw_up, dw_down)
 
     in_specs = (act_spec, act_spec, P(), P(), rows_spec, cols_spec, rows_spec, rows_spec, cols_spec, P(), P())

time: 712 us -> 709 us (level)
  no operation moved by 1% of the time
where the time goes in v10:
time: 709 us
  Pallas kernels  694 us (98%)
  local copies, waits for them, and re-layouts  12.9 us (2%)
    pallas_call x1, Pallas kernels, ring_front(): pl.pallas_call(front_kernel, out_shape=[shape((d_model, qkv_cols), bf16),...  357 us
    pallas_call x1, Pallas kernels, ring_back(): pl.pallas_call(back_kernel, out_shape=[shape((side, qkv_cols), f32), shap...  338 us

profile of v10, /device:TPU:0, one launch (start us, length us, event | category | flops | bytes accessed | tf_op | source)
XLA Modules:
  0.0 708.8 jit_solution(12516875576975906516)
XLA Ops:
  0.6 356.5 %ring_front_1.1 = (bf16[2048,1536]{1,0:T(8,128)(2,1)}, bf16[512,2048]{1,0:T(8,128)(2,1)}, bf16[8,2,32,256]{3,2,1,0:T(8,128)(2,1)}, bf16[8,2,32,256]{3,2,1,0:T(8,...) custom-call(bf16[256,1536]{1,0:T(8,128)(2,1)} %qkv_sh.1, ...), custom_call_target="tpu_custom_call" | custom-call | flops 88080384000 | bytes 58720256 | tf_op jit(solution)/shard_map/ring_front_1/pallas_call | solution.py:379
  357.2 337.5 %ring_back_2.1 = (f32[256,1536]{1,0:T(8,128)}, f32[2048,256]{1,0:T(8,128)}, f32[512,256]{1,0:T(8,128)}, f32[256,2048]{1,0:T(8,128)}, f32[256,2048]{1,0:T(8,128)}...) custom-call(bf16[256,2048]{1,0:T(8,128)(2,1)} %get-tuple-element.33., ...), custom_call_target="tpu_custom_call" | custom-call | flops 88080384000 | bytes 58720256 | tf_op jit(solution)/shard_map/ring_back_2/pallas_call | solution.py:761
  694.7 0.0 copy-start.3
  694.7 1.2 reduce_sum.9
  695.9 0.6 copy.21
  696.5 0.6 copy.20
  697.1 0.0 copy-start.4
  697.1 1.7 copy.29
  698.9 1.7 copy.30
  700.5 0.0 copy-done.3
  700.5 0.0 copy-start.2
  700.5 1.1 copy.31
  701.7 0.0 copy-done.4
  701.7 0.8 copy.32
  702.5 0.3 copy-done.2
  702.8 0.0 copy-start.1
  702.8 1.3 copy.33
  704.1 1.0 copy-done.1
  705.1 0.0 copy-start
  705.1 1.3 copy.34
  706.5 1.0 copy-done
  707.5 1.3 copy.35
  (1 shorter events, 0.0 us)
Async XLA Ops:
  694.7 5.8 copy-start.3
  697.1 4.5 copy-start.4
  700.5 2.3 copy-start.2
  702.8 2.3 copy-start.1
  705.1 2.3 copy-start

commit v11 on v10

--- a/solution.py
+++ b/solution.py
@@ -632,7 +632,7 @@
                 qkv_acc[:, cols] += along(side, block)
 
     early = {3: ((0, 0), (0, 1)), 5: ((0, 2), (0, 3)), 6: ((1, 0),)}
-    late = {2: ((2, 0), (2, 1)), 3: ((2, 2), (2, 3)), 4: ((3, 0), (3, 1)), 5: ((3, 2), (3, 3))}
+    late = {1: ((2, 0), (2, 1)), 2: ((2, 2),), 3: ((2, 3),), 4: ((3, 0), (3, 1)), 5: ((3, 2),), 6: ((3, 3),)}
     small_copy(0).start()
     small_copy(3).start()
     qkv_acc[...] = jnp.zeros_like(qkv_acc)
@@ -651,7 +651,7 @@
         forward((0, 1), step)
         if step == 2:
             blocks_wait(0)
-            norm_back(dh_blocks, mid_ref, gain_mlp, dy_ref, d_mid, 8)
+            norm_back(dh_blocks, mid_ref, gain_mlp, dy_ref, d_mid, 16)
         if step == 3:
             for hop in MATES:
                 mid_copy(hop, False).start()
@@ -722,7 +722,7 @@
     small_copy(3).wait()
     accumulate(0)
     for step in LATER:
-        if step == 2:
+        if step == 1:
             small_copy(2).wait()
             finish_ring((2, 3))
         if step in late:
@@ -754,7 +754,7 @@
     vmem = pl.BlockSpec(memory_space=pltpu.VMEM)
     hbm = pl.BlockSpec(memory_space=pl.ANY)
     shape = jax.ShapeDtypeStruct
-    gain_shape = (16, d_model // 8)
+    gain_shape = (32, d_model // 16)
     side = d_model // 8
     spread = shape(h_cols.shape[:2] + (4,) + h_cols.shape[2:], bf16)
     blocks = pltpu.VMEM((4,) + mid.shape, f32)
@@ -800,7 +800,7 @@
         (dw_qkv, dw_down, dw_out, dw_gate, dw_up, _, _, _, _, gains_all, _, _, _, _, y_loc, dx_loc) = ring_back(
             2, gated_act, attn_flat, d_gate, d_up, dh_part.reshape(whole), mlp_part.reshape(whole), h_mlp_cols, w_out, w_qkv,
             mid, x_loc, dy_loc, gain_m, gain_a, query, key_rot, value, prob, rope_cos_t, rope_sin_t, dy_cols, h_attn_cols)
-        gain_grads = jnp.sum(gains_all, axis=(0, 1)).reshape(2, -1)
+        gain_grads = [part.reshape(-1) for part in jnp.split(jnp.sum(gains_all, axis=(0, 1)), 2)]
         return (y_loc, dx_loc, gain_grads[0], gain_grads[1], dw_qkv, dw_out, dw_gate, dw_up, dw_down)
 
     in_specs = (act_spec, act_spec, P(), P(), rows_spec, cols_spec, rows_spec, rows_spec, cols_spec, P(), P())

time: 709 us -> 709 us (level)
  no operation moved by 1% of the time
where the time goes in v11:
time: 709 us; the launch traced here: 708 us
  Pallas kernels  694 us (98%)
  local copies, waits for them, and re-layouts  12.3 us (2%)
    pallas_call x1, Pallas kernels, ring_front(): pl.pallas_call(front_kernel, out_shape=[shape((d_model, qkv_cols), bf16),...  357 us
    pallas_call x1, Pallas kernels, ring_back(): pl.pallas_call(back_kernel, out_shape=[shape((side, qkv_cols), f32), shap...  338 us

profile of v11, /device:TPU:0, one launch (start us, length us, event | category | flops | bytes accessed | tf_op | source)
XLA Modules:
  0.0 708.2 jit_solution(10495177864283904805)
XLA Ops:
  0.6 356.5 %ring_front_1.1 = (bf16[2048,1536]{1,0:T(8,128)(2,1)}, bf16[512,2048]{1,0:T(8,128)(2,1)}, bf16[8,2,32,256]{3,2,1,0:T(8,128)(2,1)}, bf16[8,2,32,256]{3,2,1,0:T(8,...) custom-call(bf16[256,1536]{1,0:T(8,128)(2,1)} %qkv_sh.1, ...), custom_call_target="tpu_custom_call" | custom-call | flops 88080384000 | bytes 58720256 | tf_op jit(solution)/shard_map/ring_front_1/pallas_call | solution.py:379
  357.2 337.5 %ring_back_2.1 = (f32[256,1536]{1,0:T(8,128)}, f32[2048,256]{1,0:T(8,128)}, f32[512,256]{1,0:T(8,128)}, f32[256,2048]{1,0:T(8,128)}, f32[256,2048]{1,0:T(8,128)}...) custom-call(bf16[256,2048]{1,0:T(8,128)(2,1)} %get-tuple-element.33., ...), custom_call_target="tpu_custom_call" | custom-call | flops 88080384000 | bytes 58720256 | tf_op jit(solution)/shard_map/ring_back_2/pallas_call | solution.py:761
  694.7 0.0 copy-start.3
  694.7 1.2 reduce_sum.9
  695.9 0.6 slice_bitcast_fusion
  696.5 0.0 copy-start.4
  696.5 1.7 copy.27
  698.3 1.7 copy.28
  699.9 0.0 copy-done.3
  699.9 0.0 copy-start.2
  699.9 1.1 copy.29
  701.1 0.0 copy-done.4
  701.1 0.8 copy.30
  701.9 0.3 copy-done.2
  702.2 0.0 copy-start.1
  702.2 1.3 copy.31
  703.5 1.0 copy-done.1
  704.5 0.0 copy-start
  704.5 1.3 copy.32
  705.9 1.0 copy-done
  706.9 1.3 copy.33
Async XLA Ops:
  694.7 5.2 copy-start.3
  696.5 4.5 copy-start.4
  699.9 2.3 copy-start.2
  702.2 2.3 copy-start.1
  704.5 2.3 copy-start
